TPU v7x, 768 devices: a whole 4x8x12 slice. The times are simulated.
768 devices in a mesh: grp: 96 (over x, y_lo, z), sub: 8 (over y_hi, core).
Axes of the slice: x: 4, y: 8 (y_hi: 4, y_lo: 2; y = y_hi * 2 + y_lo), z: 12, core: 2. Of those that a mesh axis runs over, the one named last changes fastest.
Arguments:
- residual: float32 [2359296], P(('grp', 'sub')), may hold values from -6 to 6
- edge_scale: float32 [2359296], P(('grp', 'sub')), may hold values from 0.2 to 1
- tangent: float32 [3, 2359296], P(None, ('grp', 'sub')), may hold values from -6 to 6
- edge_tail: int32 [2359296], P(('grp', 'sub')), may hold values from 0 to 511
- edge_head: int32 [2359296], P(('grp', 'sub')), may hold values from 0 to 4607
- stencil_index: int32 [14, 393216], P(None, ('grp', 'sub')), may hold values from 0 to 4607
- stencil_coef: bfloat16 [4, 14, 393216], P(None, None, ('grp', 'sub')), may hold values from -1 to -0.099609375
- diag_margin: float32 [4, 393216], P(None, ('grp', 'sub')), may hold values from 0.05 to 0.5
- send_index: int32 [192, 16, 512], P('grp', 'sub'), may hold values from 0 to 511
Outputs:
- correction: float32 [2359296], P(('grp', 'sub'))
Inputs may be any that keep to these rules, and one draw needn't show every extreme that they name: `edge_tail`: positions among a device's own nodes. `edge_head`: positions in the device's extended list: own nodes first, then the 8 received blocks. `stencil_index`: positions in the extended list of the device that holds the row. `send_index`: positions among the device's own nodes; an entry may repeat.
All inputs are finite; a program needn't handle non-finite values.
Results may differ from a plain program's by a relative error of at most 0.0003.
Values sent between devices are 32-bit elements; how exact they have to be, the bound alone decides.
No kernel may reach another device: no remote copies, remote signals or barrier semaphores. Data moves between devices by JAX's collectives and lax.ppermute only.
A program may use at most 32 MiB of HBM per device.

v0:
```python
import jax
import jax.numpy as jnp
from jax import lax
from jax.sharding import PartitionSpec as P

SWEEPS = 4


def shifted(block, axis, distance):
    devices = range(lax.axis_size(axis))
    route = [((i - distance) % len(devices), i) for i in devices]
    return lax.ppermute(block, axis, route)


def with_halo(value, sides, width):
    for axis, dim in sides:
        devices, length = (lax.axis_size(axis), value.shape[dim])
        up = [(i, (i + 1) % devices) for i in range(devices)]
        down = [(j, i) for i, j in up]
        last = lax.slice_in_dim(value, length - width, length, axis=dim)
        leading = lax.slice_in_dim(value, 0, width, axis=dim)
        before = lax.ppermute(last, axis, up)
        after = lax.ppermute(leading, axis, down)
        value = jnp.concatenate([before, value, after], axis=dim)
    return value


def toward_grp(values, offset):
    return shifted(values, "grp", offset)


def toward_sub(values, offset):
    return shifted(values, "sub", offset)


def ghost_values(owned_vals, send_index):
    blocks = owned_vals[:, send_index]
    widened = with_halo(blocks, (("grp", 1), ("sub", 2)), 1)
    pieces = [widened[:, 0, 1:3], widened[:, 3, 1:3], widened[:, 1:3, 0], widened[:, 1:3, 3]]
    flat_pieces = [piece.reshape(piece.shape[0], -1) for piece in pieces]
    return jnp.concatenate([owned_vals] + flat_pieces, axis=1)


def body(
    residual,
    edge_scale,
    tangent,
    edge_tail,
    edge_head,
    stencil_index,
    stencil_coef,
    diag_margin,
    send_index,
):
    node_count = diag_margin.shape[1]
    rim_size = send_index.shape[2]
    extended = node_count + 8 * rim_size
    half_terms = 0.5 * tangent * residual[None, :]
    vals_tail = jnp.concatenate([-residual[None, :], half_terms], axis=0)
    vals_head = jnp.concatenate([residual[None, :], half_terms], axis=0)
    edge_terms = jnp.zeros((4, extended), jnp.float32)
    edge_terms = edge_terms.at[:, edge_tail].add(vals_tail).at[:, edge_head].add(vals_head)
    node_sums = edge_terms[:, :node_count]
    ghost_terms = edge_terms[:, node_count:].reshape(4, 4, 2, rim_size)
    from_above = toward_grp(ghost_terms[:, 0], -1)
    from_below = toward_grp(ghost_terms[:, 1], 1)
    from_next = toward_sub(ghost_terms[:, 2], -1)
    from_prev = toward_sub(ghost_terms[:, 3], 1)
    node_sums = node_sums.at[:, send_index[1].reshape(-1)].add(from_above.reshape(4, -1))
    node_sums = node_sums.at[:, send_index[0].reshape(-1)].add(from_below.reshape(4, -1))
    node_sums = node_sums.at[:, send_index[:, 1].reshape(-1)].add(from_next.reshape(4, -1))
    node_sums = node_sums.at[:, send_index[:, 0].reshape(-1)].add(from_prev.reshape(4, -1))
    coef_wide = stencil_coef.astype(jnp.float32)
    diag_vals = (1.0 + diag_margin) * jnp.sum(jnp.abs(coef_wide), axis=1)
    solved = node_sums / diag_vals
    for sweep in range(SWEEPS - 1):
        widened = ghost_values(solved, send_index)
        applied = diag_vals * solved + jnp.sum(coef_wide * widened[:, stencil_index], axis=1)
        solved = solved + (node_sums - applied) / diag_vals
    widened = ghost_values(solved, send_index)
    at_tail = widened[:, edge_tail]
    at_head = widened[:, edge_head]
    return (
        edge_scale * residual
        + (at_head[0] - at_tail[0])
        + 0.5 * jnp.sum(tangent * (at_tail[1:] + at_head[1:]), axis=0)
    )


def solution(mesh):
    return jax.shard_map(
        body,
        mesh=mesh,
        in_specs=(
            P(("grp", "sub")),
            P(("grp", "sub")),
            P(None, ("grp", "sub")),
            P(("grp", "sub")),
            P(("grp", "sub")),
            P(None, ("grp", "sub")),
            P(None, None, ("grp", "sub")),
            P(None, ("grp", "sub")),
            P("grp", "sub", None),
        ),
        out_specs=P(("grp", "sub")),
        check_vma=False,
    )
```

profile of v0, /device:TPU:1, one launch (start us, length us, event | category | flops | bytes accessed | tf_op | source)
XLA Modules:
  0.0 337.6 jit_solution(13057351767922245498)
XLA Ops:
  2.3 1.7 copy.103
  4.0 1.7 copy.104
  5.7 17.8 %scatter_custom_fusion = f32[4,4608]{0,1:T(8,128)S(1)} fusion(s32[3072]{0:T(1024)S(1)} %get-tuple-element.32, f32[3072,4]{1,0:T(8,128)} %copy.103, f32[]{:T(128)} %constant.6.clone.1), kind=kCustom, calls=%fused_computation.17 | custom fusion | flops 12288 | bytes 74240 | tf_op jit(solution)/shard_map/scatter-add | solution.py:62
  23.5 18.1 %scatter_fusion = f32[4,4608]{0,1:T(8,128)S(1)} fusion(f32[4,4608]{0,1:T(8,128)S(1)} %scatter_custom_fusion, s32[3072]{0:T(1024)S(1)} %get-tuple-element.39, f32[3072,4]{1,0:T(8,128)} %copy.104), kind=kCustom, calls=%fused_computation.10 | custom fusion | flops 12288 | bytes 159744 | tf_op jit(solution)/shard_map/scatter-add | solution.py:62
  43.0 18.3 %collective-permute-start = (f32[4,2,512]{0,2,1:T(8,128)}, f32[4,2,512]{0,2,1:T(8,128)}, u32[]{:S(2)}, u32[]{:S(2)}) collective-permute-start(f32[4,2,512]{0,2,1:T(8,128)} %get-tuple-element.10), channel_id=1, source_target_pairs={{8,0},{16,8},{24,16},{32,24},{40,32},{48,40},{56,48},{64,56},{72,6... | collective-permute-start | bytes 49160 | tf_op jit(solution)/shard_map/ppermute | solution.py:12
  61.3 1.9 collective-permute-start.1
  63.2 2.9 collective-permute-start.2
  66.1 4.1 %collective-permute-start.3 = (f32[4,2,512]{0,2,1:T(8,128)S(1)}, f32[4,2,512]{0,2,1:T(8,128)}, u32[]{:S(2)}, u32[]{:S(2)}) collective-permute-start(f32[4,2,512]{0,2,1:T(8,128)S(1)} %get-tuple-element.7), channel_id=1, source_target_pairs={{7,0},{0,1},{1,2},{2,3},{3,4},{4,5},{5,6},{6,7},{15,8},{8,9},{9,10... | collective-permute-start | bytes 49160 | tf_op jit(solution)/shard_map/ppermute | solution.py:12
  70.5 1.7 collective-permute-done
  72.3 6.5 %scatter_fusion.1 = f32[4,512]{0,1:T(8,128)S(1)} fusion(f32[4,512]{0,1:T(8,128)S(1)} %slice.170, s32[1024]{0:T(1024)S(1)} %bitcast.121, f32[1024,4]{1,0:T(8,128)} %bitcast.8), kind=kCustom, calls=%fused_computation.11 | custom fusion | flops 4096 | bytes 53248 | tf_op jit(solution)/shard_map/scatter-add | solution.py:69
  78.8 6.6 %collective-permute-done.1 = f32[4,2,512]{0,2,1:T(8,128)} collective-permute-done((f32[4,2,512]{0,2,1:T(8,128)}, f32[4,2,512]{0,2,1:T(8,128)}, u32[]{:S(2)}, u32[]{:S(2)}) %collective-permute-start.1) | collective-permute-done | bytes 16416 | tf_op jit(solution)/shard_map/ppermute | solution.py:12
  85.4 6.5 %scatter_fusion.2 = f32[4,512]{0,1:T(8,128)S(1)} fusion(f32[4,512]{0,1:T(8,128)S(1)} %scatter_fusion.1, s32[1024]{0:T(1024)S(1)} %bitcast.120, f32[1024,4]{1,0:T(8,128)} %bitcast.12), kind=kCustom, calls=%fused_computation.12 | custom fusion | flops 4096 | bytes 53248 | tf_op jit(solution)/shard_map/scatter-add | solution.py:70
  92.0 6.5 %scatter_fusion.3 = f32[4,512]{0,1:T(8,128)S(1)} fusion(f32[4,512]{0,1:T(8,128)S(1)} %scatter_fusion.2, s32[1024]{0:T(1024)S(1)} %bitcast.119, f32[1024,4]{1,0:T(8,128)} %bitcast.17), kind=kCustom, calls=%fused_computation.13 | custom fusion | flops 4096 | bytes 53248 | tf_op jit(solution)/shard_map/scatter-add | solution.py:71
  98.6 6.7 %scatter_fusion.4 = f32[4,512]{0,1:T(8,128)S(1)} fusion(f32[4,512]{0,1:T(8,128)S(1)} %scatter_fusion.3, s32[1024]{0:T(1024)S(1)} %bitcast.118, f32[1024,4]{1,0:T(8,128)} %bitcast.22), kind=kCustom, calls=%fused_computation.14 | custom fusion | flops 4096 | bytes 53248 | tf_op jit(solution)/shard_map/scatter-add | solution.py:72
  105.6 5.5 %gather_fusion = f32[2048,4]{1,0:T(8,128)S(1)} fusion(f32[4,512]{0,1:T(8,128)S(1)} %copy.112, s32[2048]{0:T(1024)S(1)} %broadcast_clamp_fusion.3), kind=kCustom, calls=%fused_computation | custom fusion | bytes 73728 | tf_op jit(solution)/shard_map/gather | solution.py:37
  111.4 1.9 collective-permute-start.4
  113.4 7.6 %collective-permute-start.5 = (f32[4,1,2,512]{3,1,2,0:T(1,128)S(1)}, f32[4,1,2,512]{3,1,2,0:T(1,128)S(1)}, u32[]{:S(2)}, u32[]{:S(2)}) collective-permute-start(f32[4,1,2,512]{3,1,2,0:T(1,128)S(1)} %get-tuple-element.27), channel_id=1, source_target_pairs={{8,0},{16,8},{24,16},{32,24},{40,32},{48,40},{56,48},{64,56},{72,6... | collective-permute-start | bytes 49160 | tf_op jit(solution)/shard_map/ppermute | solution.py:23
  121.9 7.6 %collective-permute-start.6 = (f32[4,4,1,512]{3,1,2,0:T(4,128)S(1)}, f32[4,4,1,512]{3,1,2,0:T(4,128)S(1)}, u32[]{:S(2)}, u32[]{:S(2)}) collective-permute-start(f32[4,4,1,512]{3,1,2,0:T(4,128)S(1)} %get-tuple-element.18), channel_id=1, source_target_pairs={{0,1},{1,2},{2,3},{3,4},{4,5},{5,6},{6,7},{7,0},{8,9},{9,10},{10,1... | collective-permute-start | bytes 98312 | tf_op jit(solution)/shard_map/ppermute | solution.py:22
  129.5 1.9 collective-permute-start.7
  133.8 1.8 collective-permute-done.7
  137.5 26.0 %gather_fusion.1 = f32[7168,4]{1,0:T(8,128)} fusion(f32[4,4608]{0,1:T(8,128)} %constant_dynamic-update-slice_fusion, s32[7168]{0:T(1024)S(1)} %broadcast_clamp_fusion), kind=kCustom, calls=%fused_computation.1 | custom fusion | bytes 258048 | tf_op jit(solution)/shard_map/gather | solution.py:78
  163.5 2.6 copy.113
  166.3 5.5 %gather_fusion.2 = f32[2048,4]{1,0:T(8,128)S(1)} fusion(f32[4,512]{0,1:T(8,128)S(1)} %copy.121, s32[2048]{0:T(1024)S(1)} %broadcast_clamp_fusion.3), kind=kCustom, calls=%fused_computation.2 | custom fusion | bytes 73728 | tf_op jit(solution)/shard_map/gather | solution.py:37
  172.2 1.9 collective-permute-start.8
  174.1 8.1 %collective-permute-start.9 = (f32[4,1,2,512]{3,1,2,0:T(1,128)S(1)}, f32[4,1,2,512]{3,1,2,0:T(1,128)S(1)}, u32[]{:S(2)}, u32[]{:S(2)}) collective-permute-start(f32[4,1,2,512]{3,1,2,0:T(1,128)S(1)} %get-tuple-element.25), channel_id=1, source_target_pairs={{8,0},{16,8},{24,16},{32,24},{40,32},{48,40},{56,48},{64,56},{72,6... | collective-permute-start | bytes 49160 | tf_op jit(solution)/shard_map/ppermute | solution.py:23
  183.2 3.6 %collective-permute-start.10 = (f32[4,4,1,512]{3,1,2,0:T(4,128)S(1)}, f32[4,4,1,512]{3,1,2,0:T(4,128)S(1)}, u32[]{:S(2)}, u32[]{:S(2)}) collective-permute-start(f32[4,4,1,512]{3,1,2,0:T(4,128)S(1)} %get-tuple-element.16), channel_id=1, source_target_pairs={{0,1},{1,2},{2,3},{3,4},{4,5},{5,6},{6,7},{7,0},{8,9},{9,10},{10,1... | collective-permute-start | bytes 98312 | tf_op jit(solution)/shard_map/ppermute | solution.py:22
  186.8 1.9 collective-permute-start.11
  191.1 1.8 collective-permute-done.11
  194.8 26.0 %gather_fusion.3 = f32[7168,4]{1,0:T(8,128)} fusion(f32[4,4608]{0,1:T(8,128)} %constant_dynamic-update-slice_fusion.5, s32[7168]{0:T(1024)S(1)} %broadcast_clamp_fusion), kind=kCustom, calls=%fused_computation.3 | custom fusion | bytes 258048 | tf_op jit(solution)/shard_map/gather | solution.py:78
  220.8 2.6 copy.122
  223.6 5.5 %gather_fusion.4 = f32[2048,4]{1,0:T(8,128)S(1)} fusion(f32[4,512]{0,1:T(8,128)S(1)} %copy.130, s32[2048]{0:T(1024)S(1)} %broadcast_clamp_fusion.3), kind=kCustom, calls=%fused_computation.4 | custom fusion | bytes 73728 | tf_op jit(solution)/shard_map/gather | solution.py:37
  229.5 1.9 collective-permute-start.12
  231.4 8.2 %collective-permute-start.13 = (f32[4,1,2,512]{3,1,2,0:T(1,128)S(1)}, f32[4,1,2,512]{3,1,2,0:T(1,128)S(1)}, u32[]{:S(2)}, u32[]{:S(2)}) collective-permute-start(f32[4,1,2,512]{3,1,2,0:T(1,128)S(1)} %get-tuple-element.23), channel_id=1, source_target_pairs={{8,0},{16,8},{24,16},{32,24},{40,32},{48,40},{56,48},{64,56},{72,6... | collective-permute-start | bytes 49160 | tf_op jit(solution)/shard_map/ppermute | solution.py:23
  240.5 3.6 %collective-permute-start.14 = (f32[4,4,1,512]{3,1,2,0:T(4,128)S(1)}, f32[4,4,1,512]{3,1,2,0:T(4,128)S(1)}, u32[]{:S(2)}, u32[]{:S(2)}) collective-permute-start(f32[4,4,1,512]{3,1,2,0:T(4,128)S(1)} %get-tuple-element.14), channel_id=1, source_target_pairs={{0,1},{1,2},{2,3},{3,4},{4,5},{5,6},{6,7},{7,0},{8,9},{9,10},{10,1... | collective-permute-start | bytes 98312 | tf_op jit(solution)/shard_map/ppermute | solution.py:22
  244.1 2.1 collective-permute-start.15
  248.6 2.2 collective-permute-done.15
  252.7 26.0 %gather_fusion.5 = f32[7168,4]{1,0:T(8,128)} fusion(f32[4,4608]{0,1:T(8,128)} %constant_dynamic-update-slice_fusion.10, s32[7168]{0:T(1024)S(1)} %broadcast_clamp_fusion), kind=kCustom, calls=%fused_computation.5 | custom fusion | bytes 258048 | tf_op jit(solution)/shard_map/gather | solution.py:78
  278.7 2.6 copy.131
  281.5 5.5 %gather_fusion.6 = f32[2048,4]{1,0:T(8,128)S(1)} fusion(f32[4,512]{0,1:T(8,128)S(1)} %copy.139, s32[2048]{0:T(1024)S(1)} %broadcast_clamp_fusion.3), kind=kCustom, calls=%fused_computation.6 | custom fusion | bytes 73728 | tf_op jit(solution)/shard_map/gather | solution.py:37
  287.4 1.9 collective-permute-start.16
  289.3 7.8 %collective-permute-start.17 = (f32[4,1,2,512]{3,1,2,0:T(1,128)S(1)}, f32[4,1,2,512]{3,1,2,0:T(1,128)S(1)}, u32[]{:S(2)}, u32[]{:S(2)}) collective-permute-start(f32[4,1,2,512]{3,1,2,0:T(1,128)S(1)} %get-tuple-element.21), channel_id=1, source_target_pairs={{8,0},{16,8},{24,16},{32,24},{40,32},{48,40},{56,48},{64,56},{72,6... | collective-permute-start | bytes 49160 | tf_op jit(solution)/shard_map/ppermute | solution.py:23
  298.1 3.8 %collective-permute-start.18 = (f32[4,4,1,512]{3,1,2,0:T(4,128)S(1)}, f32[4,4,1,512]{3,1,2,0:T(4,128)S(1)}, u32[]{:S(2)}, u32[]{:S(2)}) collective-permute-start(f32[4,4,1,512]{3,1,2,0:T(4,128)S(1)} %get-tuple-element.12), channel_id=1, source_target_pairs={{0,1},{1,2},{2,3},{3,4},{4,5},{5,6},{6,7},{7,0},{8,9},{9,10},{10,1... | collective-permute-start | bytes 98312 | tf_op jit(solution)/shard_map/ppermute | solution.py:22
  301.9 2.8 collective-permute-start.19
  305.5 3.8 %collective-permute-done.19 = f32[4,4,1,512]{3,1,2,0:T(4,128)S(1)} collective-permute-done((f32[4,4,1,512]{3,1,2,0:T(4,128)S(1)}, f32[4,4,1,512]{3,1,2,0:T(4,128)S(1)}, u32[]{:S(2)}, u32[]{:S(2)}) %collective-permute-start.19) | collective-permute-done | bytes 32800 | tf_op jit(solution)/shard_map/ppermute | solution.py:23
  311.0 9.8 %gather_fusion.8 = f32[3072,4]{1,0:T(8,128)S(1)} fusion(f32[4,4608]{0,1:T(8,128)} %copy-done.2, s32[3072]{0:T(1024)S(1)} %get-tuple-element.31), kind=kCustom, calls=%fused_computation.8 | custom fusion | bytes 110592 | tf_op jit(solution)/shard_map/gather | solution.py:81
  322.4 9.8 %gather_fusion.7 = f32[3072,4]{1,0:T(8,128)S(1)} fusion(f32[4,4608]{0,1:T(8,128)} %copy-done.2, s32[3072]{0:T(1024)S(1)} %get-tuple-element.40), kind=kCustom, calls=%fused_computation.7 | custom fusion | bytes 110592 | tf_op jit(solution)/shard_map/gather | solution.py:82
  332.2 1.6 slice.203
  334.4 2.0 copy.140
  (135 shorter events, 28.3 us)
Async XLA Ops:
  0.0 5.6 %copy-start.7 = (s32[3072]{0:T(1024)S(1)}, s32[3072]{0:T(1024)}, u32[]{:S(2)}) copy-start(s32[3072]{0:T(1024)} %param.12) | copy-start | bytes 36868
  0.0 5.6 %copy-start.8 = (s32[3072]{0:T(1024)S(1)}, s32[3072]{0:T(1024)}, u32[]{:S(2)}) copy-start(s32[3072]{0:T(1024)} %param.13) | copy-start | bytes 36868
  41.7 28.5 %copy-start.5 = (s32[2,2,512]{2,1,0:T(2,128)S(1)}, s32[2,2,512]{2,1,0:T(2,128)}, u32[]{:S(2)}) copy-start(s32[2,2,512]{2,1,0:T(2,128)} %param.17) | copy-start | bytes 24580
  41.8 28.7 %copy-start.6 = (s32[14,512]{1,0:T(8,128)S(1)}, s32[14,512]{1,0:T(8,128)}, u32[]{:S(2)}) copy-start(s32[14,512]{1,0:T(8,128)} %param.14) | copy-start | bytes 86020
  41.8 28.7 %copy-start.1 = (bf16[4,14,512]{2,0,1:T(4,128)(2,1)S(1)}, bf16[4,14,512]{2,0,1:T(4,128)(2,1)}, u32[]{:S(2)}) copy-start(bf16[4,14,512]{2,0,1:T(4,128)(2,1)} %param.15) | copy-start | bytes 172036
  41.8 63.6 %copy-start.10 = (f32[4,512]{1,0:T(4,128)S(1)}, f32[4,512]{1,0:T(4,128)}, u32[]{:S(2)}) copy-start(f32[4,512]{1,0:T(4,128)} %param.16) | copy-start | bytes 24580
  43.0 29.3 %collective-permute-start = (f32[4,2,512]{0,2,1:T(8,128)}, f32[4,2,512]{0,2,1:T(8,128)}, u32[]{:S(2)}, u32[]{:S(2)}) collective-permute-start(f32[4,2,512]{0,2,1:T(8,128)} %get-tuple-element.10), channel_id=1, source_target_pairs={{8,0},{16,8},{24,16},{32,24},{40,32},{48,40},{56,48},{64,56},{72,6... | collective-permute-start | bytes 49160 | tf_op jit(solution)/shard_map/ppermute | solution.py:12
  61.3 24.1 %collective-permute-start.1 = (f32[4,2,512]{0,2,1:T(8,128)}, f32[4,2,512]{0,2,1:T(8,128)}, u32[]{:S(2)}, u32[]{:S(2)}) collective-permute-start(f32[4,2,512]{0,2,1:T(8,128)} %get-tuple-element.9), channel_id=1, source_target_pairs={{760,0},{0,8},{8,16},{16,24},{24,32},{32,40},{40,48},{48,56},{56,6... | collective-permute-start | bytes 49160 | tf_op jit(solution)/shard_map/ppermute | solution.py:12
  63.2 28.7 %collective-permute-start.2 = (f32[4,2,512]{0,2,1:T(8,128)}, f32[4,2,512]{0,2,1:T(8,128)}, u32[]{:S(2)}, u32[]{:S(2)}) collective-permute-start(f32[4,2,512]{0,2,1:T(8,128)} %get-tuple-element.8), channel_id=1, source_target_pairs={{1,0},{2,1},{3,2},{4,3},{5,4},{6,5},{7,6},{0,7},{9,8},{10,9},{11,1... | collective-permute-start | bytes 49160 | tf_op jit(solution)/shard_map/ppermute | solution.py:12
  66.1 32.4 %collective-permute-start.3 = (f32[4,2,512]{0,2,1:T(8,128)S(1)}, f32[4,2,512]{0,2,1:T(8,128)}, u32[]{:S(2)}, u32[]{:S(2)}) collective-permute-start(f32[4,2,512]{0,2,1:T(8,128)S(1)} %get-tuple-element.7), channel_id=1, source_target_pairs={{7,0},{0,1},{1,2},{2,3},{3,4},{4,5},{5,6},{6,7},{15,8},{8,9},{9,10... | collective-permute-start | bytes 49160 | tf_op jit(solution)/shard_map/ppermute | solution.py:12
  111.4 10.3 %collective-permute-start.4 = (f32[4,1,2,512]{3,1,2,0:T(1,128)S(1)}, f32[4,1,2,512]{3,1,2,0:T(1,128)S(1)}, u32[]{:S(2)}, u32[]{:S(2)}) collective-permute-start(f32[4,1,2,512]{3,1,2,0:T(1,128)S(1)} %get-tuple-element.28), channel_id=1, source_target_pairs={{0,8},{8,16},{16,24},{24,32},{32,40},{40,48},{48,56},{56,64},{64,7... | collective-permute-start | bytes 49160 | tf_op jit(solution)/shard_map/ppermute | solution.py:22
  113.4 8.4 %collective-permute-start.5 = (f32[4,1,2,512]{3,1,2,0:T(1,128)S(1)}, f32[4,1,2,512]{3,1,2,0:T(1,128)S(1)}, u32[]{:S(2)}, u32[]{:S(2)}) collective-permute-start(f32[4,1,2,512]{3,1,2,0:T(1,128)S(1)} %get-tuple-element.27), channel_id=1, source_target_pairs={{8,0},{16,8},{24,16},{32,24},{40,32},{48,40},{56,48},{64,56},{72,6... | collective-permute-start | bytes 49160 | tf_op jit(solution)/shard_map/ppermute | solution.py:23
  121.9 11.7 %collective-permute-start.6 = (f32[4,4,1,512]{3,1,2,0:T(4,128)S(1)}, f32[4,4,1,512]{3,1,2,0:T(4,128)S(1)}, u32[]{:S(2)}, u32[]{:S(2)}) collective-permute-start(f32[4,4,1,512]{3,1,2,0:T(4,128)S(1)} %get-tuple-element.18), channel_id=1, source_target_pairs={{0,1},{1,2},{2,3},{3,4},{4,5},{5,6},{6,7},{7,0},{8,9},{9,10},{10,1... | collective-permute-start | bytes 98312 | tf_op jit(solution)/shard_map/ppermute | solution.py:22
  129.5 6.1 %collective-permute-start.7 = (f32[4,4,1,512]{3,1,2,0:T(4,128)S(1)}, f32[4,4,1,512]{3,1,2,0:T(4,128)S(1)}, u32[]{:S(2)}, u32[]{:S(2)}) collective-permute-start(f32[4,4,1,512]{3,1,2,0:T(4,128)S(1)} %get-tuple-element.17), channel_id=1, source_target_pairs={{1,0},{2,1},{3,2},{4,3},{5,4},{6,5},{7,6},{0,7},{9,8},{10,9},{11,1... | collective-permute-start | bytes 98312 | tf_op jit(solution)/shard_map/ppermute | solution.py:23
  172.2 10.8 %collective-permute-start.8 = (f32[4,1,2,512]{3,1,2,0:T(1,128)S(1)}, f32[4,1,2,512]{3,1,2,0:T(1,128)S(1)}, u32[]{:S(2)}, u32[]{:S(2)}) collective-permute-start(f32[4,1,2,512]{3,1,2,0:T(1,128)S(1)} %get-tuple-element.26), channel_id=1, source_target_pairs={{0,8},{8,16},{16,24},{24,32},{32,40},{40,48},{48,56},{56,64},{64,7... | collective-permute-start | bytes 49160 | tf_op jit(solution)/shard_map/ppermute | solution.py:22
  174.1 9.0 %collective-permute-start.9 = (f32[4,1,2,512]{3,1,2,0:T(1,128)S(1)}, f32[4,1,2,512]{3,1,2,0:T(1,128)S(1)}, u32[]{:S(2)}, u32[]{:S(2)}) collective-permute-start(f32[4,1,2,512]{3,1,2,0:T(1,128)S(1)} %get-tuple-element.25), channel_id=1, source_target_pairs={{8,0},{16,8},{24,16},{32,24},{40,32},{48,40},{56,48},{64,56},{72,6... | collective-permute-start | bytes 49160 | tf_op jit(solution)/shard_map/ppermute | solution.py:23
  183.2 7.6 %collective-permute-start.10 = (f32[4,4,1,512]{3,1,2,0:T(4,128)S(1)}, f32[4,4,1,512]{3,1,2,0:T(4,128)S(1)}, u32[]{:S(2)}, u32[]{:S(2)}) collective-permute-start(f32[4,4,1,512]{3,1,2,0:T(4,128)S(1)} %get-tuple-element.16), channel_id=1, source_target_pairs={{0,1},{1,2},{2,3},{3,4},{4,5},{5,6},{6,7},{7,0},{8,9},{9,10},{10,1... | collective-permute-start | bytes 98312 | tf_op jit(solution)/shard_map/ppermute | solution.py:22
  186.8 6.1 %collective-permute-start.11 = (f32[4,4,1,512]{3,1,2,0:T(4,128)S(1)}, f32[4,4,1,512]{3,1,2,0:T(4,128)S(1)}, u32[]{:S(2)}, u32[]{:S(2)}) collective-permute-start(f32[4,4,1,512]{3,1,2,0:T(4,128)S(1)} %get-tuple-element.15), channel_id=1, source_target_pairs={{1,0},{2,1},{3,2},{4,3},{5,4},{6,5},{7,6},{0,7},{9,8},{10,9},{11,1... | collective-permute-start | bytes 98312 | tf_op jit(solution)/shard_map/ppermute | solution.py:23
  229.5 10.8 %collective-permute-start.12 = (f32[4,1,2,512]{3,1,2,0:T(1,128)S(1)}, f32[4,1,2,512]{3,1,2,0:T(1,128)S(1)}, u32[]{:S(2)}, u32[]{:S(2)}) collective-permute-start(f32[4,1,2,512]{3,1,2,0:T(1,128)S(1)} %get-tuple-element.24), channel_id=1, source_target_pairs={{0,8},{8,16},{16,24},{24,32},{32,40},{40,48},{48,56},{56,64},{64,7... | collective-permute-start | bytes 49160 | tf_op jit(solution)/shard_map/ppermute | solution.py:22
  231.4 9.0 %collective-permute-start.13 = (f32[4,1,2,512]{3,1,2,0:T(1,128)S(1)}, f32[4,1,2,512]{3,1,2,0:T(1,128)S(1)}, u32[]{:S(2)}, u32[]{:S(2)}) collective-permute-start(f32[4,1,2,512]{3,1,2,0:T(1,128)S(1)} %get-tuple-element.23), channel_id=1, source_target_pairs={{8,0},{16,8},{24,16},{32,24},{40,32},{48,40},{56,48},{64,56},{72,6... | collective-permute-start | bytes 49160 | tf_op jit(solution)/shard_map/ppermute | solution.py:23
  240.5 7.8 %collective-permute-start.14 = (f32[4,4,1,512]{3,1,2,0:T(4,128)S(1)}, f32[4,4,1,512]{3,1,2,0:T(4,128)S(1)}, u32[]{:S(2)}, u32[]{:S(2)}) collective-permute-start(f32[4,4,1,512]{3,1,2,0:T(4,128)S(1)} %get-tuple-element.14), channel_id=1, source_target_pairs={{0,1},{1,2},{2,3},{3,4},{4,5},{5,6},{6,7},{7,0},{8,9},{9,10},{10,1... | collective-permute-start | bytes 98312 | tf_op jit(solution)/shard_map/ppermute | solution.py:22
  244.1 6.7 %collective-permute-start.15 = (f32[4,4,1,512]{3,1,2,0:T(4,128)S(1)}, f32[4,4,1,512]{3,1,2,0:T(4,128)S(1)}, u32[]{:S(2)}, u32[]{:S(2)}) collective-permute-start(f32[4,4,1,512]{3,1,2,0:T(4,128)S(1)} %get-tuple-element.13), channel_id=1, source_target_pairs={{1,0},{2,1},{3,2},{4,3},{5,4},{6,5},{7,6},{0,7},{9,8},{10,9},{11,1... | collective-permute-start | bytes 98312 | tf_op jit(solution)/shard_map/ppermute | solution.py:23
  287.4 9.8 %collective-permute-start.16 = (f32[4,1,2,512]{3,1,2,0:T(1,128)S(1)}, f32[4,1,2,512]{3,1,2,0:T(1,128)S(1)}, u32[]{:S(2)}, u32[]{:S(2)}) collective-permute-start(f32[4,1,2,512]{3,1,2,0:T(1,128)S(1)} %get-tuple-element.22), channel_id=1, source_target_pairs={{0,8},{8,16},{16,24},{24,32},{32,40},{40,48},{48,56},{56,64},{64,7... | collective-permute-start | bytes 49160 | tf_op jit(solution)/shard_map/ppermute | solution.py:22
  289.3 8.7 %collective-permute-start.17 = (f32[4,1,2,512]{3,1,2,0:T(1,128)S(1)}, f32[4,1,2,512]{3,1,2,0:T(1,128)S(1)}, u32[]{:S(2)}, u32[]{:S(2)}) collective-permute-start(f32[4,1,2,512]{3,1,2,0:T(1,128)S(1)} %get-tuple-element.21), channel_id=1, source_target_pairs={{8,0},{16,8},{24,16},{32,24},{40,32},{48,40},{56,48},{64,56},{72,6... | collective-permute-start | bytes 49160 | tf_op jit(solution)/shard_map/ppermute | solution.py:23
  298.1 7.2 %collective-permute-start.18 = (f32[4,4,1,512]{3,1,2,0:T(4,128)S(1)}, f32[4,4,1,512]{3,1,2,0:T(4,128)S(1)}, u32[]{:S(2)}, u32[]{:S(2)}) collective-permute-start(f32[4,4,1,512]{3,1,2,0:T(4,128)S(1)} %get-tuple-element.12), channel_id=1, source_target_pairs={{0,1},{1,2},{2,3},{3,4},{4,5},{5,6},{6,7},{7,0},{8,9},{9,10},{10,1... | collective-permute-start | bytes 98312 | tf_op jit(solution)/shard_map/ppermute | solution.py:22
  301.9 7.4 %collective-permute-start.19 = (f32[4,4,1,512]{3,1,2,0:T(4,128)S(1)}, f32[4,4,1,512]{3,1,2,0:T(4,128)S(1)}, u32[]{:S(2)}, u32[]{:S(2)}) collective-permute-start(f32[4,4,1,512]{3,1,2,0:T(4,128)S(1)} %get-tuple-element.11), channel_id=1, source_target_pairs={{1,0},{2,1},{3,2},{4,3},{5,4},{6,5},{7,6},{0,7},{9,8},{10,9},{11,1... | collective-permute-start | bytes 98312 | tf_op jit(solution)/shard_map/ppermute | solution.py:23
  309.6 1.4 copy-start.2
  334.4 2.0 copy-start
  334.4 2.5 copy-start.3
  334.4 2.6 copy-start.4
  334.4 2.6 copy-start.9
where the time goes:
time: 341 us; the launch traced here: 338 us
  local copies, waits for them, and re-layouts  157 us (46%)
  starting transfers between devices  94 us (28%)
  other arithmetic  66.3 us (19%)
  waiting for transfers between devices  19.2 us (6%)
    gather x6, local copies, waits for them, and re-layouts, body(): widened[:, stencil_index]  85.7 us
    ppermute x8, starting transfers between devices, with_halo(): after = lax.ppermute(leading, axis, down)  40.5 us
    scatter-add x2, other arithmetic, body(): edge_terms.at[:, edge_tail].add(vals_tail).at[:, edge_head].add(vals_head)  35.9 us
    ppermute x4, starting transfers between devices, shifted(): return lax.ppermute(block, axis, route)  27.2 us
    ppermute x8, starting transfers between devices, with_halo(): before = lax.ppermute(last, axis, up)  26.3 us
    gather x8, local copies, waits for them, and re-layouts, ghost_values(): blocks = owned_vals[:, send_index]  23.2 us
    unnamed x42, local copies, waits for them, and re-layouts  11.3 us
    ppermute x8, waiting for transfers between devices, with_halo(): after = lax.ppermute(leading, axis, down)  10.8 us
  transfers between devices with their start and end apart: 20, of which 10 were waited for; matrix products, arithmetic and copies ran while one was open for 9% of the time, Pallas kernels for 0%

commit v1 on v0

v1 whole, which is shorter than its diff:
```python
import jax
import jax.numpy as jnp
from jax import lax
from jax.experimental import pallas as pl
from jax.experimental.pallas import tpu as pltpu
from jax.sharding import PartitionSpec as P

SWEEPS = 4
LANES = 128
F32 = jnp.float32
BF16 = jnp.bfloat16
VMEM = pl.BlockSpec(memory_space=pltpu.VMEM)
SMEM = pl.BlockSpec(memory_space=pltpu.SMEM)


def call(kernel, outs, *args, flops=1 << 20):
    return pl.pallas_call(
        kernel,
        out_shape=[jax.ShapeDtypeStruct(shape, dtype) for shape, dtype in outs],
        in_specs=[SMEM] + [VMEM] * (len(args) - 1),
        out_specs=[VMEM] * len(outs),
    )(*args)


def pairs(size, offset):
    route = []
    for k in range(size // 2):
        low, high = (2 * k + offset) % size, (2 * k + 1 + offset) % size
        route += [(low, high), (high, low)]
    return route


def split3(value):
    first = value.astype(BF16).astype(F32)
    rest = value - first
    second = rest.astype(BF16).astype(F32)
    third = (rest - second).astype(BF16).astype(F32)
    return (first, second, third)


def nt_dot(left, right):
    return lax.dot_general(left, right, (((1,), (1,)), ((), ())), preferred_element_type=F32)


def lane_pick(row, lane):
    wide = jnp.broadcast_to(row, lane.shape)
    return jnp.take_along_axis(wide, lane, axis=1, mode="promise_in_bounds")


def rows_of(index):
    return lax.shift_right_logical(index, 7), jnp.bitwise_and(index, LANES - 1)


def onehot(lane):
    n = lane.shape[1]
    iota = lax.broadcasted_iota(jnp.int32, (LANES, n), 0)
    return jnp.where(iota == lane, 1.0, 0.0).astype(BF16)


def masked(values, row, count):
    iota = lax.broadcasted_iota(jnp.int32, (count, row.shape[1]), 0)
    mask = iota == row
    return jnp.concatenate([jnp.where(mask, v, 0.0) for v in values], axis=0).astype(BF16)


def sides(par, odd, even):
    low = jnp.where(par == 1, even, odd)
    high = jnp.where(par == 1, odd, even)
    return low, high


def edge_sums(par, res_ref, tan_ref, tail_ref, head_ref, own_ref, og_ref, eg_ref, os_ref, es_ref):
    edges = res_ref.shape[1]
    chunk = 512
    total_head, total_tail = None, None
    for start in range(0, edges, chunk):
        cut = slice(start, start + chunk)
        res = res_ref[:, cut]
        half = [0.5 * tan_ref[c : c + 1, cut] * res for c in range(3)]
        head_row, head_lane = rows_of(head_ref[:, cut])
        head_row = jnp.where(head_row >= 4, head_row + 4, head_row)
        tail_row, tail_lane = rows_of(tail_ref[:, cut])
        parts = [split3(v) for v in [res] + half]
        parts = [parts[c][p] for p in range(3) for c in range(4)]
        signed = [-v if i % 4 == 0 else v for i, v in enumerate(parts)]
        by_head = nt_dot(masked(parts, head_row, 40), onehot(head_lane))
        by_tail = nt_dot(masked(signed, tail_row, 8), onehot(tail_lane))
        total_head = by_head if total_head is None else total_head + by_head
        total_tail = by_tail if total_tail is None else total_tail + by_tail
    g_odd, s_odd = par[0], par[1]
    for c in range(4):
        head = total_head[40 * c : 40 * c + 40]
        tail = total_tail[8 * c : 8 * c + 8]
        for p in (1, 2):
            at = 4 * p + c
            head = head + total_head[40 * at : 40 * at + 40]
            tail = tail + total_tail[8 * at : 8 * at + 8]
        own_ref[4 * c : 4 * c + 4, :] = head[0:4] + tail[0:4]
        before, after, prev, nxt = (head[8 * i : 8 * i + 8] for i in range(1, 5))
        og_ref[c] = jnp.where(g_odd == 1, after, before)
        eg_ref[c] = jnp.where(g_odd == 1, before, after)
        os_ref[c] = jnp.where(s_odd == 1, nxt, prev)
        es_ref[c] = jnp.where(s_odd == 1, prev, nxt)


def prepare(par, idx_ref, coef_ref, margin_ref, send_ref, idx16_ref, coef16_ref, dinv_ref, send16_ref):
    count = idx_ref.shape[0]
    idx16_ref[0:count, :] = idx_ref[...]
    idx16_ref[count:16, :] = jnp.zeros((16 - count, idx_ref.shape[1]), jnp.int32)
    for k in range(4):
        wide = coef_ref[k].astype(F32)
        coef16_ref[k, 0:count, :] = wide
        coef16_ref[k, count:16, :] = jnp.zeros((16 - count, wide.shape[1]), F32)
        diag = (1.0 + margin_ref[k : k + 1, :]) * jnp.sum(jnp.abs(wide), axis=0, keepdims=True)
        inverse = 1.0 / diag
        for q in range(4):
            dinv_ref[4 * k + q : 4 * k + q + 1, :] = inverse[:, LANES * q : LANES * q + LANES]
    for a in range(2):
        for b in range(2):
            for q in range(4):
                at = 8 * a + 4 * b + q
                send16_ref[at : at + 1, :] = send_ref[a, b : b + 1, LANES * q : LANES * q + LANES]


def send_blocks(par, solved, send_ref, outs):
    g_odd, s_odd = par[0], par[1]
    og_ref, eg_ref, os_ref, es_ref = outs
    row, lane = rows_of(send_ref[...])
    for k in range(4):
        low, high = None, None
        got = []
        for half in range(2):
            part = slice(8 * half, 8 * half + 8)
            acc = lane_pick(solved[4 * k : 4 * k + 1], lane[part])
            for r in range(1, 4):
                acc = jnp.where(row[part] == r, lane_pick(solved[4 * k + r : 4 * k + r + 1], lane[part]), acc)
            got.append(acc)
        low, high = got
        og_ref[k] = jnp.where(g_odd == 1, high, low)
        eg_ref[k] = jnp.where(g_odd == 1, low, high)
        left = jnp.concatenate([low[0:4], high[0:4]], axis=0)
        right = jnp.concatenate([low[4:8], high[4:8]], axis=0)
        os_ref[k] = jnp.where(s_odd == 1, right, left)
        es_ref[k] = jnp.where(s_odd == 1, left, right)


def first_solve(par, own_ref, og, eg, os, es, send_ref, dinv_ref, rn_ref, y_ref, *outs):
    index = send_ref[...]
    row, lane = rows_of(index)
    lefts, rights = [], []
    values = []
    for c in range(4):
        before, after = sides(par[0], og[c], eg[c])
        prev, nxt = sides(par[1], os[c], es[c])
        low = before + jnp.concatenate([prev[0:4], nxt[0:4]], axis=0)
        high = after + jnp.concatenate([prev[4:8], nxt[4:8]], axis=0)
        values.append([split3(low), split3(high)])
    for half in range(2):
        for i in range(8):
            at = 8 * half + i
            cut = [values[c][half][p][i : i + 1] for p in range(3) for c in range(4)]
            lefts.append(masked(cut, row[at : at + 1], 8))
            rights.append(onehot(lane[at : at + 1]))
    total = nt_dot(jnp.concatenate(lefts, axis=1), jnp.concatenate(rights, axis=1))
    rows = []
    for c in range(4):
        rows.append(sum(total[8 * (4 * p + c) : 8 * (4 * p + c) + 4] for p in range(3)))
    rn = own_ref[...] + jnp.concatenate(rows, axis=0)
    solved = rn * dinv_ref[...]
    rn_ref[...] = rn
    y_ref[...] = solved
    send_blocks(par, solved, send_ref, outs)


def tables(par, y, og, eg, os, es):
    result = []
    for k in range(4):
        before, after = sides(par[0], og[k], eg[k])
        prev, nxt = sides(par[1], os[k], es[k])
        blocks = [y[4 * k : 4 * k + 4], before, after, prev, nxt]
        result.append([block[r : r + 1] for block in blocks for r in range(block.shape[0])])
    return result


def gathered(table, index):
    rows, lanes = zip(*(rows_of(i) for i in index))
    acc = [[None] * 4 for _ in index]
    for r in range(len(table[0])):
        for v in range(len(index)):
            mask = rows[v] == r
            for k in range(4):
                got = lane_pick(table[k][r], lanes[v])
                acc[v][k] = got if r == 0 else jnp.where(mask, got, acc[v][k])
    return acc


def sweep(par, y_ref, og, eg, os, es, idx_ref, coef_ref, rn_ref, dinv_ref, send_ref, new_ref, *outs):
    table = tables(par, y_ref[...], og, eg, os, es)
    index = [idx_ref[8 * u : 8 * u + 8, LANES * q : LANES * q + LANES] for q in range(4) for u in range(2)]
    got = gathered(table, index)
    rows = []
    for k in range(4):
        for q in range(4):
            cols = slice(LANES * q, LANES * q + LANES)
            total = got[2 * q][k] * coef_ref[k, 0:8, cols] + got[2 * q + 1][k] * coef_ref[k, 8:16, cols]
            rows.append(jnp.sum(total, axis=0, keepdims=True))
    solved = (rn_ref[...] - jnp.concatenate(rows, axis=0)) * dinv_ref[...]
    new_ref[...] = solved
    send_blocks(par, solved, send_ref, outs)


def edge_values(par, y_ref, og, eg, os, es, res_ref, scale_ref, tan_ref, tail_ref, head_ref, out_ref):
    table = tables(par, y_ref[...], og, eg, os, es)
    groups = res_ref.shape[0] // 8
    heads = gathered(table, [head_ref[8 * v : 8 * v + 8] for v in range(groups)])
    tails = gathered([t[:4] for t in table], [tail_ref[8 * v : 8 * v + 8] for v in range(groups)])
    for v in range(groups):
        part = slice(8 * v, 8 * v + 8)
        total = scale_ref[part] * res_ref[part] + (heads[v][0] - tails[v][0])
        mixed = None
        for c in range(3):
            pieces = [tan_ref[c : c + 1, LANES * i : LANES * i + LANES] for i in range(8 * v, 8 * v + 8)]
            term = jnp.concatenate(pieces, axis=0) * (tails[v][c + 1] + heads[v][c + 1])
            mixed = term if mixed is None else mixed + term
        out_ref[part] = total + 0.5 * mixed


def exchange(blocks):
    og, eg, os, es = blocks
    grp, sub = lax.axis_size("grp"), lax.axis_size("sub")
    og = lax.ppermute(og, "grp", pairs(grp, 1))
    eg = lax.ppermute(eg, "grp", pairs(grp, 0))
    os = lax.ppermute(os, "sub", pairs(sub, 1))
    es = lax.ppermute(es, "sub", pairs(sub, 0))
    return og, eg, os, es


def body(
    residual,
    edge_scale,
    tangent,
    edge_tail,
    edge_head,
    stencil_index,
    stencil_coef,
    diag_margin,
    send_index,
):
    nodes = diag_margin.shape[1]
    par = jnp.stack([lax.axis_index("grp") % 2, lax.axis_index("sub") % 2]).astype(jnp.int32)
    own = ((16, LANES), F32)
    block = [((4, 8, LANES), F32)] * 4
    flat = lambda x: x.reshape(1, -1)
    tile = lambda x: x.reshape(-1, LANES)

    partial, *ghost = call(edge_sums, [own] + block, par, flat(residual), tangent, flat(edge_tail), flat(edge_head))
    idx16, coef16, dinv, send16 = call(
        prepare,
        [((16, nodes), jnp.int32), ((4, 16, nodes), F32), own, ((16, LANES), jnp.int32)],
        par, stencil_index, stencil_coef, diag_margin, send_index,
    )
    ghost = exchange(ghost)
    rn, solved, *blocks = call(first_solve, [own, own] + block, par, partial, *ghost, send16, dinv)
    for _ in range(SWEEPS - 1):
        blocks = exchange(blocks)
        solved, *blocks = call(
            sweep, [own] + block, par, solved, *blocks, idx16, coef16, rn, dinv, send16
        )
    blocks = exchange(blocks)
    (out,) = call(
        edge_values,
        [((residual.shape[0] // LANES, LANES), F32)],
        par, solved, *blocks, tile(residual), tile(edge_scale), tangent, tile(edge_tail), tile(edge_head),
    )
    return out.reshape(-1)


def solution(mesh):
    return jax.shard_map(
        body,
        mesh=mesh,
        in_specs=(
            P(("grp", "sub")),
            P(("grp", "sub")),
            P(None, ("grp", "sub")),
            P(("grp", "sub")),
            P(("grp", "sub")),
            P(None, ("grp", "sub")),
            P(None, None, ("grp", "sub")),
            P(None, ("grp", "sub")),
            P("grp", "sub", None),
        ),
        out_specs=P(("grp", "sub")),
        check_vma=False,
    )
```

time: 341 us -> 110 us (0.32)
  local copies, waits for them, and re-layouts: 157 us -> 3.63 us
  other arithmetic: 66.3 us -> 0.65 us
  Pallas kernels: 0 us -> 20.6 us
  waiting for transfers between devices: 19.2 us -> 4.4 us
  starting transfers between devices: 94 us -> 79.7 us
    gather x16 -> x0, local copies, waits for them, and re-layouts: 128 us -> none  [the longest x6 85.7 us: body(): widened[:, stencil_index]]
    scatter-add x6 -> x0, other arithmetic: 62.3 us -> none  [the longest x2 35.9 us: body(): edge_terms.at[:, edge_tail].add(vals_tail).at[:, edge_head].add(vals_head)]
    pallas_call x0 -> x7, Pallas kernels: none -> 20.6 us  [call(): pl.pallas_call(kernel, out_shape=[jax.ShapeDtypeStruct(shape, dtype) for...]
    ppermute x20, waiting for transfers between devices: 19.2 us -> 4.4 us  [the longest x5 3.55 us: exchange(): es = lax.ppermute(es, 'sub', pairs(sub, 0))]
    ppermute x20, starting transfers between devices: 94 us -> 79.7 us  [the longest x5 36.1 us: exchange(): og = lax.ppermute(og, 'grp', pairs(grp, 1))]
    slice x31 -> x0, local copies, waits for them, and re-layouts: 7.9 us -> none  [the longest x2 3.6 us: body(): at_tail[1:] + at_head[1:]]
    unnamed x42 -> x43, local copies, waits for them, and re-layouts: 11.3 us -> 3.63 us
    concatenate x6 -> x0, local copies, waits for them, and re-layouts: 5.88 us -> none  [the longest x4 2.55 us: ghost_values(): return jnp.concatenate([owned_vals] + flat_pieces, axis=1)]
  transfers between devices with their start and end apart: 20 -> 20, of which waited for: 10 -> 5; matrix products, arithmetic and copies ran while one was open for 9% -> 1% of each run, Pallas kernels for 0% -> 1%
where the time goes in v1:
time: 110 us; the launch traced here: 109 us
  starting transfers between devices  79.7 us (72%)
  Pallas kernels  20.6 us (19%)
  waiting for transfers between devices  4.4 us (4%)
  local copies, waits for them, and re-layouts  3.63 us (3%)
    ppermute x5, starting transfers between devices, exchange(): og = lax.ppermute(og, 'grp', pairs(grp, 1))  36.1 us
    ppermute x5, starting transfers between devices, exchange(): os = lax.ppermute(os, 'sub', pairs(sub, 1))  22.1 us
    pallas_call x7, Pallas kernels, call(): pl.pallas_call(kernel, out_shape=[jax.ShapeDtypeStruct(shape, dtype) for...  20.6 us
    ppermute x5, starting transfers between devices, exchange(): es = lax.ppermute(es, 'sub', pairs(sub, 0))  11.1 us
    ppermute x5, starting transfers between devices, exchange(): eg = lax.ppermute(eg, 'grp', pairs(grp, 0))  10.5 us
    unnamed x43, local copies, waits for them, and re-layouts  3.63 us
    ppermute x5, waiting for transfers between devices, exchange(): es = lax.ppermute(es, 'sub', pairs(sub, 0))  3.55 us
  transfers between devices with their start and end apart: 20, of which 5 were waited for; matrix products, arithmetic and copies ran while one was open for 1% of the time, Pallas kernels for 1%

profile of v1, /device:TPU:1, one launch (start us, length us, event | category | flops | bytes accessed | tf_op | source)
XLA Modules:
  0.0 109.4 jit_solution(16293472715978127810)
XLA Ops:
  0.0 0.6 pad_add_fusion.par
  0.6 2.6 %shard_map.91 = (f32[16,128]{1,0:T(8,128)}, f32[4,8,128]{2,1,0:T(8,128)}, f32[4,8,128]{2,1,0:T(8,128)}, f32[4,8,128]{2,1,0:T(8,128)}, f32[4,8,128]{2,1,0:T(8,128)}) custom-call(s32[2]{0:T(128)} %pad_add_fusion.par, f32[1,3072]{1,0:T(1,128)} %bitcast.10, f32[3,3072]{1,0:T(4,128)} %tan_ref.3, s32[1,3072]{1,0:T(1,128)} %bitcast.12, s32[1,3072]{1,0:T(1,128)} %bitcast.14), custom_call_target="tpu_custom_call" | custom-call | tf_op jit(solution)/shard_map/pallas_call | solution.py:17
  3.3 18.3 %collective-permute-start = (f32[4,8,128]{2,1,0:T(8,128)}, f32[4,8,128]{2,1,0:T(8,128)S(1)}, u32[]{:S(2)}, u32[]{:S(2)}) collective-permute-start(f32[4,8,128]{2,1,0:T(8,128)} %get-tuple-element.36), channel_id=1, source_target_pairs={{8,16},{16,8},{24,32},{32,24},{40,48},{48,40},{56,64},{64,56},{72,... | collective-permute-start | bytes 49160 | tf_op jit(solution)/shard_map/ppermute | solution.py:231
  21.6 1.9 %collective-permute-start.1 = (f32[4,8,128]{2,1,0:T(8,128)}, f32[4,8,128]{2,1,0:T(8,128)S(1)}, u32[]{:S(2)}, u32[]{:S(2)}) collective-permute-start(f32[4,8,128]{2,1,0:T(8,128)} %get-tuple-element.37), channel_id=1, source_target_pairs={{0,8},{8,0},{16,24},{24,16},{32,40},{40,32},{48,56},{56,48},{64,72... | collective-permute-start | bytes 49160 | tf_op jit(solution)/shard_map/ppermute | solution.py:232
  23.5 5.1 %collective-permute-start.2 = (f32[4,8,128]{2,1,0:T(8,128)}, f32[4,8,128]{2,1,0:T(8,128)S(1)}, u32[]{:S(2)}, u32[]{:S(2)}) collective-permute-start(f32[4,8,128]{2,1,0:T(8,128)} %get-tuple-element.38), channel_id=1, source_target_pairs={{1,2},{2,1},{3,4},{4,3},{5,6},{6,5},{7,0},{0,7},{9,10},{10,9},{11,... | collective-permute-start | bytes 49160 | tf_op jit(solution)/shard_map/ppermute | solution.py:233
  28.6 2.2 %collective-permute-start.3 = (f32[4,8,128]{2,1,0:T(8,128)}, f32[4,8,128]{2,1,0:T(8,128)S(1)}, u32[]{:S(2)}, u32[]{:S(2)}) collective-permute-start(f32[4,8,128]{2,1,0:T(8,128)} %get-tuple-element.39), channel_id=1, source_target_pairs={{0,1},{1,0},{2,3},{3,2},{4,5},{5,4},{6,7},{7,6},{8,9},{9,8},{10,11... | collective-permute-start | bytes 49160 | tf_op jit(solution)/shard_map/ppermute | solution.py:234
  30.8 0.6 copy.10.coef_ref
  31.5 1.6 %shard_map.92 = (s32[16,512]{1,0:T(8,128)}, f32[4,16,512]{2,1,0:T(8,128)}, f32[16,128]{1,0:T(8,128)}, s32[16,128]{1,0:T(8,128)}) custom-call(s32[2]{0:T(128)} %pad_add_fusion.par, s32[14,512]{1,0:T(8,128)} %idx_ref.1, bf16[4,14,512]{2,1,0:T(8,128)(2,1)} %copy.10.coef_ref, f32[4,512]{1,0:T(4,128)} %margin_ref.1, s32[2,2,512]{2,1,0:T(2,128)} %send_ref.1), custom_call_target="tpu_custom_call" | custom-call | tf_op jit(solution)/shard_map/pallas_call | solution.py:17
  33.0 0.0 collective-permute-done.1.eg
  33.1 0.0 collective-permute-done.2.os
  33.1 0.5 copy-done.17
  33.6 0.0 copy-done.18
  33.7 0.0 copy-done.19
  33.7 0.0 copy-done.20
  33.7 1.9 %shard_map.93 = (f32[16,128]{1,0:T(8,128)}, f32[16,128]{1,0:T(8,128)}, f32[4,8,128]{2,1,0:T(8,128)}, f32[4,8,128]{2,1,0:T(8,128)}, f32[4,8,128]{2,1,0:T(8,128)}, /*index=5*/f32[4,8,128]{2,1,0:T(8,128)}) custom-call(s32[2]{0:T(128)} %pad_add_fusion.par, f32[16,128]{1,0:T(8,128)} %get-tuple-element.35.own_ref, f32[4,8,128]{2,1,0:T(8,128)} %copy-done.17, ...), custom_call_target="tpu_custom_call" | custom-call | tf_op jit(solution)/shard_map/pallas_call | solution.py:17
  35.6 2.4 %collective-permute-start.4 = (f32[4,8,128]{2,1,0:T(8,128)}, f32[4,8,128]{2,1,0:T(8,128)S(1)}, u32[]{:S(2)}, u32[]{:S(2)}) collective-permute-start(f32[4,8,128]{2,1,0:T(8,128)} %get-tuple-element.43), channel_id=1, source_target_pairs={{8,16},{16,8},{24,32},{32,24},{40,48},{48,40},{56,64},{64,56},{72,... | collective-permute-start | bytes 49160 | tf_op jit(solution)/shard_map/ppermute | solution.py:231
  38.0 2.8 %collective-permute-start.5 = (f32[4,8,128]{2,1,0:T(8,128)}, f32[4,8,128]{2,1,0:T(8,128)S(1)}, u32[]{:S(2)}, u32[]{:S(2)}) collective-permute-start(f32[4,8,128]{2,1,0:T(8,128)} %get-tuple-element.44), channel_id=1, source_target_pairs={{0,8},{8,0},{16,24},{24,16},{32,40},{40,32},{48,56},{56,48},{64,72... | collective-permute-start | bytes 49160 | tf_op jit(solution)/shard_map/ppermute | solution.py:232
  40.9 5.2 %collective-permute-start.6 = (f32[4,8,128]{2,1,0:T(8,128)}, f32[4,8,128]{2,1,0:T(8,128)S(1)}, u32[]{:S(2)}, u32[]{:S(2)}) collective-permute-start(f32[4,8,128]{2,1,0:T(8,128)} %get-tuple-element.45), channel_id=1, source_target_pairs={{1,2},{2,1},{3,4},{4,3},{5,6},{6,5},{7,0},{0,7},{9,10},{10,9},{11,... | collective-permute-start | bytes 49160 | tf_op jit(solution)/shard_map/ppermute | solution.py:233
  46.0 1.9 %collective-permute-start.7 = (f32[4,8,128]{2,1,0:T(8,128)}, f32[4,8,128]{2,1,0:T(8,128)S(1)}, u32[]{:S(2)}, u32[]{:S(2)}) collective-permute-start(f32[4,8,128]{2,1,0:T(8,128)} %get-tuple-element.46), channel_id=1, source_target_pairs={{0,1},{1,0},{2,3},{3,2},{4,5},{5,4},{6,7},{7,6},{8,9},{9,8},{10,11... | collective-permute-start | bytes 49160 | tf_op jit(solution)/shard_map/ppermute | solution.py:234
  48.0 0.0 collective-permute-done.4.og
  48.0 0.0 collective-permute-done.6.os
  48.0 1.3 %collective-permute-done.7.es = f32[4,8,128]{2,1,0:T(8,128)S(1)} collective-permute-done((f32[4,8,128]{2,1,0:T(8,128)}, f32[4,8,128]{2,1,0:T(8,128)S(1)}, u32[]{:S(2)}, u32[]{:S(2)}) %collective-permute-start.7) | collective-permute-done | bytes 16416 | tf_op jit(solution)/shard_map/ppermute | solution.py:234
  49.3 0.6 copy-done.13
  49.9 4.0 %shard_map.94 = (f32[16,128]{1,0:T(8,128)}, f32[4,8,128]{2,1,0:T(8,128)}, f32[4,8,128]{2,1,0:T(8,128)}, f32[4,8,128]{2,1,0:T(8,128)}, f32[4,8,128]{2,1,0:T(8,128)}) custom-call(s32[2]{0:T(128)} %pad_add_fusion.par, f32[16,128]{1,0:T(8,128)} %get-tuple-element.42.y_ref, f32[4,8,128]{2,1,0:T(8,128)} %copy-done.3, f32[4,8,128]{2,1,0:T(8,128)} %copy-done.6, ...), custom_call_target="tpu_custom_call" | custom-call | tf_op jit(solution)/shard_map/pallas_call | solution.py:17
  54.0 5.8 %collective-permute-start.8 = (f32[4,8,128]{2,1,0:T(8,128)}, f32[4,8,128]{2,1,0:T(8,128)S(1)}, u32[]{:S(2)}, u32[]{:S(2)}) collective-permute-start(f32[4,8,128]{2,1,0:T(8,128)} %get-tuple-element.51), channel_id=1, source_target_pairs={{8,16},{16,8},{24,32},{32,24},{40,48},{48,40},{56,64},{64,56},{72,... | collective-permute-start | bytes 49160 | tf_op jit(solution)/shard_map/ppermute | solution.py:231
  59.8 1.9 %collective-permute-start.9 = (f32[4,8,128]{2,1,0:T(8,128)}, f32[4,8,128]{2,1,0:T(8,128)S(1)}, u32[]{:S(2)}, u32[]{:S(2)}) collective-permute-start(f32[4,8,128]{2,1,0:T(8,128)} %get-tuple-element.52), channel_id=1, source_target_pairs={{0,8},{8,0},{16,24},{24,16},{32,40},{40,32},{48,56},{56,48},{64,72... | collective-permute-start | bytes 49160 | tf_op jit(solution)/shard_map/ppermute | solution.py:232
  61.7 3.2 %collective-permute-start.10 = (f32[4,8,128]{2,1,0:T(8,128)}, f32[4,8,128]{2,1,0:T(8,128)S(1)}, u32[]{:S(2)}, u32[]{:S(2)}) collective-permute-start(f32[4,8,128]{2,1,0:T(8,128)} %get-tuple-element.53), channel_id=1, source_target_pairs={{1,2},{2,1},{3,4},{4,3},{5,6},{6,5},{7,0},{0,7},{9,10},{10,9},{11,... | collective-permute-start | bytes 49160 | tf_op jit(solution)/shard_map/ppermute | solution.py:233
  64.9 2.1 %collective-permute-start.11 = (f32[4,8,128]{2,1,0:T(8,128)}, f32[4,8,128]{2,1,0:T(8,128)S(1)}, u32[]{:S(2)}, u32[]{:S(2)}) collective-permute-start(f32[4,8,128]{2,1,0:T(8,128)} %get-tuple-element.54), channel_id=1, source_target_pairs={{0,1},{1,0},{2,3},{3,2},{4,5},{5,4},{6,7},{7,6},{8,9},{9,8},{10,11... | collective-permute-start | bytes 49160 | tf_op jit(solution)/shard_map/ppermute | solution.py:234
  67.0 0.0 collective-permute-done.8.og
  67.1 0.8 collective-permute-done.10.os
  67.9 0.3 collective-permute-done.11.es
  68.2 0.3 copy-done.11
  68.5 0.3 copy-done.14
  68.8 4.0 %shard_map.95 = (f32[16,128]{1,0:T(8,128)}, f32[4,8,128]{2,1,0:T(8,128)}, f32[4,8,128]{2,1,0:T(8,128)}, f32[4,8,128]{2,1,0:T(8,128)}, f32[4,8,128]{2,1,0:T(8,128)}) custom-call(s32[2]{0:T(128)} %pad_add_fusion.par, f32[16,128]{1,0:T(8,128)} %get-tuple-element.50.y_ref, f32[4,8,128]{2,1,0:T(8,128)} %copy-done.4, f32[4,8,128]{2,1,0:T(8,128)} %copy-done.7, ...), custom_call_target="tpu_custom_call" | custom-call | tf_op jit(solution)/shard_map/pallas_call | solution.py:17
  72.9 3.6 %collective-permute-start.12 = (f32[4,8,128]{2,1,0:T(8,128)}, f32[4,8,128]{2,1,0:T(8,128)S(1)}, u32[]{:S(2)}, u32[]{:S(2)}) collective-permute-start(f32[4,8,128]{2,1,0:T(8,128)} %get-tuple-element.56), channel_id=1, source_target_pairs={{8,16},{16,8},{24,32},{32,24},{40,48},{48,40},{56,64},{64,56},{72,... | collective-permute-start | bytes 49160 | tf_op jit(solution)/shard_map/ppermute | solution.py:231
  76.5 1.9 %collective-permute-start.13 = (f32[4,8,128]{2,1,0:T(8,128)}, f32[4,8,128]{2,1,0:T(8,128)S(1)}, u32[]{:S(2)}, u32[]{:S(2)}) collective-permute-start(f32[4,8,128]{2,1,0:T(8,128)} %get-tuple-element.57), channel_id=1, source_target_pairs={{0,8},{8,0},{16,24},{24,16},{32,40},{40,32},{48,56},{56,48},{64,72... | collective-permute-start | bytes 49160 | tf_op jit(solution)/shard_map/ppermute | solution.py:232
  78.4 4.4 %collective-permute-start.14 = (f32[4,8,128]{2,1,0:T(8,128)}, f32[4,8,128]{2,1,0:T(8,128)S(1)}, u32[]{:S(2)}, u32[]{:S(2)}) collective-permute-start(f32[4,8,128]{2,1,0:T(8,128)} %get-tuple-element.58), channel_id=1, source_target_pairs={{1,2},{2,1},{3,4},{4,3},{5,6},{6,5},{7,0},{0,7},{9,10},{10,9},{11,... | collective-permute-start | bytes 49160 | tf_op jit(solution)/shard_map/ppermute | solution.py:233
  82.9 2.4 %collective-permute-start.15 = (f32[4,8,128]{2,1,0:T(8,128)}, f32[4,8,128]{2,1,0:T(8,128)S(1)}, u32[]{:S(2)}, u32[]{:S(2)}) collective-permute-start(f32[4,8,128]{2,1,0:T(8,128)} %get-tuple-element.59), channel_id=1, source_target_pairs={{0,1},{1,0},{2,3},{3,2},{4,5},{5,4},{6,7},{7,6},{8,9},{9,8},{10,11... | collective-permute-start | bytes 49160 | tf_op jit(solution)/shard_map/ppermute | solution.py:234
  85.3 1.0 collective-permute-done.15.es
  86.3 0.6 copy-done.8
  86.9 4.0 %shard_map.96 = (f32[16,128]{1,0:T(8,128)}, f32[4,8,128]{2,1,0:T(8,128)}, f32[4,8,128]{2,1,0:T(8,128)}, f32[4,8,128]{2,1,0:T(8,128)}, f32[4,8,128]{2,1,0:T(8,128)}) custom-call(s32[2]{0:T(128)} %pad_add_fusion.par, f32[16,128]{1,0:T(8,128)} %get-tuple-element.55.y_ref, f32[4,8,128]{2,1,0:T(8,128)} %copy-done.1, f32[4,8,128]{2,1,0:T(8,128)} %copy-done.2, ...), custom_call_target="tpu_custom_call" | custom-call | tf_op jit(solution)/shard_map/pallas_call | solution.py:17
  90.9 5.8 %collective-permute-start.16 = (f32[4,8,128]{2,1,0:T(8,128)}, f32[4,8,128]{2,1,0:T(8,128)S(1)}, u32[]{:S(2)}, u32[]{:S(2)}) collective-permute-start(f32[4,8,128]{2,1,0:T(8,128)} %get-tuple-element.61), channel_id=1, source_target_pairs={{8,16},{16,8},{24,32},{32,24},{40,48},{48,40},{56,64},{64,56},{72,... | collective-permute-start | bytes 49160 | tf_op jit(solution)/shard_map/ppermute | solution.py:231
  96.8 1.9 %collective-permute-start.17 = (f32[4,8,128]{2,1,0:T(8,128)}, f32[4,8,128]{2,1,0:T(8,128)S(1)}, u32[]{:S(2)}, u32[]{:S(2)}) collective-permute-start(f32[4,8,128]{2,1,0:T(8,128)} %get-tuple-element.62), channel_id=1, source_target_pairs={{0,8},{8,0},{16,24},{24,16},{32,40},{40,32},{48,56},{56,48},{64,72... | collective-permute-start | bytes 49160 | tf_op jit(solution)/shard_map/ppermute | solution.py:232
  98.7 4.2 %collective-permute-start.18 = (f32[4,8,128]{2,1,0:T(8,128)}, f32[4,8,128]{2,1,0:T(8,128)S(1)}, u32[]{:S(2)}, u32[]{:S(2)}) collective-permute-start(f32[4,8,128]{2,1,0:T(8,128)} %get-tuple-element.63), channel_id=1, source_target_pairs={{1,2},{2,1},{3,4},{4,3},{5,6},{6,5},{7,0},{0,7},{9,10},{10,9},{11,... | collective-permute-start | bytes 49160 | tf_op jit(solution)/shard_map/ppermute | solution.py:233
  103.0 2.4 %collective-permute-start.19 = (f32[4,8,128]{2,1,0:T(8,128)}, f32[4,8,128]{2,1,0:T(8,128)S(1)}, u32[]{:S(2)}, u32[]{:S(2)}) collective-permute-start(f32[4,8,128]{2,1,0:T(8,128)} %get-tuple-element.64), channel_id=1, source_target_pairs={{0,1},{1,0},{2,3},{3,2},{4,5},{5,4},{6,7},{7,6},{8,9},{9,8},{10,11... | collective-permute-start | bytes 49160 | tf_op jit(solution)/shard_map/ppermute | solution.py:234
  105.4 1.0 collective-permute-done.19.es
  106.4 0.6 copy-done.16
  107.0 2.4 %shard_map.97 = f32[24,128]{1,0:T(8,128)} custom-call(s32[2]{0:T(128)} %pad_add_fusion.par, f32[16,128]{1,0:T(8,128)} %get-tuple-element.60.y_ref, f32[4,8,128]{2,1,0:T(8,128)} %copy-done.9, f32[4,8,128]{2,1,0:T(8,128)} %copy-done.12, f32[4,8,128]{2,1,0:T(8,128)} %copy-done.15, f32[4,8,128]{2,1,0:T(8,128)} %copy-done.16, f32[24,128]{1,0:T(8,128)} %bitcast.11, ...), custom_call_target="tpu_custom_call" | custom-call | tf_op jit(solution)/shard_map/pallas_call | solution.py:17
  (43 shorter events, 0.1 us)
Async XLA Ops:
  0.0 30.8 %copy-start = (bf16[4,14,512]{2,0,1:T(4,128)(2,1)S(1)}, bf16[4,14,512]{2,0,1:T(4,128)(2,1)}, u32[]{:S(2)}) copy-start(bf16[4,14,512]{2,0,1:T(4,128)(2,1)} %param.15) | copy-start | bytes 172036
  3.3 29.8 %collective-permute-start = (f32[4,8,128]{2,1,0:T(8,128)}, f32[4,8,128]{2,1,0:T(8,128)S(1)}, u32[]{:S(2)}, u32[]{:S(2)}) collective-permute-start(f32[4,8,128]{2,1,0:T(8,128)} %get-tuple-element.36), channel_id=1, source_target_pairs={{8,16},{16,8},{24,32},{32,24},{40,48},{48,40},{56,64},{64,56},{72,... | collective-permute-start | bytes 49160 | tf_op jit(solution)/shard_map/ppermute | solution.py:231
  21.6 11.4 %collective-permute-start.1 = (f32[4,8,128]{2,1,0:T(8,128)}, f32[4,8,128]{2,1,0:T(8,128)S(1)}, u32[]{:S(2)}, u32[]{:S(2)}) collective-permute-start(f32[4,8,128]{2,1,0:T(8,128)} %get-tuple-element.37), channel_id=1, source_target_pairs={{0,8},{8,0},{16,24},{24,16},{32,40},{40,32},{48,56},{56,48},{64,72... | collective-permute-start | bytes 49160 | tf_op jit(solution)/shard_map/ppermute | solution.py:232
  23.5 9.5 %collective-permute-start.2 = (f32[4,8,128]{2,1,0:T(8,128)}, f32[4,8,128]{2,1,0:T(8,128)S(1)}, u32[]{:S(2)}, u32[]{:S(2)}) collective-permute-start(f32[4,8,128]{2,1,0:T(8,128)} %get-tuple-element.38), channel_id=1, source_target_pairs={{1,2},{2,1},{3,4},{4,3},{5,6},{6,5},{7,0},{0,7},{9,10},{10,9},{11,... | collective-permute-start | bytes 49160 | tf_op jit(solution)/shard_map/ppermute | solution.py:233
  28.6 4.5 %collective-permute-start.3 = (f32[4,8,128]{2,1,0:T(8,128)}, f32[4,8,128]{2,1,0:T(8,128)S(1)}, u32[]{:S(2)}, u32[]{:S(2)}) collective-permute-start(f32[4,8,128]{2,1,0:T(8,128)} %get-tuple-element.39), channel_id=1, source_target_pairs={{0,1},{1,0},{2,3},{3,2},{4,5},{5,4},{6,7},{7,6},{8,9},{9,8},{10,11... | collective-permute-start | bytes 49160 | tf_op jit(solution)/shard_map/ppermute | solution.py:234
  33.0 0.6 copy-start.17
  33.1 0.6 copy-start.18
  33.1 0.6 copy-start.19
  33.1 0.6 copy-start.20
  35.6 12.4 %collective-permute-start.4 = (f32[4,8,128]{2,1,0:T(8,128)}, f32[4,8,128]{2,1,0:T(8,128)S(1)}, u32[]{:S(2)}, u32[]{:S(2)}) collective-permute-start(f32[4,8,128]{2,1,0:T(8,128)} %get-tuple-element.43), channel_id=1, source_target_pairs={{8,16},{16,8},{24,32},{32,24},{40,48},{48,40},{56,64},{64,56},{72,... | collective-permute-start | bytes 49160 | tf_op jit(solution)/shard_map/ppermute | solution.py:231
  38.0 10.0 %collective-permute-start.5 = (f32[4,8,128]{2,1,0:T(8,128)}, f32[4,8,128]{2,1,0:T(8,128)S(1)}, u32[]{:S(2)}, u32[]{:S(2)}) collective-permute-start(f32[4,8,128]{2,1,0:T(8,128)} %get-tuple-element.44), channel_id=1, source_target_pairs={{0,8},{8,0},{16,24},{24,16},{32,40},{40,32},{48,56},{56,48},{64,72... | collective-permute-start | bytes 49160 | tf_op jit(solution)/shard_map/ppermute | solution.py:232
  40.9 7.1 %collective-permute-start.6 = (f32[4,8,128]{2,1,0:T(8,128)}, f32[4,8,128]{2,1,0:T(8,128)S(1)}, u32[]{:S(2)}, u32[]{:S(2)}) collective-permute-start(f32[4,8,128]{2,1,0:T(8,128)} %get-tuple-element.45), channel_id=1, source_target_pairs={{1,2},{2,1},{3,4},{4,3},{5,6},{6,5},{7,0},{0,7},{9,10},{10,9},{11,... | collective-permute-start | bytes 49160 | tf_op jit(solution)/shard_map/ppermute | solution.py:233
  46.0 3.3 %collective-permute-start.7 = (f32[4,8,128]{2,1,0:T(8,128)}, f32[4,8,128]{2,1,0:T(8,128)S(1)}, u32[]{:S(2)}, u32[]{:S(2)}) collective-permute-start(f32[4,8,128]{2,1,0:T(8,128)} %get-tuple-element.46), channel_id=1, source_target_pairs={{0,1},{1,0},{2,3},{3,2},{4,5},{5,4},{6,7},{7,6},{8,9},{9,8},{10,11... | collective-permute-start | bytes 49160 | tf_op jit(solution)/shard_map/ppermute | solution.py:234
  48.0 1.4 %copy-start.3 = (f32[4,8,128]{2,1,0:T(8,128)}, f32[4,8,128]{2,1,0:T(8,128)S(1)}, u32[]{:S(2)}) copy-start(f32[4,8,128]{2,1,0:T(8,128)S(1)} %collective-permute-done.4.og) | copy-start | bytes 49156
  48.0 1.3 %copy-start.6 = (f32[4,8,128]{2,1,0:T(8,128)}, f32[4,8,128]{2,1,0:T(8,128)S(1)}, u32[]{:S(2)}) copy-start(f32[4,8,128]{2,1,0:T(8,128)S(1)} %collective-permute-done.5.eg) | copy-start | bytes 49156
  48.0 1.3 %copy-start.10 = (f32[4,8,128]{2,1,0:T(8,128)}, f32[4,8,128]{2,1,0:T(8,128)S(1)}, u32[]{:S(2)}) copy-start(f32[4,8,128]{2,1,0:T(8,128)S(1)} %collective-permute-done.6.os) | copy-start | bytes 49156
  49.3 0.6 copy-start.13
  54.0 13.1 %collective-permute-start.8 = (f32[4,8,128]{2,1,0:T(8,128)}, f32[4,8,128]{2,1,0:T(8,128)S(1)}, u32[]{:S(2)}, u32[]{:S(2)}) collective-permute-start(f32[4,8,128]{2,1,0:T(8,128)} %get-tuple-element.51), channel_id=1, source_target_pairs={{8,16},{16,8},{24,32},{32,24},{40,48},{48,40},{56,64},{64,56},{72,... | collective-permute-start | bytes 49160 | tf_op jit(solution)/shard_map/ppermute | solution.py:231
  59.8 7.3 %collective-permute-start.9 = (f32[4,8,128]{2,1,0:T(8,128)}, f32[4,8,128]{2,1,0:T(8,128)S(1)}, u32[]{:S(2)}, u32[]{:S(2)}) collective-permute-start(f32[4,8,128]{2,1,0:T(8,128)} %get-tuple-element.52), channel_id=1, source_target_pairs={{0,8},{8,0},{16,24},{24,16},{32,40},{40,32},{48,56},{56,48},{64,72... | collective-permute-start | bytes 49160 | tf_op jit(solution)/shard_map/ppermute | solution.py:232
  61.7 6.2 %collective-permute-start.10 = (f32[4,8,128]{2,1,0:T(8,128)}, f32[4,8,128]{2,1,0:T(8,128)S(1)}, u32[]{:S(2)}, u32[]{:S(2)}) collective-permute-start(f32[4,8,128]{2,1,0:T(8,128)} %get-tuple-element.53), channel_id=1, source_target_pairs={{1,2},{2,1},{3,4},{4,3},{5,6},{6,5},{7,0},{0,7},{9,10},{10,9},{11,... | collective-permute-start | bytes 49160 | tf_op jit(solution)/shard_map/ppermute | solution.py:233
  64.9 3.3 %collective-permute-start.11 = (f32[4,8,128]{2,1,0:T(8,128)}, f32[4,8,128]{2,1,0:T(8,128)S(1)}, u32[]{:S(2)}, u32[]{:S(2)}) collective-permute-start(f32[4,8,128]{2,1,0:T(8,128)} %get-tuple-element.54), channel_id=1, source_target_pairs={{0,1},{1,0},{2,3},{3,2},{4,5},{5,4},{6,7},{7,6},{8,9},{9,8},{10,11... | collective-permute-start | bytes 49160 | tf_op jit(solution)/shard_map/ppermute | solution.py:234
  67.1 1.2 %copy-start.4 = (f32[4,8,128]{2,1,0:T(8,128)}, f32[4,8,128]{2,1,0:T(8,128)S(1)}, u32[]{:S(2)}) copy-start(f32[4,8,128]{2,1,0:T(8,128)S(1)} %collective-permute-done.8.og) | copy-start | bytes 49156
  67.1 1.1 %copy-start.7 = (f32[4,8,128]{2,1,0:T(8,128)}, f32[4,8,128]{2,1,0:T(8,128)S(1)}, u32[]{:S(2)}) copy-start(f32[4,8,128]{2,1,0:T(8,128)S(1)} %collective-permute-done.9.eg) | copy-start | bytes 49156
  67.9 0.6 copy-start.11
  68.2 0.6 copy-start.14
  72.9 12.4 %collective-permute-start.12 = (f32[4,8,128]{2,1,0:T(8,128)}, f32[4,8,128]{2,1,0:T(8,128)S(1)}, u32[]{:S(2)}, u32[]{:S(2)}) collective-permute-start(f32[4,8,128]{2,1,0:T(8,128)} %get-tuple-element.56), channel_id=1, source_target_pairs={{8,16},{16,8},{24,32},{32,24},{40,48},{48,40},{56,64},{64,56},{72,... | collective-permute-start | bytes 49160 | tf_op jit(solution)/shard_map/ppermute | solution.py:231
  76.5 8.8 %collective-permute-start.13 = (f32[4,8,128]{2,1,0:T(8,128)}, f32[4,8,128]{2,1,0:T(8,128)S(1)}, u32[]{:S(2)}, u32[]{:S(2)}) collective-permute-start(f32[4,8,128]{2,1,0:T(8,128)} %get-tuple-element.57), channel_id=1, source_target_pairs={{0,8},{8,0},{16,24},{24,16},{32,40},{40,32},{48,56},{56,48},{64,72... | collective-permute-start | bytes 49160 | tf_op jit(solution)/shard_map/ppermute | solution.py:232
  78.4 6.9 %collective-permute-start.14 = (f32[4,8,128]{2,1,0:T(8,128)}, f32[4,8,128]{2,1,0:T(8,128)S(1)}, u32[]{:S(2)}, u32[]{:S(2)}) collective-permute-start(f32[4,8,128]{2,1,0:T(8,128)} %get-tuple-element.58), channel_id=1, source_target_pairs={{1,2},{2,1},{3,4},{4,3},{5,6},{6,5},{7,0},{0,7},{9,10},{10,9},{11,... | collective-permute-start | bytes 49160 | tf_op jit(solution)/shard_map/ppermute | solution.py:233
  82.9 3.4 %collective-permute-start.15 = (f32[4,8,128]{2,1,0:T(8,128)}, f32[4,8,128]{2,1,0:T(8,128)S(1)}, u32[]{:S(2)}, u32[]{:S(2)}) collective-permute-start(f32[4,8,128]{2,1,0:T(8,128)} %get-tuple-element.59), channel_id=1, source_target_pairs={{0,1},{1,0},{2,3},{3,2},{4,5},{5,4},{6,7},{7,6},{8,9},{9,8},{10,11... | collective-permute-start | bytes 49160 | tf_op jit(solution)/shard_map/ppermute | solution.py:234
  85.3 1.0 copy-start.1
  85.3 1.0 copy-start.2
  85.3 1.0 copy-start.5
  86.3 0.6 copy-start.8
  90.9 14.5 %collective-permute-start.16 = (f32[4,8,128]{2,1,0:T(8,128)}, f32[4,8,128]{2,1,0:T(8,128)S(1)}, u32[]{:S(2)}, u32[]{:S(2)}) collective-permute-start(f32[4,8,128]{2,1,0:T(8,128)} %get-tuple-element.61), channel_id=1, source_target_pairs={{8,16},{16,8},{24,32},{32,24},{40,48},{48,40},{56,64},{64,56},{72,... | collective-permute-start | bytes 49160 | tf_op jit(solution)/shard_map/ppermute | solution.py:231
  96.8 8.6 %collective-permute-start.17 = (f32[4,8,128]{2,1,0:T(8,128)}, f32[4,8,128]{2,1,0:T(8,128)S(1)}, u32[]{:S(2)}, u32[]{:S(2)}) collective-permute-start(f32[4,8,128]{2,1,0:T(8,128)} %get-tuple-element.62), channel_id=1, source_target_pairs={{0,8},{8,0},{16,24},{24,16},{32,40},{40,32},{48,56},{56,48},{64,72... | collective-permute-start | bytes 49160 | tf_op jit(solution)/shard_map/ppermute | solution.py:232
  98.7 6.7 %collective-permute-start.18 = (f32[4,8,128]{2,1,0:T(8,128)}, f32[4,8,128]{2,1,0:T(8,128)S(1)}, u32[]{:S(2)}, u32[]{:S(2)}) collective-permute-start(f32[4,8,128]{2,1,0:T(8,128)} %get-tuple-element.63), channel_id=1, source_target_pairs={{1,2},{2,1},{3,4},{4,3},{5,6},{6,5},{7,0},{0,7},{9,10},{10,9},{11,... | collective-permute-start | bytes 49160 | tf_op jit(solution)/shard_map/ppermute | solution.py:233
  103.0 3.4 %collective-permute-start.19 = (f32[4,8,128]{2,1,0:T(8,128)}, f32[4,8,128]{2,1,0:T(8,128)S(1)}, u32[]{:S(2)}, u32[]{:S(2)}) collective-permute-start(f32[4,8,128]{2,1,0:T(8,128)} %get-tuple-element.64), channel_id=1, source_target_pairs={{0,1},{1,0},{2,3},{3,2},{4,5},{5,4},{6,7},{7,6},{8,9},{9,8},{10,11... | collective-permute-start | bytes 49160 | tf_op jit(solution)/shard_map/ppermute | solution.py:234
  105.4 1.0 copy-start.9
  105.4 1.0 copy-start.12
  105.4 1.0 copy-start.15
  106.4 0.6 copy-start.16

commit v2 on v1

--- a/solution.py
+++ b/solution.py
@@ -10,15 +10,15 @@
 F32 = jnp.float32
 BF16 = jnp.bfloat16
 VMEM = pl.BlockSpec(memory_space=pltpu.VMEM)
-SMEM = pl.BlockSpec(memory_space=pltpu.SMEM)
-
-
-def call(kernel, outs, *args, flops=1 << 20):
+
+
+def call(kernel, outs, *args):
     return pl.pallas_call(
         kernel,
         out_shape=[jax.ShapeDtypeStruct(shape, dtype) for shape, dtype in outs],
-        in_specs=[SMEM] + [VMEM] * (len(args) - 1),
+        in_specs=[VMEM] * len(args),
         out_specs=[VMEM] * len(outs),
+        compiler_params=pltpu.CompilerParams(vmem_limit_bytes=16 << 20),
     )(*args)
 
 
@@ -63,13 +63,17 @@
     return jnp.concatenate([jnp.where(mask, v, 0.0) for v in values], axis=0).astype(BF16)
 
 
-def sides(par, odd, even):
-    low = jnp.where(par == 1, even, odd)
-    high = jnp.where(par == 1, odd, even)
+def odd(axis):
+    return jnp.bitwise_and(lax.axis_index(axis), 1)
+
+
+def sides(parity, by_odd, by_even):
+    low = jnp.where(parity == 1, by_even, by_odd)
+    high = jnp.where(parity == 1, by_odd, by_even)
     return low, high
 
 
-def edge_sums(par, res_ref, tan_ref, tail_ref, head_ref, own_ref, og_ref, eg_ref, os_ref, es_ref):
+def edge_sums(res_ref, tan_ref, tail_ref, head_ref, own_ref, og_ref, eg_ref, os_ref, es_ref):
     edges = res_ref.shape[1]
     chunk = 512
     total_head, total_tail = None, None
@@ -87,7 +91,7 @@
         by_tail = nt_dot(masked(signed, tail_row, 8), onehot(tail_lane))
         total_head = by_head if total_head is None else total_head + by_head
         total_tail = by_tail if total_tail is None else total_tail + by_tail
-    g_odd, s_odd = par[0], par[1]
+    g_odd, s_odd = odd("grp"), odd("sub")
     for c in range(4):
         head = total_head[40 * c : 40 * c + 40]
         tail = total_tail[8 * c : 8 * c + 8]
@@ -103,7 +107,7 @@
         es_ref[c] = jnp.where(s_odd == 1, prev, nxt)
 
 
-def prepare(par, idx_ref, coef_ref, margin_ref, send_ref, idx16_ref, coef16_ref, dinv_ref, send16_ref):
+def prepare(idx_ref, coef_ref, margin_ref, send_ref, idx16_ref, coef16_ref, dinv_ref, send16_ref):
     count = idx_ref.shape[0]
     idx16_ref[0:count, :] = idx_ref[...]
     idx16_ref[count:16, :] = jnp.zeros((16 - count, idx_ref.shape[1]), jnp.int32)
@@ -122,8 +126,8 @@
                 send16_ref[at : at + 1, :] = send_ref[a, b : b + 1, LANES * q : LANES * q + LANES]
 
 
-def send_blocks(par, solved, send_ref, outs):
-    g_odd, s_odd = par[0], par[1]
+def send_blocks(solved, send_ref, outs):
+    g_odd, s_odd = odd("grp"), odd("sub")
     og_ref, eg_ref, os_ref, es_ref = outs
     row, lane = rows_of(send_ref[...])
     for k in range(4):
@@ -144,14 +148,14 @@
         es_ref[k] = jnp.where(s_odd == 1, left, right)
 
 
-def first_solve(par, own_ref, og, eg, os, es, send_ref, dinv_ref, rn_ref, y_ref, *outs):
+def first_solve(own_ref, og, eg, os, es, send_ref, dinv_ref, rn_ref, y_ref, *outs):
     index = send_ref[...]
     row, lane = rows_of(index)
     lefts, rights = [], []
     values = []
     for c in range(4):
-        before, after = sides(par[0], og[c], eg[c])
-        prev, nxt = sides(par[1], os[c], es[c])
+        before, after = sides(odd("grp"), og[c], eg[c])
+        prev, nxt = sides(odd("sub"), os[c], es[c])
         low = before + jnp.concatenate([prev[0:4], nxt[0:4]], axis=0)
         high = after + jnp.concatenate([prev[4:8], nxt[4:8]], axis=0)
         values.append([split3(low), split3(high)])
@@ -169,14 +173,14 @@
     solved = rn * dinv_ref[...]
     rn_ref[...] = rn
     y_ref[...] = solved
-    send_blocks(par, solved, send_ref, outs)
-
-
-def tables(par, y, og, eg, os, es):
+    send_blocks(solved, send_ref, outs)
+
+
+def tables(y, og, eg, os, es):
     result = []
     for k in range(4):
-        before, after = sides(par[0], og[k], eg[k])
-        prev, nxt = sides(par[1], os[k], es[k])
+        before, after = sides(odd("grp"), og[k], eg[k])
+        prev, nxt = sides(odd("sub"), os[k], es[k])
         blocks = [y[4 * k : 4 * k + 4], before, after, prev, nxt]
         result.append([block[r : r + 1] for block in blocks for r in range(block.shape[0])])
     return result
@@ -194,8 +198,8 @@
     return acc
 
 
-def sweep(par, y_ref, og, eg, os, es, idx_ref, coef_ref, rn_ref, dinv_ref, send_ref, new_ref, *outs):
-    table = tables(par, y_ref[...], og, eg, os, es)
+def sweep(y_ref, og, eg, os, es, idx_ref, coef_ref, rn_ref, dinv_ref, send_ref, new_ref, *outs):
+    table = tables(y_ref[...], og, eg, os, es)
     index = [idx_ref[8 * u : 8 * u + 8, LANES * q : LANES * q + LANES] for q in range(4) for u in range(2)]
     got = gathered(table, index)
     rows = []
@@ -206,11 +210,11 @@
             rows.append(jnp.sum(total, axis=0, keepdims=True))
     solved = (rn_ref[...] - jnp.concatenate(rows, axis=0)) * dinv_ref[...]
     new_ref[...] = solved
-    send_blocks(par, solved, send_ref, outs)
-
-
-def edge_values(par, y_ref, og, eg, os, es, res_ref, scale_ref, tan_ref, tail_ref, head_ref, out_ref):
-    table = tables(par, y_ref[...], og, eg, os, es)
+    send_blocks(solved, send_ref, outs)
+
+
+def edge_values(y_ref, og, eg, os, es, res_ref, scale_ref, tan_ref, tail_ref, head_ref, out_ref):
+    table = tables(y_ref[...], og, eg, os, es)
     groups = res_ref.shape[0] // 8
     heads = gathered(table, [head_ref[8 * v : 8 * v + 8] for v in range(groups)])
     tails = gathered([t[:4] for t in table], [tail_ref[8 * v : 8 * v + 8] for v in range(groups)])
@@ -247,30 +251,29 @@
     send_index,
 ):
     nodes = diag_margin.shape[1]
-    par = jnp.stack([lax.axis_index("grp") % 2, lax.axis_index("sub") % 2]).astype(jnp.int32)
     own = ((16, LANES), F32)
     block = [((4, 8, LANES), F32)] * 4
     flat = lambda x: x.reshape(1, -1)
     tile = lambda x: x.reshape(-1, LANES)
 
-    partial, *ghost = call(edge_sums, [own] + block, par, flat(residual), tangent, flat(edge_tail), flat(edge_head))
+    partial, *ghost = call(edge_sums, [own] + block, flat(residual), tangent, flat(edge_tail), flat(edge_head))
     idx16, coef16, dinv, send16 = call(
         prepare,
         [((16, nodes), jnp.int32), ((4, 16, nodes), F32), own, ((16, LANES), jnp.int32)],
-        par, stencil_index, stencil_coef, diag_margin, send_index,
+        stencil_index, stencil_coef, diag_margin, send_index,
     )
     ghost = exchange(ghost)
-    rn, solved, *blocks = call(first_solve, [own, own] + block, par, partial, *ghost, send16, dinv)
+    rn, solved, *blocks = call(first_solve, [own, own] + block, partial, *ghost, send16, dinv)
     for _ in range(SWEEPS - 1):
         blocks = exchange(blocks)
         solved, *blocks = call(
-            sweep, [own] + block, par, solved, *blocks, idx16, coef16, rn, dinv, send16
+            sweep, [own] + block, solved, *blocks, idx16, coef16, rn, dinv, send16
         )
     blocks = exchange(blocks)
     (out,) = call(
         edge_values,
         [((residual.shape[0] // LANES, LANES), F32)],
-        par, solved, *blocks, tile(residual), tile(edge_scale), tangent, tile(edge_tail), tile(edge_head),
+        solved, *blocks, tile(residual), tile(edge_scale), tangent, tile(edge_tail), tile(edge_head),
     )
     return out.reshape(-1)
 

time: 110 us -> 99.8 us (0.907)
  Pallas kernels: 20.6 us -> 10.5 us
    pallas_call x7, Pallas kernels: 20.6 us -> 10.5 us  [call(): pl.pallas_call(kernel, out_shape=[jax.ShapeDtypeStruct(shape, dtype) for...]
    ppermute x5, waiting for transfers between devices: 3.55 us -> 5.16 us  [exchange(): es = lax.ppermute(es, 'sub', pairs(sub, 0))]
    unnamed x43 -> x27, local copies, waits for them, and re-layouts: 3.63 us -> 2.98 us
  transfers between devices with their start and end apart: 20 -> 20, of which waited for: 5 -> 5; matrix products, arithmetic and copies ran while one was open for 1% -> 0% of each run, Pallas kernels for 1% -> 0%
where the time goes in v2:
time: 99.8 us; the launch traced here: 98.9 us
  starting transfers between devices  79.8 us (80%)
  Pallas kernels  10.5 us (11%)
  waiting for transfers between devices  5.2 us (5%)
  local copies, waits for them, and re-layouts  2.98 us (3%)
    ppermute x5, starting transfers between devices, exchange(): og = lax.ppermute(og, 'grp', pairs(grp, 1))  36.4 us
    ppermute x5, starting transfers between devices, exchange(): os = lax.ppermute(os, 'sub', pairs(sub, 1))  22.8 us
    ppermute x5, starting transfers between devices, exchange(): eg = lax.ppermute(eg, 'grp', pairs(grp, 0))  10.5 us
    pallas_call x7, Pallas kernels, call(): pl.pallas_call(kernel, out_shape=[jax.ShapeDtypeStruct(shape, dtype) for...  10.5 us
    ppermute x5, starting transfers between devices, exchange(): es = lax.ppermute(es, 'sub', pairs(sub, 0))  10 us
    ppermute x5, waiting for transfers between devices, exchange(): es = lax.ppermute(es, 'sub', pairs(sub, 0))  5.16 us
    unnamed x27, local copies, waits for them, and re-layouts  2.98 us
  transfers between devices with their start and end apart: 20, of which 5 were waited for; matrix products, arithmetic and copies ran while one was open for 0% of the time, Pallas kernels for 0%

profile of v2, /device:TPU:1, one launch (start us, length us, event | category | flops | bytes accessed | tf_op | source)
XLA Modules:
  0.0 98.9 jit_solution(5649671116450202415)
XLA Ops:
  0.0 0.8 copy-done
  0.8 0.7 copy-done.2
  1.5 0.7 copy-done.4
  2.2 0.7 copy-done.6
  2.9 1.2 %shard_map.91 = (f32[16,128]{1,0:T(8,128)S(1)}, f32[4,8,128]{2,1,0:T(8,128)S(1)}, f32[4,8,128]{2,1,0:T(8,128)S(1)}, f32[4,8,128]{2,1,0:T(8,128)S(1)}, f32[4,8,128]{2,1,0:T(8,128)S(1)}) custom-call(f32[1,3072]{1,0:T(1,128)S(1)} %bitcast.8, f32[3,3072]{1,0:T(4,128)S(1)} %copy-done, s32[1,3072]{1,0:T(1,128)S(1)} %bitcast.10, s32[1,3072]{1,0:T(1,128)S(1)} %bitcast.12), custom_call_target="tpu_custom_call" | custom-call | tf_op jit(solution)/shard_map/pallas_call | solution.py:16
  4.1 18.3 %collective-permute-start = (f32[4,8,128]{2,1,0:T(8,128)S(1)}, f32[4,8,128]{2,1,0:T(8,128)S(1)}, u32[]{:S(2)}, u32[]{:S(2)}) collective-permute-start(f32[4,8,128]{2,1,0:T(8,128)S(1)} %get-tuple-element.36), channel_id=1, source_target_pairs={{8,16},{16,8},{24,32},{32,24},{40,48},{48,40},{56,64},{64,56},{72,... | collective-permute-start | bytes 49160 | tf_op jit(solution)/shard_map/ppermute | solution.py:235
  22.4 1.9 %collective-permute-start.1 = (f32[4,8,128]{2,1,0:T(8,128)S(1)}, f32[4,8,128]{2,1,0:T(8,128)S(1)}, u32[]{:S(2)}, u32[]{:S(2)}) collective-permute-start(f32[4,8,128]{2,1,0:T(8,128)S(1)} %get-tuple-element.37), channel_id=1, source_target_pairs={{0,8},{8,0},{16,24},{24,16},{32,40},{40,32},{48,56},{56,48},{64,72... | collective-permute-start | bytes 49160 | tf_op jit(solution)/shard_map/ppermute | solution.py:236
  24.4 5.1 %collective-permute-start.2 = (f32[4,8,128]{2,1,0:T(8,128)S(1)}, f32[4,8,128]{2,1,0:T(8,128)S(1)}, u32[]{:S(2)}, u32[]{:S(2)}) collective-permute-start(f32[4,8,128]{2,1,0:T(8,128)S(1)} %get-tuple-element.38), channel_id=1, source_target_pairs={{1,2},{2,1},{3,4},{4,3},{5,6},{6,5},{7,0},{0,7},{9,10},{10,9},{11,... | collective-permute-start | bytes 49160 | tf_op jit(solution)/shard_map/ppermute | solution.py:237
  29.4 0.0 copy-start.8
  29.4 0.0 copy-start.10
  29.5 0.0 copy-start.11
  29.5 2.4 %collective-permute-start.3 = (f32[4,8,128]{2,1,0:T(8,128)S(1)}, f32[4,8,128]{2,1,0:T(8,128)S(1)}, u32[]{:S(2)}, u32[]{:S(2)}) collective-permute-start(f32[4,8,128]{2,1,0:T(8,128)S(1)} %get-tuple-element.39), channel_id=1, source_target_pairs={{0,1},{1,0},{2,3},{3,2},{4,5},{5,4},{6,7},{7,6},{8,9},{9,8},{10,11... | collective-permute-start | bytes 49160 | tf_op jit(solution)/shard_map/ppermute | solution.py:238
  31.9 0.1 shard_map.92
  32.0 0.0 collective-permute-done.1.eg
  32.0 0.0 collective-permute-done.2.os
  32.0 0.7 collective-permute-done.3.es
  32.7 0.4 shard_map.93
  33.1 2.7 %collective-permute-start.4 = (f32[4,8,128]{2,1,0:T(8,128)S(1)}, f32[4,8,128]{2,1,0:T(8,128)S(1)}, u32[]{:S(2)}, u32[]{:S(2)}) collective-permute-start(f32[4,8,128]{2,1,0:T(8,128)S(1)} %get-tuple-element.43), channel_id=1, source_target_pairs={{8,16},{16,8},{24,32},{32,24},{40,48},{48,40},{56,64},{64,56},{72,... | collective-permute-start | bytes 49160 | tf_op jit(solution)/shard_map/ppermute | solution.py:235
  35.8 2.8 %collective-permute-start.5 = (f32[4,8,128]{2,1,0:T(8,128)S(1)}, f32[4,8,128]{2,1,0:T(8,128)S(1)}, u32[]{:S(2)}, u32[]{:S(2)}) collective-permute-start(f32[4,8,128]{2,1,0:T(8,128)S(1)} %get-tuple-element.44), channel_id=1, source_target_pairs={{0,8},{8,0},{16,24},{24,16},{32,40},{40,32},{48,56},{56,48},{64,72... | collective-permute-start | bytes 49160 | tf_op jit(solution)/shard_map/ppermute | solution.py:236
  38.7 4.9 %collective-permute-start.6 = (f32[4,8,128]{2,1,0:T(8,128)S(1)}, f32[4,8,128]{2,1,0:T(8,128)S(1)}, u32[]{:S(2)}, u32[]{:S(2)}) collective-permute-start(f32[4,8,128]{2,1,0:T(8,128)S(1)} %get-tuple-element.45), channel_id=1, source_target_pairs={{1,2},{2,1},{3,4},{4,3},{5,6},{6,5},{7,0},{0,7},{9,10},{10,9},{11,... | collective-permute-start | bytes 49160 | tf_op jit(solution)/shard_map/ppermute | solution.py:237
  43.6 1.9 %collective-permute-start.7 = (f32[4,8,128]{2,1,0:T(8,128)S(1)}, f32[4,8,128]{2,1,0:T(8,128)S(1)}, u32[]{:S(2)}, u32[]{:S(2)}) collective-permute-start(f32[4,8,128]{2,1,0:T(8,128)S(1)} %get-tuple-element.46), channel_id=1, source_target_pairs={{0,1},{1,0},{2,3},{3,2},{4,5},{5,4},{6,7},{7,6},{8,9},{9,8},{10,11... | collective-permute-start | bytes 49160 | tf_op jit(solution)/shard_map/ppermute | solution.py:238
  45.5 0.0 collective-permute-done.4.og
  45.5 0.0 collective-permute-done.5.eg
  45.5 1.1 %collective-permute-done.7.es = f32[4,8,128]{2,1,0:T(8,128)S(1)} collective-permute-done((f32[4,8,128]{2,1,0:T(8,128)S(1)}, f32[4,8,128]{2,1,0:T(8,128)S(1)}, u32[]{:S(2)}, u32[]{:S(2)}) %collective-permute-start.7) | collective-permute-done | bytes 16416 | tf_op jit(solution)/shard_map/ppermute | solution.py:238
  46.6 2.4 %shard_map.94 = (f32[16,128]{1,0:T(8,128)S(1)}, f32[4,8,128]{2,1,0:T(8,128)S(1)}, f32[4,8,128]{2,1,0:T(8,128)S(1)}, f32[4,8,128]{2,1,0:T(8,128)S(1)}, f32[4,8,128]{2,1,0:T(8,128)S(1)}) custom-call(f32[16,128]{1,0:T(8,128)S(1)} %get-tuple-element.42.y_ref, f32[4,8,128]{2,1,0:T(8,128)S(1)} %collective-permute-done.4.og, ...), custom_call_target="tpu_custom_call" | custom-call | tf_op jit(solution)/shard_map/pallas_call | solution.py:16
  49.1 5.9 %collective-permute-start.8 = (f32[4,8,128]{2,1,0:T(8,128)S(1)}, f32[4,8,128]{2,1,0:T(8,128)S(1)}, u32[]{:S(2)}, u32[]{:S(2)}) collective-permute-start(f32[4,8,128]{2,1,0:T(8,128)S(1)} %get-tuple-element.51), channel_id=1, source_target_pairs={{8,16},{16,8},{24,32},{32,24},{40,48},{48,40},{56,64},{64,56},{72,... | collective-permute-start | bytes 49160 | tf_op jit(solution)/shard_map/ppermute | solution.py:235
  54.9 1.9 %collective-permute-start.9 = (f32[4,8,128]{2,1,0:T(8,128)S(1)}, f32[4,8,128]{2,1,0:T(8,128)S(1)}, u32[]{:S(2)}, u32[]{:S(2)}) collective-permute-start(f32[4,8,128]{2,1,0:T(8,128)S(1)} %get-tuple-element.52), channel_id=1, source_target_pairs={{0,8},{8,0},{16,24},{24,16},{32,40},{40,32},{48,56},{56,48},{64,72... | collective-permute-start | bytes 49160 | tf_op jit(solution)/shard_map/ppermute | solution.py:236
  56.9 4.2 %collective-permute-start.10 = (f32[4,8,128]{2,1,0:T(8,128)S(1)}, f32[4,8,128]{2,1,0:T(8,128)S(1)}, u32[]{:S(2)}, u32[]{:S(2)}) collective-permute-start(f32[4,8,128]{2,1,0:T(8,128)S(1)} %get-tuple-element.53), channel_id=1, source_target_pairs={{1,2},{2,1},{3,4},{4,3},{5,6},{6,5},{7,0},{0,7},{9,10},{10,9},{11,... | collective-permute-start | bytes 49160 | tf_op jit(solution)/shard_map/ppermute | solution.py:237
  61.1 1.9 %collective-permute-start.11 = (f32[4,8,128]{2,1,0:T(8,128)S(1)}, f32[4,8,128]{2,1,0:T(8,128)S(1)}, u32[]{:S(2)}, u32[]{:S(2)}) collective-permute-start(f32[4,8,128]{2,1,0:T(8,128)S(1)} %get-tuple-element.54), channel_id=1, source_target_pairs={{0,1},{1,0},{2,3},{3,2},{4,5},{5,4},{6,7},{7,6},{8,9},{9,8},{10,11... | collective-permute-start | bytes 49160 | tf_op jit(solution)/shard_map/ppermute | solution.py:238
  63.0 0.0 collective-permute-done.9.eg
  63.0 0.0 collective-permute-done.10.os
  63.0 1.1 %collective-permute-done.11.es = f32[4,8,128]{2,1,0:T(8,128)S(1)} collective-permute-done((f32[4,8,128]{2,1,0:T(8,128)S(1)}, f32[4,8,128]{2,1,0:T(8,128)S(1)}, u32[]{:S(2)}, u32[]{:S(2)}) %collective-permute-start.11) | collective-permute-done | bytes 16416 | tf_op jit(solution)/shard_map/ppermute | solution.py:238
  64.1 2.4 %shard_map.95 = (f32[16,128]{1,0:T(8,128)S(1)}, f32[4,8,128]{2,1,0:T(8,128)S(1)}, f32[4,8,128]{2,1,0:T(8,128)S(1)}, f32[4,8,128]{2,1,0:T(8,128)S(1)}, f32[4,8,128]{2,1,0:T(8,128)S(1)}) custom-call(f32[16,128]{1,0:T(8,128)S(1)} %get-tuple-element.50.y_ref, f32[4,8,128]{2,1,0:T(8,128)S(1)} %collective-permute-done.8.og, ...), custom_call_target="tpu_custom_call" | custom-call | tf_op jit(solution)/shard_map/pallas_call | solution.py:16
  66.6 3.6 %collective-permute-start.12 = (f32[4,8,128]{2,1,0:T(8,128)S(1)}, f32[4,8,128]{2,1,0:T(8,128)S(1)}, u32[]{:S(2)}, u32[]{:S(2)}) collective-permute-start(f32[4,8,128]{2,1,0:T(8,128)S(1)} %get-tuple-element.56), channel_id=1, source_target_pairs={{8,16},{16,8},{24,32},{32,24},{40,48},{48,40},{56,64},{64,56},{72,... | collective-permute-start | bytes 49160 | tf_op jit(solution)/shard_map/ppermute | solution.py:235
  70.2 1.9 %collective-permute-start.13 = (f32[4,8,128]{2,1,0:T(8,128)S(1)}, f32[4,8,128]{2,1,0:T(8,128)S(1)}, u32[]{:S(2)}, u32[]{:S(2)}) collective-permute-start(f32[4,8,128]{2,1,0:T(8,128)S(1)} %get-tuple-element.57), channel_id=1, source_target_pairs={{0,8},{8,0},{16,24},{24,16},{32,40},{40,32},{48,56},{56,48},{64,72... | collective-permute-start | bytes 49160 | tf_op jit(solution)/shard_map/ppermute | solution.py:236
  72.1 4.4 %collective-permute-start.14 = (f32[4,8,128]{2,1,0:T(8,128)S(1)}, f32[4,8,128]{2,1,0:T(8,128)S(1)}, u32[]{:S(2)}, u32[]{:S(2)}) collective-permute-start(f32[4,8,128]{2,1,0:T(8,128)S(1)} %get-tuple-element.58), channel_id=1, source_target_pairs={{1,2},{2,1},{3,4},{4,3},{5,6},{6,5},{7,0},{0,7},{9,10},{10,9},{11,... | collective-permute-start | bytes 49160 | tf_op jit(solution)/shard_map/ppermute | solution.py:237
  76.5 1.9 %collective-permute-start.15 = (f32[4,8,128]{2,1,0:T(8,128)S(1)}, f32[4,8,128]{2,1,0:T(8,128)S(1)}, u32[]{:S(2)}, u32[]{:S(2)}) collective-permute-start(f32[4,8,128]{2,1,0:T(8,128)S(1)} %get-tuple-element.59), channel_id=1, source_target_pairs={{0,1},{1,0},{2,3},{3,2},{4,5},{5,4},{6,7},{7,6},{8,9},{9,8},{10,11... | collective-permute-start | bytes 49160 | tf_op jit(solution)/shard_map/ppermute | solution.py:238
  78.4 0.0 collective-permute-done.12.og
  78.4 0.0 collective-permute-done.13.eg
  78.5 1.1 %collective-permute-done.15.es = f32[4,8,128]{2,1,0:T(8,128)S(1)} collective-permute-done((f32[4,8,128]{2,1,0:T(8,128)S(1)}, f32[4,8,128]{2,1,0:T(8,128)S(1)}, u32[]{:S(2)}, u32[]{:S(2)}) %collective-permute-start.15) | collective-permute-done | bytes 16416 | tf_op jit(solution)/shard_map/ppermute | solution.py:238
  79.6 2.4 %shard_map.96 = (f32[16,128]{1,0:T(8,128)S(1)}, f32[4,8,128]{2,1,0:T(8,128)S(1)}, f32[4,8,128]{2,1,0:T(8,128)S(1)}, f32[4,8,128]{2,1,0:T(8,128)S(1)}, f32[4,8,128]{2,1,0:T(8,128)S(1)}) custom-call(f32[16,128]{1,0:T(8,128)S(1)} %get-tuple-element.55.y_ref, f32[4,8,128]{2,1,0:T(8,128)S(1)} %collective-permute-done.12.og, ...), custom_call_target="tpu_custom_call" | custom-call | tf_op jit(solution)/shard_map/pallas_call | solution.py:16
  82.0 0.0 copy-start.3
  82.0 5.9 %collective-permute-start.16 = (f32[4,8,128]{2,1,0:T(8,128)S(1)}, f32[4,8,128]{2,1,0:T(8,128)S(1)}, u32[]{:S(2)}, u32[]{:S(2)}) collective-permute-start(f32[4,8,128]{2,1,0:T(8,128)S(1)} %get-tuple-element.61), channel_id=1, source_target_pairs={{8,16},{16,8},{24,32},{32,24},{40,48},{48,40},{56,64},{64,56},{72,... | collective-permute-start | bytes 49160 | tf_op jit(solution)/shard_map/ppermute | solution.py:235
  87.9 1.9 %collective-permute-start.17 = (f32[4,8,128]{2,1,0:T(8,128)S(1)}, f32[4,8,128]{2,1,0:T(8,128)S(1)}, u32[]{:S(2)}, u32[]{:S(2)}) collective-permute-start(f32[4,8,128]{2,1,0:T(8,128)S(1)} %get-tuple-element.62), channel_id=1, source_target_pairs={{0,8},{8,0},{16,24},{24,16},{32,40},{40,32},{48,56},{56,48},{64,72... | collective-permute-start | bytes 49160 | tf_op jit(solution)/shard_map/ppermute | solution.py:236
  89.8 4.4 %collective-permute-start.18 = (f32[4,8,128]{2,1,0:T(8,128)S(1)}, f32[4,8,128]{2,1,0:T(8,128)S(1)}, u32[]{:S(2)}, u32[]{:S(2)}) collective-permute-start(f32[4,8,128]{2,1,0:T(8,128)S(1)} %get-tuple-element.63), channel_id=1, source_target_pairs={{1,2},{2,1},{3,4},{4,3},{5,6},{6,5},{7,0},{0,7},{9,10},{10,9},{11,... | collective-permute-start | bytes 49160 | tf_op jit(solution)/shard_map/ppermute | solution.py:237
  94.2 1.9 %collective-permute-start.19 = (f32[4,8,128]{2,1,0:T(8,128)S(1)}, f32[4,8,128]{2,1,0:T(8,128)S(1)}, u32[]{:S(2)}, u32[]{:S(2)}) collective-permute-start(f32[4,8,128]{2,1,0:T(8,128)S(1)} %get-tuple-element.64), channel_id=1, source_target_pairs={{0,1},{1,0},{2,3},{3,2},{4,5},{5,4},{6,7},{7,6},{8,9},{9,8},{10,11... | collective-permute-start | bytes 49160 | tf_op jit(solution)/shard_map/ppermute | solution.py:238
  96.2 1.1 %collective-permute-done.19.es = f32[4,8,128]{2,1,0:T(8,128)S(1)} collective-permute-done((f32[4,8,128]{2,1,0:T(8,128)S(1)}, f32[4,8,128]{2,1,0:T(8,128)S(1)}, u32[]{:S(2)}, u32[]{:S(2)}) %collective-permute-start.19) | collective-permute-done | bytes 16416 | tf_op jit(solution)/shard_map/ppermute | solution.py:238
  97.3 1.6 %shard_map.97 = f32[24,128]{1,0:T(8,128)} custom-call(f32[16,128]{1,0:T(8,128)S(1)} %get-tuple-element.60.y_ref, f32[4,8,128]{2,1,0:T(8,128)S(1)} %collective-permute-done.16.og, f32[4,8,128]{2,1,0:T(8,128)S(1)} %collective-permute-done.17.eg, f32[4,8,128]{2,1,0:T(8,128)S(1)} %collective-permute-done.18.os, f32[4,8,128]{2,1,0:T(8,128)S(1)} %collective-permute-done.19.es, ...), custom_call_target="tpu_custom_call" | custom-call | tf_op jit(solution)/shard_map/pallas_call | solution.py:16
  (26 shorter events, 0.1 us)
Async XLA Ops:
  0.0 0.8 copy-start
  0.8 0.7 copy-start.2
  1.5 0.7 copy-start.4
  2.2 0.7 copy-start.6
  2.9 28.9 %copy-start.12 = (bf16[4,14,512]{2,0,1:T(4,128)(2,1)S(1)}, bf16[4,14,512]{2,0,1:T(4,128)(2,1)}, u32[]{:S(2)}) copy-start(bf16[4,14,512]{2,0,1:T(4,128)(2,1)} %param.15) | copy-start | bytes 172036
  4.1 27.9 %collective-permute-start = (f32[4,8,128]{2,1,0:T(8,128)S(1)}, f32[4,8,128]{2,1,0:T(8,128)S(1)}, u32[]{:S(2)}, u32[]{:S(2)}) collective-permute-start(f32[4,8,128]{2,1,0:T(8,128)S(1)} %get-tuple-element.36), channel_id=1, source_target_pairs={{8,16},{16,8},{24,32},{32,24},{40,48},{48,40},{56,64},{64,56},{72,... | collective-permute-start | bytes 49160 | tf_op jit(solution)/shard_map/ppermute | solution.py:235
  22.4 9.5 %collective-permute-start.1 = (f32[4,8,128]{2,1,0:T(8,128)S(1)}, f32[4,8,128]{2,1,0:T(8,128)S(1)}, u32[]{:S(2)}, u32[]{:S(2)}) collective-permute-start(f32[4,8,128]{2,1,0:T(8,128)S(1)} %get-tuple-element.37), channel_id=1, source_target_pairs={{0,8},{8,0},{16,24},{24,16},{32,40},{40,32},{48,56},{56,48},{64,72... | collective-permute-start | bytes 49160 | tf_op jit(solution)/shard_map/ppermute | solution.py:236
  24.4 7.6 %collective-permute-start.2 = (f32[4,8,128]{2,1,0:T(8,128)S(1)}, f32[4,8,128]{2,1,0:T(8,128)S(1)}, u32[]{:S(2)}, u32[]{:S(2)}) collective-permute-start(f32[4,8,128]{2,1,0:T(8,128)S(1)} %get-tuple-element.38), channel_id=1, source_target_pairs={{1,2},{2,1},{3,4},{4,3},{5,6},{6,5},{7,0},{0,7},{9,10},{10,9},{11,... | collective-permute-start | bytes 49160 | tf_op jit(solution)/shard_map/ppermute | solution.py:237
  29.4 2.4 %copy-start.8 = (s32[14,512]{1,0:T(8,128)S(1)}, s32[14,512]{1,0:T(8,128)}, u32[]{:S(2)}) copy-start(s32[14,512]{1,0:T(8,128)} %idx_ref.1) | copy-start | bytes 86020
  29.4 2.4 %copy-start.10 = (f32[4,512]{1,0:T(4,128)S(1)}, f32[4,512]{1,0:T(4,128)}, u32[]{:S(2)}) copy-start(f32[4,512]{1,0:T(4,128)} %margin_ref.1) | copy-start | bytes 24580
  29.5 2.4 %copy-start.11 = (s32[2,2,512]{2,1,0:T(2,128)S(1)}, s32[2,2,512]{2,1,0:T(2,128)}, u32[]{:S(2)}) copy-start(s32[2,2,512]{2,1,0:T(2,128)} %send_ref.1) | copy-start | bytes 24580
  29.5 3.2 %collective-permute-start.3 = (f32[4,8,128]{2,1,0:T(8,128)S(1)}, f32[4,8,128]{2,1,0:T(8,128)S(1)}, u32[]{:S(2)}, u32[]{:S(2)}) collective-permute-start(f32[4,8,128]{2,1,0:T(8,128)S(1)} %get-tuple-element.39), channel_id=1, source_target_pairs={{0,1},{1,0},{2,3},{3,2},{4,5},{5,4},{6,7},{7,6},{8,9},{9,8},{10,11... | collective-permute-start | bytes 49160 | tf_op jit(solution)/shard_map/ppermute | solution.py:238
  33.1 12.4 %collective-permute-start.4 = (f32[4,8,128]{2,1,0:T(8,128)S(1)}, f32[4,8,128]{2,1,0:T(8,128)S(1)}, u32[]{:S(2)}, u32[]{:S(2)}) collective-permute-start(f32[4,8,128]{2,1,0:T(8,128)S(1)} %get-tuple-element.43), channel_id=1, source_target_pairs={{8,16},{16,8},{24,32},{32,24},{40,48},{48,40},{56,64},{64,56},{72,... | collective-permute-start | bytes 49160 | tf_op jit(solution)/shard_map/ppermute | solution.py:235
  35.8 9.7 %collective-permute-start.5 = (f32[4,8,128]{2,1,0:T(8,128)S(1)}, f32[4,8,128]{2,1,0:T(8,128)S(1)}, u32[]{:S(2)}, u32[]{:S(2)}) collective-permute-start(f32[4,8,128]{2,1,0:T(8,128)S(1)} %get-tuple-element.44), channel_id=1, source_target_pairs={{0,8},{8,0},{16,24},{24,16},{32,40},{40,32},{48,56},{56,48},{64,72... | collective-permute-start | bytes 49160 | tf_op jit(solution)/shard_map/ppermute | solution.py:236
  38.7 6.8 %collective-permute-start.6 = (f32[4,8,128]{2,1,0:T(8,128)S(1)}, f32[4,8,128]{2,1,0:T(8,128)S(1)}, u32[]{:S(2)}, u32[]{:S(2)}) collective-permute-start(f32[4,8,128]{2,1,0:T(8,128)S(1)} %get-tuple-element.45), channel_id=1, source_target_pairs={{1,2},{2,1},{3,4},{4,3},{5,6},{6,5},{7,0},{0,7},{9,10},{10,9},{11,... | collective-permute-start | bytes 49160 | tf_op jit(solution)/shard_map/ppermute | solution.py:237
  43.6 3.1 %collective-permute-start.7 = (f32[4,8,128]{2,1,0:T(8,128)S(1)}, f32[4,8,128]{2,1,0:T(8,128)S(1)}, u32[]{:S(2)}, u32[]{:S(2)}) collective-permute-start(f32[4,8,128]{2,1,0:T(8,128)S(1)} %get-tuple-element.46), channel_id=1, source_target_pairs={{0,1},{1,0},{2,3},{3,2},{4,5},{5,4},{6,7},{7,6},{8,9},{9,8},{10,11... | collective-permute-start | bytes 49160 | tf_op jit(solution)/shard_map/ppermute | solution.py:238
  49.1 13.9 %collective-permute-start.8 = (f32[4,8,128]{2,1,0:T(8,128)S(1)}, f32[4,8,128]{2,1,0:T(8,128)S(1)}, u32[]{:S(2)}, u32[]{:S(2)}) collective-permute-start(f32[4,8,128]{2,1,0:T(8,128)S(1)} %get-tuple-element.51), channel_id=1, source_target_pairs={{8,16},{16,8},{24,32},{32,24},{40,48},{48,40},{56,64},{64,56},{72,... | collective-permute-start | bytes 49160 | tf_op jit(solution)/shard_map/ppermute | solution.py:235
  54.9 8.1 %collective-permute-start.9 = (f32[4,8,128]{2,1,0:T(8,128)S(1)}, f32[4,8,128]{2,1,0:T(8,128)S(1)}, u32[]{:S(2)}, u32[]{:S(2)}) collective-permute-start(f32[4,8,128]{2,1,0:T(8,128)S(1)} %get-tuple-element.52), channel_id=1, source_target_pairs={{0,8},{8,0},{16,24},{24,16},{32,40},{40,32},{48,56},{56,48},{64,72... | collective-permute-start | bytes 49160 | tf_op jit(solution)/shard_map/ppermute | solution.py:236
  56.9 6.2 %collective-permute-start.10 = (f32[4,8,128]{2,1,0:T(8,128)S(1)}, f32[4,8,128]{2,1,0:T(8,128)S(1)}, u32[]{:S(2)}, u32[]{:S(2)}) collective-permute-start(f32[4,8,128]{2,1,0:T(8,128)S(1)} %get-tuple-element.53), channel_id=1, source_target_pairs={{1,2},{2,1},{3,4},{4,3},{5,6},{6,5},{7,0},{0,7},{9,10},{10,9},{11,... | collective-permute-start | bytes 49160 | tf_op jit(solution)/shard_map/ppermute | solution.py:237
  61.1 3.1 %collective-permute-start.11 = (f32[4,8,128]{2,1,0:T(8,128)S(1)}, f32[4,8,128]{2,1,0:T(8,128)S(1)}, u32[]{:S(2)}, u32[]{:S(2)}) collective-permute-start(f32[4,8,128]{2,1,0:T(8,128)S(1)} %get-tuple-element.54), channel_id=1, source_target_pairs={{0,1},{1,0},{2,3},{3,2},{4,5},{5,4},{6,7},{7,6},{8,9},{9,8},{10,11... | collective-permute-start | bytes 49160 | tf_op jit(solution)/shard_map/ppermute | solution.py:238
  66.6 11.9 %collective-permute-start.12 = (f32[4,8,128]{2,1,0:T(8,128)S(1)}, f32[4,8,128]{2,1,0:T(8,128)S(1)}, u32[]{:S(2)}, u32[]{:S(2)}) collective-permute-start(f32[4,8,128]{2,1,0:T(8,128)S(1)} %get-tuple-element.56), channel_id=1, source_target_pairs={{8,16},{16,8},{24,32},{32,24},{40,48},{48,40},{56,64},{64,56},{72,... | collective-permute-start | bytes 49160 | tf_op jit(solution)/shard_map/ppermute | solution.py:235
  70.2 8.2 %collective-permute-start.13 = (f32[4,8,128]{2,1,0:T(8,128)S(1)}, f32[4,8,128]{2,1,0:T(8,128)S(1)}, u32[]{:S(2)}, u32[]{:S(2)}) collective-permute-start(f32[4,8,128]{2,1,0:T(8,128)S(1)} %get-tuple-element.57), channel_id=1, source_target_pairs={{0,8},{8,0},{16,24},{24,16},{32,40},{40,32},{48,56},{56,48},{64,72... | collective-permute-start | bytes 49160 | tf_op jit(solution)/shard_map/ppermute | solution.py:236
  72.1 6.3 %collective-permute-start.14 = (f32[4,8,128]{2,1,0:T(8,128)S(1)}, f32[4,8,128]{2,1,0:T(8,128)S(1)}, u32[]{:S(2)}, u32[]{:S(2)}) collective-permute-start(f32[4,8,128]{2,1,0:T(8,128)S(1)} %get-tuple-element.58), channel_id=1, source_target_pairs={{1,2},{2,1},{3,4},{4,3},{5,6},{6,5},{7,0},{0,7},{9,10},{10,9},{11,... | collective-permute-start | bytes 49160 | tf_op jit(solution)/shard_map/ppermute | solution.py:237
  76.5 3.1 %collective-permute-start.15 = (f32[4,8,128]{2,1,0:T(8,128)S(1)}, f32[4,8,128]{2,1,0:T(8,128)S(1)}, u32[]{:S(2)}, u32[]{:S(2)}) collective-permute-start(f32[4,8,128]{2,1,0:T(8,128)S(1)} %get-tuple-element.59), channel_id=1, source_target_pairs={{0,1},{1,0},{2,3},{3,2},{4,5},{5,4},{6,7},{7,6},{8,9},{9,8},{10,11... | collective-permute-start | bytes 49160 | tf_op jit(solution)/shard_map/ppermute | solution.py:238
  79.6 17.7 %copy-start.1 = (f32[3,3072]{1,0:T(4,128)S(1)}, f32[3,3072]{1,0:T(4,128)}, u32[]{:S(2)}) copy-start(f32[3,3072]{1,0:T(4,128)} %tan_ref.3) | copy-start | bytes 110596
  79.6 17.7 %copy-start.5 = (s32[3072]{0:T(1024)S(1)}, s32[3072]{0:T(1024)}, u32[]{:S(2)}) copy-start(s32[3072]{0:T(1024)} %param.12) | copy-start | bytes 36868
  79.6 17.7 %copy-start.7 = (s32[3072]{0:T(1024)S(1)}, s32[3072]{0:T(1024)}, u32[]{:S(2)}) copy-start(s32[3072]{0:T(1024)} %param.13) | copy-start | bytes 36868
  79.6 17.7 %copy-start.9 = (f32[3072]{0:T(1024)S(1)}, f32[3072]{0:T(1024)}, u32[]{:S(2)}) copy-start(f32[3072]{0:T(1024)} %param.10) | copy-start | bytes 36868
  82.0 15.3 %copy-start.3 = (f32[3072]{0:T(1024)S(1)}, f32[3072]{0:T(1024)}, u32[]{:S(2)}) copy-start(f32[3072]{0:T(1024)} %param.9) | copy-start | bytes 36868
  82.0 14.1 %collective-permute-start.16 = (f32[4,8,128]{2,1,0:T(8,128)S(1)}, f32[4,8,128]{2,1,0:T(8,128)S(1)}, u32[]{:S(2)}, u32[]{:S(2)}) collective-permute-start(f32[4,8,128]{2,1,0:T(8,128)S(1)} %get-tuple-element.61), channel_id=1, source_target_pairs={{8,16},{16,8},{24,32},{32,24},{40,48},{48,40},{56,64},{64,56},{72,... | collective-permute-start | bytes 49160 | tf_op jit(solution)/shard_map/ppermute | solution.py:235
  87.9 8.2 %collective-permute-start.17 = (f32[4,8,128]{2,1,0:T(8,128)S(1)}, f32[4,8,128]{2,1,0:T(8,128)S(1)}, u32[]{:S(2)}, u32[]{:S(2)}) collective-permute-start(f32[4,8,128]{2,1,0:T(8,128)S(1)} %get-tuple-element.62), channel_id=1, source_target_pairs={{0,8},{8,0},{16,24},{24,16},{32,40},{40,32},{48,56},{56,48},{64,72... | collective-permute-start | bytes 49160 | tf_op jit(solution)/shard_map/ppermute | solution.py:236
  89.8 6.3 %collective-permute-start.18 = (f32[4,8,128]{2,1,0:T(8,128)S(1)}, f32[4,8,128]{2,1,0:T(8,128)S(1)}, u32[]{:S(2)}, u32[]{:S(2)}) collective-permute-start(f32[4,8,128]{2,1,0:T(8,128)S(1)} %get-tuple-element.63), channel_id=1, source_target_pairs={{1,2},{2,1},{3,4},{4,3},{5,6},{6,5},{7,0},{0,7},{9,10},{10,9},{11,... | collective-permute-start | bytes 49160 | tf_op jit(solution)/shard_map/ppermute | solution.py:237
  94.2 3.1 %collective-permute-start.19 = (f32[4,8,128]{2,1,0:T(8,128)S(1)}, f32[4,8,128]{2,1,0:T(8,128)S(1)}, u32[]{:S(2)}, u32[]{:S(2)}) collective-permute-start(f32[4,8,128]{2,1,0:T(8,128)S(1)} %get-tuple-element.64), channel_id=1, source_target_pairs={{0,1},{1,0},{2,3},{3,2},{4,5},{5,4},{6,7},{7,6},{8,9},{9,8},{10,11... | collective-permute-start | bytes 49160 | tf_op jit(solution)/shard_map/ppermute | solution.py:238

commit v3 on v2

--- a/solution.py
+++ b/solution.py
@@ -5,19 +5,22 @@
 from jax.experimental.pallas import tpu as pltpu
 from jax.sharding import PartitionSpec as P
 
+
 SWEEPS = 4
 LANES = 128
 F32 = jnp.float32
 BF16 = jnp.bfloat16
 VMEM = pl.BlockSpec(memory_space=pltpu.VMEM)
-
-
-def call(kernel, outs, *args):
+HBM = pl.BlockSpec(memory_space=pltpu.HBM)
+
+
+def call(kernel, outs, *args, space=VMEM, scratch=()):
     return pl.pallas_call(
         kernel,
         out_shape=[jax.ShapeDtypeStruct(shape, dtype) for shape, dtype in outs],
-        in_specs=[VMEM] * len(args),
+        in_specs=[space] * len(args),
         out_specs=[VMEM] * len(outs),
+        scratch_shapes=list(scratch),
         compiler_params=pltpu.CompilerParams(vmem_limit_bytes=16 << 20),
     )(*args)
 
@@ -73,7 +76,13 @@
     return low, high
 
 
-def edge_sums(res_ref, tan_ref, tail_ref, head_ref, own_ref, og_ref, eg_ref, os_ref, es_ref):
+def edge_sums(res_hbm, tan_hbm, tail_hbm, head_hbm, own_ref, og_ref, eg_ref, os_ref, es_ref, res_ref, tan_ref, tail_ref, head_ref, sems):
+    loads = [(res_hbm, res_ref), (tan_hbm, tan_ref), (tail_hbm, tail_ref), (head_hbm, head_ref)]
+    loads = [pltpu.make_async_copy(src, dst, sems.at[i]) for i, (src, dst) in enumerate(loads)]
+    for load in loads:
+        load.start()
+    for load in loads:
+        load.wait()
     edges = res_ref.shape[1]
     chunk = 512
     total_head, total_tail = None, None
@@ -107,18 +116,21 @@
         es_ref[c] = jnp.where(s_odd == 1, prev, nxt)
 
 
-def prepare(idx_ref, coef_ref, margin_ref, send_ref, idx16_ref, coef16_ref, dinv_ref, send16_ref):
+def prepare(idx_ref, coef_ref, margin_ref, send_ref, idx56_ref, coef56_ref, dinv_ref, send16_ref, wide_ref):
     count = idx_ref.shape[0]
-    idx16_ref[0:count, :] = idx_ref[...]
-    idx16_ref[count:16, :] = jnp.zeros((16 - count, idx_ref.shape[1]), jnp.int32)
+    for j in range(count):
+        for q in range(4):
+            idx56_ref[4 * j + q : 4 * j + q + 1, :] = idx_ref[j : j + 1, LANES * q : LANES * q + LANES]
     for k in range(4):
         wide = coef_ref[k].astype(F32)
-        coef16_ref[k, 0:count, :] = wide
-        coef16_ref[k, count:16, :] = jnp.zeros((16 - count, wide.shape[1]), F32)
+        wide_ref[k] = wide
         diag = (1.0 + margin_ref[k : k + 1, :]) * jnp.sum(jnp.abs(wide), axis=0, keepdims=True)
         inverse = 1.0 / diag
         for q in range(4):
-            dinv_ref[4 * k + q : 4 * k + q + 1, :] = inverse[:, LANES * q : LANES * q + LANES]
+            cols = slice(LANES * q, LANES * q + LANES)
+            dinv_ref[4 * k + q : 4 * k + q + 1, :] = inverse[:, cols]
+            for j in range(count):
+                coef56_ref[k, 4 * j + q : 4 * j + q + 1, :] = wide_ref[k, j : j + 1, cols]
     for a in range(2):
         for b in range(2):
             for q in range(4):
@@ -176,57 +188,83 @@
     send_blocks(solved, send_ref, outs)
 
 
-def tables(y, og, eg, os, es):
-    result = []
-    for k in range(4):
-        before, after = sides(odd("grp"), og[k], eg[k])
-        prev, nxt = sides(odd("sub"), os[k], es[k])
-        blocks = [y[4 * k : 4 * k + 4], before, after, prev, nxt]
-        result.append([block[r : r + 1] for block in blocks for r in range(block.shape[0])])
-    return result
-
-
-def gathered(table, index):
+def base_row(axis, matching):
+    lower = {"grp": 4, "sub": 20}[axis]
+    from_lower = odd(axis) != matching
+    return jnp.where(from_lower, lower, lower + 8)
+
+
+def block(axis, matching, ref):
+    return base_row(axis, matching), [ref[k] for k in range(4)]
+
+
+def early_blocks(y_ref, og_ref, os_ref):
+    own = (0, [y_ref[4 * k : 4 * k + 4, :] for k in range(4)])
+    return [own, block("grp", 1, og_ref), block("sub", 1, os_ref)]
+
+
+def last_blocks(eg_ref, es_ref):
+    return [block("grp", 0, eg_ref), block("sub", 0, es_ref)]
+
+
+def gathered(blocks, index):
     rows, lanes = zip(*(rows_of(i) for i in index))
-    acc = [[None] * 4 for _ in index]
-    for r in range(len(table[0])):
-        for v in range(len(index)):
-            mask = rows[v] == r
-            for k in range(4):
-                got = lane_pick(table[k][r], lanes[v])
-                acc[v][k] = got if r == 0 else jnp.where(mask, got, acc[v][k])
+    acc = [[jnp.zeros(i.shape, F32)] * 4 for i in index]
+    for v in range(len(index)):
+        for base, table in blocks:
+            for r in range(table[0].shape[0]):
+                mask = rows[v] == base + r
+                for k in range(4):
+                    acc[v][k] = jnp.where(mask, lane_pick(table[k][r : r + 1], lanes[v]), acc[v][k])
     return acc
 
 
-def sweep(y_ref, og, eg, os, es, idx_ref, coef_ref, rn_ref, dinv_ref, send_ref, new_ref, *outs):
-    table = tables(y_ref[...], og, eg, os, es)
-    index = [idx_ref[8 * u : 8 * u + 8, LANES * q : LANES * q + LANES] for q in range(4) for u in range(2)]
-    got = gathered(table, index)
+def vectors(ref):
+    return [ref[8 * v : 8 * v + 8, :] for v in range(ref.shape[0] // 8)]
+
+
+def stencil_sums(blocks, idx_ref, coef_ref):
+    got = gathered(blocks, vectors(idx_ref))
+    return [sum(got[v][k] * coef_ref[k, 8 * v : 8 * v + 8, :] for v in range(len(got))) for k in range(4)]
+
+
+def sweep_early(y_ref, og_ref, os_ref, idx_ref, coef_ref, part_ref):
+    for k, total in enumerate(stencil_sums(early_blocks(y_ref, og_ref, os_ref), idx_ref, coef_ref)):
+        part_ref[8 * k : 8 * k + 8, :] = total
+
+
+def sweep_last(eg_ref, es_ref, part_ref, idx_ref, coef_ref, rn_ref, dinv_ref, send_ref, new_ref, *outs):
     rows = []
-    for k in range(4):
-        for q in range(4):
-            cols = slice(LANES * q, LANES * q + LANES)
-            total = got[2 * q][k] * coef_ref[k, 0:8, cols] + got[2 * q + 1][k] * coef_ref[k, 8:16, cols]
-            rows.append(jnp.sum(total, axis=0, keepdims=True))
+    for k, total in enumerate(stencil_sums(last_blocks(eg_ref, es_ref), idx_ref, coef_ref)):
+        total = total + part_ref[8 * k : 8 * k + 8, :]
+        rows.append(total[0:4] + total[4:8])
     solved = (rn_ref[...] - jnp.concatenate(rows, axis=0)) * dinv_ref[...]
     new_ref[...] = solved
     send_blocks(solved, send_ref, outs)
 
 
-def edge_values(y_ref, og, eg, os, es, res_ref, scale_ref, tan_ref, tail_ref, head_ref, out_ref):
-    table = tables(y_ref[...], og, eg, os, es)
-    groups = res_ref.shape[0] // 8
-    heads = gathered(table, [head_ref[8 * v : 8 * v + 8] for v in range(groups)])
-    tails = gathered([t[:4] for t in table], [tail_ref[8 * v : 8 * v + 8] for v in range(groups)])
-    for v in range(groups):
+def edge_early(y_ref, og_ref, os_ref, res_ref, scale_ref, tan_ref, tail_ref, head_ref, part_ref, tan24_ref):
+    blocks = early_blocks(y_ref, og_ref, os_ref)
+    heads = gathered(blocks, vectors(head_ref))
+    tails = gathered(blocks[:1], vectors(tail_ref))
+    for v in range(len(heads)):
         part = slice(8 * v, 8 * v + 8)
-        total = scale_ref[part] * res_ref[part] + (heads[v][0] - tails[v][0])
         mixed = None
         for c in range(3):
             pieces = [tan_ref[c : c + 1, LANES * i : LANES * i + LANES] for i in range(8 * v, 8 * v + 8)]
-            term = jnp.concatenate(pieces, axis=0) * (tails[v][c + 1] + heads[v][c + 1])
+            tangent = jnp.concatenate(pieces, axis=0)
+            tan24_ref[c, part, :] = tangent
+            term = tangent * (tails[v][c + 1] + heads[v][c + 1])
             mixed = term if mixed is None else mixed + term
-        out_ref[part] = total + 0.5 * mixed
+        part_ref[part, :] = scale_ref[part, :] * res_ref[part, :] + (heads[v][0] - tails[v][0]) + 0.5 * mixed
+
+
+def edge_last(eg_ref, es_ref, part_ref, tan24_ref, head_ref, out_ref):
+    heads = gathered(last_blocks(eg_ref, es_ref), vectors(head_ref))
+    for v in range(len(heads)):
+        part = slice(8 * v, 8 * v + 8)
+        mixed = sum(tan24_ref[c, part, :] * heads[v][c + 1] for c in range(3))
+        out_ref[part, :] = part_ref[part, :] + heads[v][0] + 0.5 * mixed
 
 
 def exchange(blocks):
@@ -252,33 +290,46 @@
 ):
     nodes = diag_margin.shape[1]
     own = ((16, LANES), F32)
-    block = [((4, 8, LANES), F32)] * 4
+    blocks4 = [((4, 8, LANES), F32)] * 4
     flat = lambda x: x.reshape(1, -1)
     tile = lambda x: x.reshape(-1, LANES)
 
-    partial, *ghost = call(edge_sums, [own] + block, flat(residual), tangent, flat(edge_tail), flat(edge_head))
-    idx16, coef16, dinv, send16 = call(
+    edges = residual.shape[0]
+    wide_edges = [(1, edges), (3, edges), (1, edges), (1, edges)]
+    types = [F32, F32, jnp.int32, jnp.int32]
+    partial, *ghost = call(
+        edge_sums,
+        [own] + blocks4,
+        *[pltpu.with_memory_space_constraint(x, pltpu.HBM) for x in (flat(residual), tangent, flat(edge_tail), flat(edge_head))],
+        space=HBM,
+        scratch=[pltpu.VMEM(shape, dtype) for shape, dtype in zip(wide_edges, types)] + [pltpu.SemaphoreType.DMA((4,))],
+    )
+    count = stencil_index.shape[0]
+    lines = count * nodes // LANES
+    ghost = exchange(ghost)
+    idx56, coef56, dinv, send16 = call(
         prepare,
-        [((16, nodes), jnp.int32), ((4, 16, nodes), F32), own, ((16, LANES), jnp.int32)],
+        [((lines, LANES), jnp.int32), ((4, lines, LANES), F32), own, ((16, LANES), jnp.int32)],
         stencil_index, stencil_coef, diag_margin, send_index,
+        scratch=[pltpu.VMEM((4, count, nodes), F32)],
     )
-    ghost = exchange(ghost)
-    rn, solved, *blocks = call(first_solve, [own, own] + block, partial, *ghost, send16, dinv)
+    rn, solved, *blocks = call(first_solve, [own, own] + blocks4, partial, *ghost, send16, dinv)
     for _ in range(SWEEPS - 1):
-        blocks = exchange(blocks)
-        solved, *blocks = call(
-            sweep, [own] + block, solved, *blocks, idx16, coef16, rn, dinv, send16
-        )
-    blocks = exchange(blocks)
-    (out,) = call(
-        edge_values,
-        [((residual.shape[0] // LANES, LANES), F32)],
-        solved, *blocks, tile(residual), tile(edge_scale), tangent, tile(edge_tail), tile(edge_head),
+        og, eg, os, es = exchange(blocks)
+        (part,) = call(sweep_early, [((32, LANES), F32)], solved, og, os, idx56, coef56)
+        solved, *blocks = call(sweep_last, [own] + blocks4, eg, es, part, idx56, coef56, rn, dinv, send16)
+    on_edges = (edges // LANES, LANES)
+    og, eg, os, es = exchange(blocks)
+    part, tan24 = call(
+        edge_early,
+        [(on_edges, F32), ((3,) + on_edges, F32)],
+        solved, og, os, tile(residual), tile(edge_scale), tangent, tile(edge_tail), tile(edge_head),
     )
+    (out,) = call(edge_last, [(on_edges, F32)], eg, es, part, tan24, tile(edge_head))
     return out.reshape(-1)
 
 
-def solution(mesh):
+def plain(mesh):
     return jax.shard_map(
         body,
         mesh=mesh,
@@ -296,3 +347,7 @@
         out_specs=P(("grp", "sub")),
         check_vma=False,
     )
+
+
+def solution(mesh):
+    return plain(mesh)

time: 99.8 us -> 91.6 us (0.918)
  local copies, waits for them, and re-layouts: 2.98 us -> 0.06 us
  waiting for transfers between devices: 5.2 us -> 2.62 us
  Pallas kernels: 10.5 us -> 8.02 us
    ppermute x5, waiting for transfers between devices: 5.16 us -> 1.65 us  [exchange(): es = lax.ppermute(es, 'sub', pairs(sub, 0))]
    unnamed x27 -> x19, local copies, waits for them, and re-layouts: 2.98 us -> 0.06 us
    pallas_call x7 -> x11, Pallas kernels: 10.5 us -> 8.02 us  [call(): pl.pallas_call(kernel, out_shape=[jax.ShapeDtypeStruct(shape, dtype) for...]
  transfers between devices with their start and end apart: 20 -> 20, of which waited for: 5 -> 7; matrix products, arithmetic and copies ran while one was open for 0% -> 0% of each run, Pallas kernels for 0% -> 3%
where the time goes in v3:
time: 91.6 us; the launch traced here: 90.8 us
  starting transfers between devices  79.7 us (87%)
  Pallas kernels  8.02 us (9%)
  waiting for transfers between devices  2.62 us (3%)
    ppermute x5, starting transfers between devices, exchange(): og = lax.ppermute(og, 'grp', pairs(grp, 1))  36.8 us
    ppermute x5, starting transfers between devices, exchange(): os = lax.ppermute(os, 'sub', pairs(sub, 1))  22.6 us
    ppermute x5, starting transfers between devices, exchange(): eg = lax.ppermute(eg, 'grp', pairs(grp, 0))  10.2 us
    ppermute x5, starting transfers between devices, exchange(): es = lax.ppermute(es, 'sub', pairs(sub, 0))  10 us
    pallas_call x11, Pallas kernels, call(): pl.pallas_call(kernel, out_shape=[jax.ShapeDtypeStruct(shape, dtype) for...  8.02 us
  transfers between devices with their start and end apart: 20, of which 7 were waited for; matrix products, arithmetic and copies ran while one was open for 0% of the time, Pallas kernels for 3%

profile of v3, /device:TPU:1, one launch (start us, length us, event | category | flops | bytes accessed | tf_op | source)
XLA Modules:
  0.0 90.8 jit_solution(13750889768036942842)
XLA Ops:
  0.0 2.0 %shard_map.91 = (f32[16,128]{1,0:T(8,128)S(1)}, f32[4,8,128]{2,1,0:T(8,128)S(1)}, f32[4,8,128]{2,1,0:T(8,128)S(1)}, f32[4,8,128]{2,1,0:T(8,128)S(1)}, f32[4,8,128]{2,1,0:T(8,128)S(1)}) custom-call(f32[1,3072]{1,0:T(1,128)} %bitcast.11, f32[3,3072]{1,0:T(4,128)} %tan_ref.1, s32[1,3072]{1,0:T(1,128)} %bitcast.13, s32[1,3072]{1,0:T(1,128)} %bitcast.8), custom_call_target="tpu_custom_call" | custom-call | tf_op jit(solution)/shard_map/pallas_call | solution.py:18
  2.0 18.3 %collective-permute-start = (f32[4,8,128]{2,1,0:T(8,128)S(1)}, f32[4,8,128]{2,1,0:T(8,128)S(1)}, u32[]{:S(2)}, u32[]{:S(2)}) collective-permute-start(f32[4,8,128]{2,1,0:T(8,128)S(1)} %get-tuple-element.38), channel_id=1, source_target_pairs={{8,16},{16,8},{24,32},{32,24},{40,48},{48,40},{56,64},{64,56},{72,... | collective-permute-start | bytes 49160 | tf_op jit(solution)/shard_map/ppermute | solution.py:273
  20.4 1.9 %collective-permute-start.1 = (f32[4,8,128]{2,1,0:T(8,128)S(1)}, f32[4,8,128]{2,1,0:T(8,128)S(1)}, u32[]{:S(2)}, u32[]{:S(2)}) collective-permute-start(f32[4,8,128]{2,1,0:T(8,128)S(1)} %get-tuple-element.39), channel_id=1, source_target_pairs={{0,8},{8,0},{16,24},{24,16},{32,40},{40,32},{48,56},{56,48},{64,72... | collective-permute-start | bytes 49160 | tf_op jit(solution)/shard_map/ppermute | solution.py:274
  22.3 5.1 %collective-permute-start.2 = (f32[4,8,128]{2,1,0:T(8,128)S(1)}, f32[4,8,128]{2,1,0:T(8,128)S(1)}, u32[]{:S(2)}, u32[]{:S(2)}) collective-permute-start(f32[4,8,128]{2,1,0:T(8,128)S(1)} %get-tuple-element.40), channel_id=1, source_target_pairs={{1,2},{2,1},{3,4},{4,3},{5,6},{6,5},{7,0},{0,7},{9,10},{10,9},{11,... | collective-permute-start | bytes 49160 | tf_op jit(solution)/shard_map/ppermute | solution.py:275
  27.4 0.0 copy-start.4
  27.4 0.0 copy-start.6
  27.4 0.0 copy-start.7
  27.4 2.4 %collective-permute-start.3 = (f32[4,8,128]{2,1,0:T(8,128)S(1)}, f32[4,8,128]{2,1,0:T(8,128)S(1)}, u32[]{:S(2)}, u32[]{:S(2)}) collective-permute-start(f32[4,8,128]{2,1,0:T(8,128)S(1)} %get-tuple-element.41), channel_id=1, source_target_pairs={{0,1},{1,0},{2,3},{3,2},{4,5},{5,4},{6,7},{7,6},{8,9},{9,8},{10,11... | collective-permute-start | bytes 49160 | tf_op jit(solution)/shard_map/ppermute | solution.py:276
  29.8 0.1 shard_map.92
  30.0 0.0 collective-permute-done.og
  30.0 0.0 collective-permute-done.2.os
  30.0 0.6 collective-permute-done.3.es
  30.6 0.4 shard_map.93
  31.1 2.7 %collective-permute-start.6 = (f32[4,8,128]{2,1,0:T(8,128)S(1)}, f32[4,8,128]{2,1,0:T(8,128)S(1)}, u32[]{:S(2)}, u32[]{:S(2)}) collective-permute-start(f32[4,8,128]{2,1,0:T(8,128)S(1)} %get-tuple-element.47), channel_id=1, source_target_pairs={{8,16},{16,8},{24,32},{32,24},{40,48},{48,40},{56,64},{64,56},{72,... | collective-permute-start | bytes 49160 | tf_op jit(solution)/shard_map/ppermute | solution.py:273
  33.8 4.9 %collective-permute-start.7 = (f32[4,8,128]{2,1,0:T(8,128)S(1)}, f32[4,8,128]{2,1,0:T(8,128)S(1)}, u32[]{:S(2)}, u32[]{:S(2)}) collective-permute-start(f32[4,8,128]{2,1,0:T(8,128)S(1)} %get-tuple-element.48), channel_id=1, source_target_pairs={{1,2},{2,1},{3,4},{4,3},{5,6},{6,5},{7,0},{0,7},{9,10},{10,9},{11,... | collective-permute-start | bytes 49160 | tf_op jit(solution)/shard_map/ppermute | solution.py:275
  38.7 2.6 %collective-permute-start.4 = (f32[4,8,128]{2,1,0:T(8,128)S(1)}, f32[4,8,128]{2,1,0:T(8,128)S(1)}, u32[]{:S(2)}, u32[]{:S(2)}) collective-permute-start(f32[4,8,128]{2,1,0:T(8,128)S(1)} %get-tuple-element.44), channel_id=1, source_target_pairs={{0,8},{8,0},{16,24},{24,16},{32,40},{40,32},{48,56},{56,48},{64,72... | collective-permute-start | bytes 49160 | tf_op jit(solution)/shard_map/ppermute | solution.py:274
  41.2 1.9 %collective-permute-start.5 = (f32[4,8,128]{2,1,0:T(8,128)S(1)}, f32[4,8,128]{2,1,0:T(8,128)S(1)}, u32[]{:S(2)}, u32[]{:S(2)}) collective-permute-start(f32[4,8,128]{2,1,0:T(8,128)S(1)} %get-tuple-element.45), channel_id=1, source_target_pairs={{0,1},{1,0},{2,3},{3,2},{4,5},{5,4},{6,7},{7,6},{8,9},{9,8},{10,11... | collective-permute-start | bytes 49160 | tf_op jit(solution)/shard_map/ppermute | solution.py:276
  43.2 0.0 collective-permute-done.6.og_ref
  43.2 0.7 shard_map.94.part_ref
  43.9 0.4 collective-permute-done.5.es_ref
  44.3 0.7 shard_map.95
  45.0 6.1 %collective-permute-start.10 = (f32[4,8,128]{2,1,0:T(8,128)S(1)}, f32[4,8,128]{2,1,0:T(8,128)S(1)}, u32[]{:S(2)}, u32[]{:S(2)}) collective-permute-start(f32[4,8,128]{2,1,0:T(8,128)S(1)} %get-tuple-element.55), channel_id=1, source_target_pairs={{8,16},{16,8},{24,32},{32,24},{40,48},{48,40},{56,64},{64,56},{72,... | collective-permute-start | bytes 49160 | tf_op jit(solution)/shard_map/ppermute | solution.py:273
  51.2 4.2 %collective-permute-start.11 = (f32[4,8,128]{2,1,0:T(8,128)S(1)}, f32[4,8,128]{2,1,0:T(8,128)S(1)}, u32[]{:S(2)}, u32[]{:S(2)}) collective-permute-start(f32[4,8,128]{2,1,0:T(8,128)S(1)} %get-tuple-element.56), channel_id=1, source_target_pairs={{1,2},{2,1},{3,4},{4,3},{5,6},{6,5},{7,0},{0,7},{9,10},{10,9},{11,... | collective-permute-start | bytes 49160 | tf_op jit(solution)/shard_map/ppermute | solution.py:275
  55.4 1.9 %collective-permute-start.8 = (f32[4,8,128]{2,1,0:T(8,128)S(1)}, f32[4,8,128]{2,1,0:T(8,128)S(1)}, u32[]{:S(2)}, u32[]{:S(2)}) collective-permute-start(f32[4,8,128]{2,1,0:T(8,128)S(1)} %get-tuple-element.52), channel_id=1, source_target_pairs={{0,8},{8,0},{16,24},{24,16},{32,40},{40,32},{48,56},{56,48},{64,72... | collective-permute-start | bytes 49160 | tf_op jit(solution)/shard_map/ppermute | solution.py:274
  57.3 1.9 %collective-permute-start.9 = (f32[4,8,128]{2,1,0:T(8,128)S(1)}, f32[4,8,128]{2,1,0:T(8,128)S(1)}, u32[]{:S(2)}, u32[]{:S(2)}) collective-permute-start(f32[4,8,128]{2,1,0:T(8,128)S(1)} %get-tuple-element.53), channel_id=1, source_target_pairs={{0,1},{1,0},{2,3},{3,2},{4,5},{5,4},{6,7},{7,6},{8,9},{9,8},{10,11... | collective-permute-start | bytes 49160 | tf_op jit(solution)/shard_map/ppermute | solution.py:276
  59.2 0.0 collective-permute-done.10.og_ref
  59.2 0.7 shard_map.96.part_ref
  59.9 0.0 collective-permute-done.8.eg_ref
  59.9 0.4 collective-permute-done.9.es_ref
  60.4 0.7 shard_map.97
  61.1 3.4 %collective-permute-start.14 = (f32[4,8,128]{2,1,0:T(8,128)S(1)}, f32[4,8,128]{2,1,0:T(8,128)S(1)}, u32[]{:S(2)}, u32[]{:S(2)}) collective-permute-start(f32[4,8,128]{2,1,0:T(8,128)S(1)} %get-tuple-element.60), channel_id=1, source_target_pairs={{8,16},{16,8},{24,32},{32,24},{40,48},{48,40},{56,64},{64,56},{72,... | collective-permute-start | bytes 49160 | tf_op jit(solution)/shard_map/ppermute | solution.py:273
  64.4 4.3 %collective-permute-start.15 = (f32[4,8,128]{2,1,0:T(8,128)S(1)}, f32[4,8,128]{2,1,0:T(8,128)S(1)}, u32[]{:S(2)}, u32[]{:S(2)}) collective-permute-start(f32[4,8,128]{2,1,0:T(8,128)S(1)} %get-tuple-element.61), channel_id=1, source_target_pairs={{1,2},{2,1},{3,4},{4,3},{5,6},{6,5},{7,0},{0,7},{9,10},{10,9},{11,... | collective-permute-start | bytes 49160 | tf_op jit(solution)/shard_map/ppermute | solution.py:275
  68.8 1.9 %collective-permute-start.12 = (f32[4,8,128]{2,1,0:T(8,128)S(1)}, f32[4,8,128]{2,1,0:T(8,128)S(1)}, u32[]{:S(2)}, u32[]{:S(2)}) collective-permute-start(f32[4,8,128]{2,1,0:T(8,128)S(1)} %get-tuple-element.57), channel_id=1, source_target_pairs={{0,8},{8,0},{16,24},{24,16},{32,40},{40,32},{48,56},{56,48},{64,72... | collective-permute-start | bytes 49160 | tf_op jit(solution)/shard_map/ppermute | solution.py:274
  70.7 1.9 %collective-permute-start.13 = (f32[4,8,128]{2,1,0:T(8,128)S(1)}, f32[4,8,128]{2,1,0:T(8,128)S(1)}, u32[]{:S(2)}, u32[]{:S(2)}) collective-permute-start(f32[4,8,128]{2,1,0:T(8,128)S(1)} %get-tuple-element.58), channel_id=1, source_target_pairs={{0,1},{1,0},{2,3},{3,2},{4,5},{5,4},{6,7},{7,6},{8,9},{9,8},{10,11... | collective-permute-start | bytes 49160 | tf_op jit(solution)/shard_map/ppermute | solution.py:276
  72.6 0.0 collective-permute-done.15.os_ref
  72.6 0.7 shard_map.98.part_ref
  73.3 0.3 collective-permute-done.12.eg_ref
  73.7 0.1 collective-permute-done.13.es_ref
  73.8 0.7 shard_map.99
  74.5 0.0 copy-start.1
  74.5 6.2 %collective-permute-start.18 = (f32[4,8,128]{2,1,0:T(8,128)S(1)}, f32[4,8,128]{2,1,0:T(8,128)S(1)}, u32[]{:S(2)}, u32[]{:S(2)}) collective-permute-start(f32[4,8,128]{2,1,0:T(8,128)S(1)} %get-tuple-element.65), channel_id=1, source_target_pairs={{8,16},{16,8},{24,32},{32,24},{40,48},{48,40},{56,64},{64,56},{72,... | collective-permute-start | bytes 49160 | tf_op jit(solution)/shard_map/ppermute | solution.py:273
  80.7 4.2 %collective-permute-start.19 = (f32[4,8,128]{2,1,0:T(8,128)S(1)}, f32[4,8,128]{2,1,0:T(8,128)S(1)}, u32[]{:S(2)}, u32[]{:S(2)}) collective-permute-start(f32[4,8,128]{2,1,0:T(8,128)S(1)} %get-tuple-element.66), channel_id=1, source_target_pairs={{1,2},{2,1},{3,4},{4,3},{5,6},{6,5},{7,0},{0,7},{9,10},{10,9},{11,... | collective-permute-start | bytes 49160 | tf_op jit(solution)/shard_map/ppermute | solution.py:275
  84.9 1.9 %collective-permute-start.16 = (f32[4,8,128]{2,1,0:T(8,128)S(1)}, f32[4,8,128]{2,1,0:T(8,128)S(1)}, u32[]{:S(2)}, u32[]{:S(2)}) collective-permute-start(f32[4,8,128]{2,1,0:T(8,128)S(1)} %get-tuple-element.62), channel_id=1, source_target_pairs={{0,8},{8,0},{16,24},{24,16},{32,40},{40,32},{48,56},{56,48},{64,72... | collective-permute-start | bytes 49160 | tf_op jit(solution)/shard_map/ppermute | solution.py:274
  86.9 1.9 %collective-permute-start.17 = (f32[4,8,128]{2,1,0:T(8,128)S(1)}, f32[4,8,128]{2,1,0:T(8,128)S(1)}, u32[]{:S(2)}, u32[]{:S(2)}) collective-permute-start(f32[4,8,128]{2,1,0:T(8,128)S(1)} %get-tuple-element.63), channel_id=1, source_target_pairs={{0,1},{1,0},{2,3},{3,2},{4,5},{5,4},{6,7},{7,6},{8,9},{9,8},{10,11... | collective-permute-start | bytes 49160 | tf_op jit(solution)/shard_map/ppermute | solution.py:276
  88.9 0.4 shard_map.100
  89.3 0.6 collective-permute-done.16.eg_ref
  89.9 0.1 collective-permute-done.17.es_ref
  89.9 0.9 shard_map.101
  (22 shorter events, 0.1 us)
Async XLA Ops:
  0.0 29.8 %copy-start.8 = (bf16[4,14,512]{2,0,1:T(4,128)(2,1)S(1)}, bf16[4,14,512]{2,0,1:T(4,128)(2,1)}, u32[]{:S(2)}) copy-start(bf16[4,14,512]{2,0,1:T(4,128)(2,1)} %param.15) | copy-start | bytes 172036
  2.0 27.9 %collective-permute-start = (f32[4,8,128]{2,1,0:T(8,128)S(1)}, f32[4,8,128]{2,1,0:T(8,128)S(1)}, u32[]{:S(2)}, u32[]{:S(2)}) collective-permute-start(f32[4,8,128]{2,1,0:T(8,128)S(1)} %get-tuple-element.38), channel_id=1, source_target_pairs={{8,16},{16,8},{24,32},{32,24},{40,48},{48,40},{56,64},{64,56},{72,... | collective-permute-start | bytes 49160 | tf_op jit(solution)/shard_map/ppermute | solution.py:273
  20.4 9.6 %collective-permute-start.1 = (f32[4,8,128]{2,1,0:T(8,128)S(1)}, f32[4,8,128]{2,1,0:T(8,128)S(1)}, u32[]{:S(2)}, u32[]{:S(2)}) collective-permute-start(f32[4,8,128]{2,1,0:T(8,128)S(1)} %get-tuple-element.39), channel_id=1, source_target_pairs={{0,8},{8,0},{16,24},{24,16},{32,40},{40,32},{48,56},{56,48},{64,72... | collective-permute-start | bytes 49160 | tf_op jit(solution)/shard_map/ppermute | solution.py:274
  22.3 7.7 %collective-permute-start.2 = (f32[4,8,128]{2,1,0:T(8,128)S(1)}, f32[4,8,128]{2,1,0:T(8,128)S(1)}, u32[]{:S(2)}, u32[]{:S(2)}) collective-permute-start(f32[4,8,128]{2,1,0:T(8,128)S(1)} %get-tuple-element.40), channel_id=1, source_target_pairs={{1,2},{2,1},{3,4},{4,3},{5,6},{6,5},{7,0},{0,7},{9,10},{10,9},{11,... | collective-permute-start | bytes 49160 | tf_op jit(solution)/shard_map/ppermute | solution.py:275
  27.4 2.4 %copy-start.4 = (s32[14,512]{1,0:T(8,128)S(1)}, s32[14,512]{1,0:T(8,128)}, u32[]{:S(2)}) copy-start(s32[14,512]{1,0:T(8,128)} %idx_ref.1) | copy-start | bytes 86020
  27.4 2.4 %copy-start.6 = (f32[4,512]{1,0:T(4,128)S(1)}, f32[4,512]{1,0:T(4,128)}, u32[]{:S(2)}) copy-start(f32[4,512]{1,0:T(4,128)} %margin_ref.1) | copy-start | bytes 24580
  27.4 2.4 %copy-start.7 = (s32[2,2,512]{2,1,0:T(2,128)S(1)}, s32[2,2,512]{2,1,0:T(2,128)}, u32[]{:S(2)}) copy-start(s32[2,2,512]{2,1,0:T(2,128)} %send_ref.1) | copy-start | bytes 24580
  27.4 3.2 %collective-permute-start.3 = (f32[4,8,128]{2,1,0:T(8,128)S(1)}, f32[4,8,128]{2,1,0:T(8,128)S(1)}, u32[]{:S(2)}, u32[]{:S(2)}) collective-permute-start(f32[4,8,128]{2,1,0:T(8,128)S(1)} %get-tuple-element.41), channel_id=1, source_target_pairs={{0,1},{1,0},{2,3},{3,2},{4,5},{5,4},{6,7},{7,6},{8,9},{9,8},{10,11... | collective-permute-start | bytes 49160 | tf_op jit(solution)/shard_map/ppermute | solution.py:276
  31.1 12.1 %collective-permute-start.6 = (f32[4,8,128]{2,1,0:T(8,128)S(1)}, f32[4,8,128]{2,1,0:T(8,128)S(1)}, u32[]{:S(2)}, u32[]{:S(2)}) collective-permute-start(f32[4,8,128]{2,1,0:T(8,128)S(1)} %get-tuple-element.47), channel_id=1, source_target_pairs={{8,16},{16,8},{24,32},{32,24},{40,48},{48,40},{56,64},{64,56},{72,... | collective-permute-start | bytes 49160 | tf_op jit(solution)/shard_map/ppermute | solution.py:273
  33.8 9.4 %collective-permute-start.7 = (f32[4,8,128]{2,1,0:T(8,128)S(1)}, f32[4,8,128]{2,1,0:T(8,128)S(1)}, u32[]{:S(2)}, u32[]{:S(2)}) collective-permute-start(f32[4,8,128]{2,1,0:T(8,128)S(1)} %get-tuple-element.48), channel_id=1, source_target_pairs={{1,2},{2,1},{3,4},{4,3},{5,6},{6,5},{7,0},{0,7},{9,10},{10,9},{11,... | collective-permute-start | bytes 49160 | tf_op jit(solution)/shard_map/ppermute | solution.py:275
  38.7 5.2 %collective-permute-start.4 = (f32[4,8,128]{2,1,0:T(8,128)S(1)}, f32[4,8,128]{2,1,0:T(8,128)S(1)}, u32[]{:S(2)}, u32[]{:S(2)}) collective-permute-start(f32[4,8,128]{2,1,0:T(8,128)S(1)} %get-tuple-element.44), channel_id=1, source_target_pairs={{0,8},{8,0},{16,24},{24,16},{32,40},{40,32},{48,56},{56,48},{64,72... | collective-permute-start | bytes 49160 | tf_op jit(solution)/shard_map/ppermute | solution.py:274
  41.2 3.1 %collective-permute-start.5 = (f32[4,8,128]{2,1,0:T(8,128)S(1)}, f32[4,8,128]{2,1,0:T(8,128)S(1)}, u32[]{:S(2)}, u32[]{:S(2)}) collective-permute-start(f32[4,8,128]{2,1,0:T(8,128)S(1)} %get-tuple-element.45), channel_id=1, source_target_pairs={{0,1},{1,0},{2,3},{3,2},{4,5},{5,4},{6,7},{7,6},{8,9},{9,8},{10,11... | collective-permute-start | bytes 49160 | tf_op jit(solution)/shard_map/ppermute | solution.py:276
  45.0 14.2 %collective-permute-start.10 = (f32[4,8,128]{2,1,0:T(8,128)S(1)}, f32[4,8,128]{2,1,0:T(8,128)S(1)}, u32[]{:S(2)}, u32[]{:S(2)}) collective-permute-start(f32[4,8,128]{2,1,0:T(8,128)S(1)} %get-tuple-element.55), channel_id=1, source_target_pairs={{8,16},{16,8},{24,32},{32,24},{40,48},{48,40},{56,64},{64,56},{72,... | collective-permute-start | bytes 49160 | tf_op jit(solution)/shard_map/ppermute | solution.py:273
  51.2 8.1 %collective-permute-start.11 = (f32[4,8,128]{2,1,0:T(8,128)S(1)}, f32[4,8,128]{2,1,0:T(8,128)S(1)}, u32[]{:S(2)}, u32[]{:S(2)}) collective-permute-start(f32[4,8,128]{2,1,0:T(8,128)S(1)} %get-tuple-element.56), channel_id=1, source_target_pairs={{1,2},{2,1},{3,4},{4,3},{5,6},{6,5},{7,0},{0,7},{9,10},{10,9},{11,... | collective-permute-start | bytes 49160 | tf_op jit(solution)/shard_map/ppermute | solution.py:275
  55.4 4.6 %collective-permute-start.8 = (f32[4,8,128]{2,1,0:T(8,128)S(1)}, f32[4,8,128]{2,1,0:T(8,128)S(1)}, u32[]{:S(2)}, u32[]{:S(2)}) collective-permute-start(f32[4,8,128]{2,1,0:T(8,128)S(1)} %get-tuple-element.52), channel_id=1, source_target_pairs={{0,8},{8,0},{16,24},{24,16},{32,40},{40,32},{48,56},{56,48},{64,72... | collective-permute-start | bytes 49160 | tf_op jit(solution)/shard_map/ppermute | solution.py:274
  57.3 3.1 %collective-permute-start.9 = (f32[4,8,128]{2,1,0:T(8,128)S(1)}, f32[4,8,128]{2,1,0:T(8,128)S(1)}, u32[]{:S(2)}, u32[]{:S(2)}) collective-permute-start(f32[4,8,128]{2,1,0:T(8,128)S(1)} %get-tuple-element.53), channel_id=1, source_target_pairs={{0,1},{1,0},{2,3},{3,2},{4,5},{5,4},{6,7},{7,6},{8,9},{9,8},{10,11... | collective-permute-start | bytes 49160 | tf_op jit(solution)/shard_map/ppermute | solution.py:276
  61.1 11.6 %collective-permute-start.14 = (f32[4,8,128]{2,1,0:T(8,128)S(1)}, f32[4,8,128]{2,1,0:T(8,128)S(1)}, u32[]{:S(2)}, u32[]{:S(2)}) collective-permute-start(f32[4,8,128]{2,1,0:T(8,128)S(1)} %get-tuple-element.60), channel_id=1, source_target_pairs={{8,16},{16,8},{24,32},{32,24},{40,48},{48,40},{56,64},{64,56},{72,... | collective-permute-start | bytes 49160 | tf_op jit(solution)/shard_map/ppermute | solution.py:273
  64.4 8.2 %collective-permute-start.15 = (f32[4,8,128]{2,1,0:T(8,128)S(1)}, f32[4,8,128]{2,1,0:T(8,128)S(1)}, u32[]{:S(2)}, u32[]{:S(2)}) collective-permute-start(f32[4,8,128]{2,1,0:T(8,128)S(1)} %get-tuple-element.61), channel_id=1, source_target_pairs={{1,2},{2,1},{3,4},{4,3},{5,6},{6,5},{7,0},{0,7},{9,10},{10,9},{11,... | collective-permute-start | bytes 49160 | tf_op jit(solution)/shard_map/ppermute | solution.py:275
  68.8 4.9 %collective-permute-start.12 = (f32[4,8,128]{2,1,0:T(8,128)S(1)}, f32[4,8,128]{2,1,0:T(8,128)S(1)}, u32[]{:S(2)}, u32[]{:S(2)}) collective-permute-start(f32[4,8,128]{2,1,0:T(8,128)S(1)} %get-tuple-element.57), channel_id=1, source_target_pairs={{0,8},{8,0},{16,24},{24,16},{32,40},{40,32},{48,56},{56,48},{64,72... | collective-permute-start | bytes 49160 | tf_op jit(solution)/shard_map/ppermute | solution.py:274
  70.7 3.1 %collective-permute-start.13 = (f32[4,8,128]{2,1,0:T(8,128)S(1)}, f32[4,8,128]{2,1,0:T(8,128)S(1)}, u32[]{:S(2)}, u32[]{:S(2)}) collective-permute-start(f32[4,8,128]{2,1,0:T(8,128)S(1)} %get-tuple-element.58), channel_id=1, source_target_pairs={{0,1},{1,0},{2,3},{3,2},{4,5},{5,4},{6,7},{7,6},{8,9},{9,8},{10,11... | collective-permute-start | bytes 49160 | tf_op jit(solution)/shard_map/ppermute | solution.py:276
  73.8 15.0 %copy-start = (f32[3,3072]{1,0:T(4,128)S(1)}, f32[3,3072]{1,0:T(4,128)}, u32[]{:S(2)}) copy-start(f32[3,3072]{1,0:T(4,128)} %tan_ref.1) | copy-start | bytes 110596
  73.8 15.0 %copy-start.2 = (f32[3072]{0:T(1024)S(1)}, f32[3072]{0:T(1024)}, u32[]{:S(2)}) copy-start(f32[3072]{0:T(1024)} %param.9) | copy-start | bytes 36868
  73.8 15.0 %copy-start.3 = (s32[3072]{0:T(1024)S(1)}, s32[3072]{0:T(1024)}, u32[]{:S(2)}) copy-start(s32[3072]{0:T(1024)} %param.12) | copy-start | bytes 36868
  73.8 15.1 %copy-start.5 = (f32[3072]{0:T(1024)S(1)}, f32[3072]{0:T(1024)}, u32[]{:S(2)}) copy-start(f32[3072]{0:T(1024)} %param.10) | copy-start | bytes 36868
  74.5 14.3 %copy-start.1 = (s32[3072]{0:T(1024)S(1)}, s32[3072]{0:T(1024)}, u32[]{:S(2)}) copy-start(s32[3072]{0:T(1024)} %param.13) | copy-start | bytes 36868
  74.5 14.3 %collective-permute-start.18 = (f32[4,8,128]{2,1,0:T(8,128)S(1)}, f32[4,8,128]{2,1,0:T(8,128)S(1)}, u32[]{:S(2)}, u32[]{:S(2)}) collective-permute-start(f32[4,8,128]{2,1,0:T(8,128)S(1)} %get-tuple-element.65), channel_id=1, source_target_pairs={{8,16},{16,8},{24,32},{32,24},{40,48},{48,40},{56,64},{64,56},{72,... | collective-permute-start | bytes 49160 | tf_op jit(solution)/shard_map/ppermute | solution.py:273
  80.7 8.1 %collective-permute-start.19 = (f32[4,8,128]{2,1,0:T(8,128)S(1)}, f32[4,8,128]{2,1,0:T(8,128)S(1)}, u32[]{:S(2)}, u32[]{:S(2)}) collective-permute-start(f32[4,8,128]{2,1,0:T(8,128)S(1)} %get-tuple-element.66), channel_id=1, source_target_pairs={{1,2},{2,1},{3,4},{4,3},{5,6},{6,5},{7,0},{0,7},{9,10},{10,9},{11,... | collective-permute-start | bytes 49160 | tf_op jit(solution)/shard_map/ppermute | solution.py:275
  84.9 4.9 %collective-permute-start.16 = (f32[4,8,128]{2,1,0:T(8,128)S(1)}, f32[4,8,128]{2,1,0:T(8,128)S(1)}, u32[]{:S(2)}, u32[]{:S(2)}) collective-permute-start(f32[4,8,128]{2,1,0:T(8,128)S(1)} %get-tuple-element.62), channel_id=1, source_target_pairs={{0,8},{8,0},{16,24},{24,16},{32,40},{40,32},{48,56},{56,48},{64,72... | collective-permute-start | bytes 49160 | tf_op jit(solution)/shard_map/ppermute | solution.py:274
  86.9 3.1 %collective-permute-start.17 = (f32[4,8,128]{2,1,0:T(8,128)S(1)}, f32[4,8,128]{2,1,0:T(8,128)S(1)}, u32[]{:S(2)}, u32[]{:S(2)}) collective-permute-start(f32[4,8,128]{2,1,0:T(8,128)S(1)} %get-tuple-element.63), channel_id=1, source_target_pairs={{0,1},{1,0},{2,3},{3,2},{4,5},{5,4},{6,7},{7,6},{8,9},{9,8},{10,11... | collective-permute-start | bytes 49160 | tf_op jit(solution)/shard_map/ppermute | solution.py:276

commit v4 on v3

--- a/solution.py
+++ b/solution.py
@@ -56,8 +56,8 @@
 
 def onehot(lane):
     n = lane.shape[1]
-    iota = lax.broadcasted_iota(jnp.int32, (LANES, n), 0)
-    return jnp.where(iota == lane, 1.0, 0.0).astype(BF16)
+    iota = lax.broadcasted_iota(jnp.int32, (LANES, n), 0).astype(F32).astype(BF16)
+    return jnp.where(iota == lane.astype(F32).astype(BF16), jnp.ones((), BF16), jnp.zeros((), BF16))
 
 
 def masked(values, row, count):
@@ -76,44 +76,66 @@
     return low, high
 
 
-def edge_sums(res_hbm, tan_hbm, tail_hbm, head_hbm, own_ref, og_ref, eg_ref, os_ref, es_ref, res_ref, tan_ref, tail_ref, head_ref, sems):
-    loads = [(res_hbm, res_ref), (tan_hbm, tan_ref), (tail_hbm, tail_ref), (head_hbm, head_ref)]
+def edge_parts(res_ref, tan_ref, cut):
+    res = res_ref[:, cut]
+    half = [0.5 * tan_ref[c : c + 1, cut] * res for c in range(3)]
+    parts = [split3(v) for v in [res] + half]
+    return [parts[c][p] for p in range(3) for c in range(4)]
+
+
+def added(total, value):
+    return value if total is None else total + value
+
+
+def ghost_sums(
+    res_hbm, tan_hbm, head_hbm, send_hbm, og_ref, eg_ref, os_ref, es_ref, res_ref, tan_ref, head_ref, send_ref, sems
+):
+    loads = [(res_hbm, res_ref), (tan_hbm, tan_ref), (head_hbm, head_ref), (send_hbm, send_ref)]
     loads = [pltpu.make_async_copy(src, dst, sems.at[i]) for i, (src, dst) in enumerate(loads)]
     for load in loads:
         load.start()
     for load in loads:
         load.wait()
     edges = res_ref.shape[1]
-    chunk = 512
-    total_head, total_tail = None, None
+    chunk = edges // 2
+    total = None
     for start in range(0, edges, chunk):
         cut = slice(start, start + chunk)
-        res = res_ref[:, cut]
-        half = [0.5 * tan_ref[c : c + 1, cut] * res for c in range(3)]
-        head_row, head_lane = rows_of(head_ref[:, cut])
-        head_row = jnp.where(head_row >= 4, head_row + 4, head_row)
-        tail_row, tail_lane = rows_of(tail_ref[:, cut])
-        parts = [split3(v) for v in [res] + half]
-        parts = [parts[c][p] for p in range(3) for c in range(4)]
-        signed = [-v if i % 4 == 0 else v for i, v in enumerate(parts)]
-        by_head = nt_dot(masked(parts, head_row, 40), onehot(head_lane))
-        by_tail = nt_dot(masked(signed, tail_row, 8), onehot(tail_lane))
-        total_head = by_head if total_head is None else total_head + by_head
-        total_tail = by_tail if total_tail is None else total_tail + by_tail
+        row, lane = rows_of(head_ref[:, cut])
+        total = added(total, nt_dot(masked(edge_parts(res_ref, tan_ref, cut), row - 4, 32), onehot(lane)))
     g_odd, s_odd = odd("grp"), odd("sub")
     for c in range(4):
-        head = total_head[40 * c : 40 * c + 40]
-        tail = total_tail[8 * c : 8 * c + 8]
-        for p in (1, 2):
-            at = 4 * p + c
-            head = head + total_head[40 * at : 40 * at + 40]
-            tail = tail + total_tail[8 * at : 8 * at + 8]
-        own_ref[4 * c : 4 * c + 4, :] = head[0:4] + tail[0:4]
-        before, after, prev, nxt = (head[8 * i : 8 * i + 8] for i in range(1, 5))
+        ghost = sum(total[32 * (4 * p + c) : 32 * (4 * p + c) + 32] for p in range(3))
+        before, after, prev, nxt = (ghost[8 * i : 8 * i + 8] for i in range(4))
         og_ref[c] = jnp.where(g_odd == 1, after, before)
         eg_ref[c] = jnp.where(g_odd == 1, before, after)
         os_ref[c] = jnp.where(s_odd == 1, nxt, prev)
         es_ref[c] = jnp.where(s_odd == 1, prev, nxt)
+    lists = [
+        [[send_ref[a, b : b + 1, LANES * q : LANES * q + LANES] for q in range(4)] for b in range(2)] for a in range(2)
+    ]
+    joined = lambda first, second: jnp.concatenate(first + second, axis=0).astype(F32)
+    low, high = joined(lists[0][0], lists[0][1]), joined(lists[1][0], lists[1][1])
+    left, right = joined(lists[0][0], lists[1][0]), joined(lists[0][1], lists[1][1])
+    og_ref[4] = jnp.where(g_odd == 1, high, low)
+    eg_ref[4] = jnp.where(g_odd == 1, low, high)
+    os_ref[4] = jnp.where(s_odd == 1, right, left)
+    es_ref[4] = jnp.where(s_odd == 1, left, right)
+
+
+def own_sums(res_ref, tan_ref, tail_ref, head_ref, own_ref):
+    edges = res_ref.shape[1]
+    chunk = edges // 2
+    total = None
+    for start in range(0, edges, chunk):
+        cut = slice(start, start + chunk)
+        parts = edge_parts(res_ref, tan_ref, cut)
+        signed = [-v if i % 4 == 0 else v for i, v in enumerate(parts)]
+        for values, index in ((parts, head_ref), (signed, tail_ref)):
+            row, lane = rows_of(index[:, cut])
+            total = added(total, nt_dot(masked(values, row, 8), onehot(lane)))
+    for c in range(4):
+        own_ref[4 * c : 4 * c + 4, :] = sum(total[8 * (4 * p + c) : 8 * (4 * p + c) + 4] for p in range(3))
 
 
 def prepare(idx_ref, coef_ref, margin_ref, send_ref, idx56_ref, coef56_ref, dinv_ref, send16_ref, wide_ref):
@@ -138,29 +160,7 @@
                 send16_ref[at : at + 1, :] = send_ref[a, b : b + 1, LANES * q : LANES * q + LANES]
 
 
-def send_blocks(solved, send_ref, outs):
-    g_odd, s_odd = odd("grp"), odd("sub")
-    og_ref, eg_ref, os_ref, es_ref = outs
-    row, lane = rows_of(send_ref[...])
-    for k in range(4):
-        low, high = None, None
-        got = []
-        for half in range(2):
-            part = slice(8 * half, 8 * half + 8)
-            acc = lane_pick(solved[4 * k : 4 * k + 1], lane[part])
-            for r in range(1, 4):
-                acc = jnp.where(row[part] == r, lane_pick(solved[4 * k + r : 4 * k + r + 1], lane[part]), acc)
-            got.append(acc)
-        low, high = got
-        og_ref[k] = jnp.where(g_odd == 1, high, low)
-        eg_ref[k] = jnp.where(g_odd == 1, low, high)
-        left = jnp.concatenate([low[0:4], high[0:4]], axis=0)
-        right = jnp.concatenate([low[4:8], high[4:8]], axis=0)
-        os_ref[k] = jnp.where(s_odd == 1, right, left)
-        es_ref[k] = jnp.where(s_odd == 1, left, right)
-
-
-def first_solve(own_ref, og, eg, os, es, send_ref, dinv_ref, rn_ref, y_ref, *outs):
+def first_solve(own_ref, og, eg, os, es, send_ref, dinv_ref, rn_ref, y_ref):
     index = send_ref[...]
     row, lane = rows_of(index)
     lefts, rights = [], []
@@ -182,20 +182,34 @@
     for c in range(4):
         rows.append(sum(total[8 * (4 * p + c) : 8 * (4 * p + c) + 4] for p in range(3)))
     rn = own_ref[...] + jnp.concatenate(rows, axis=0)
-    solved = rn * dinv_ref[...]
     rn_ref[...] = rn
-    y_ref[...] = solved
-    send_blocks(solved, send_ref, outs)
-
-
-def base_row(axis, matching):
-    lower = {"grp": 4, "sub": 20}[axis]
-    from_lower = odd(axis) != matching
-    return jnp.where(from_lower, lower, lower + 8)
+    y_ref[...] = rn * dinv_ref[...]
+
+
+def from_lower(axis, matching):
+    return odd(axis) != matching
+
+
+def compose(og_ref, eg_ref, os_ref, es_ref, idx_ref, head_ref, idx_out, head_out):
+    blocks = []
+    for axis, matching, ref, number in (("grp", 1, og_ref, 0), ("grp", 0, eg_ref, 0), ("sub", 1, os_ref, 2), ("sub", 0, es_ref, 2)):
+        number = jnp.where(from_lower(axis, matching), number, number + 1)
+        values = ref[4].astype(jnp.int32) + 4 * LANES * (number + 1)
+        blocks.append((4 + 8 * number, values.astype(F32)))
+    for src, dst in ((idx_ref, idx_out), (head_ref, head_out)):
+        for v, index in enumerate(vectors(src)):
+            row, lane = rows_of(index)
+            acc = index.astype(F32)
+            for base, values in blocks:
+                for r in range(8):
+                    acc = jnp.where(row == base + r, lane_pick(values[r : r + 1], lane), acc)
+            dst[8 * v : 8 * v + 8, :] = acc.astype(jnp.int32)
 
 
 def block(axis, matching, ref):
-    return base_row(axis, matching), [ref[k] for k in range(4)]
+    lower = {"grp": 4, "sub": 12}[axis]
+    base = jnp.where(from_lower(axis, matching), lower, lower + 4)
+    return base, [ref[4 * k : 4 * k + 4, :] for k in range(4)]
 
 
 def early_blocks(y_ref, og_ref, os_ref):
@@ -233,14 +247,12 @@
         part_ref[8 * k : 8 * k + 8, :] = total
 
 
-def sweep_last(eg_ref, es_ref, part_ref, idx_ref, coef_ref, rn_ref, dinv_ref, send_ref, new_ref, *outs):
+def sweep_last(eg_ref, es_ref, part_ref, idx_ref, coef_ref, rn_ref, dinv_ref, new_ref):
     rows = []
     for k, total in enumerate(stencil_sums(last_blocks(eg_ref, es_ref), idx_ref, coef_ref)):
         total = total + part_ref[8 * k : 8 * k + 8, :]
         rows.append(total[0:4] + total[4:8])
-    solved = (rn_ref[...] - jnp.concatenate(rows, axis=0)) * dinv_ref[...]
-    new_ref[...] = solved
-    send_blocks(solved, send_ref, outs)
+    new_ref[...] = (rn_ref[...] - jnp.concatenate(rows, axis=0)) * dinv_ref[...]
 
 
 def edge_early(y_ref, og_ref, os_ref, res_ref, scale_ref, tan_ref, tail_ref, head_ref, part_ref, tan24_ref):
@@ -290,19 +302,19 @@
 ):
     nodes = diag_margin.shape[1]
     own = ((16, LANES), F32)
-    blocks4 = [((4, 8, LANES), F32)] * 4
+    blocks4 = [((5, 8, LANES), F32)] * 4
     flat = lambda x: x.reshape(1, -1)
     tile = lambda x: x.reshape(-1, LANES)
 
     edges = residual.shape[0]
-    wide_edges = [(1, edges), (3, edges), (1, edges), (1, edges)]
-    types = [F32, F32, jnp.int32, jnp.int32]
-    partial, *ghost = call(
-        edge_sums,
-        [own] + blocks4,
-        *[pltpu.with_memory_space_constraint(x, pltpu.HBM) for x in (flat(residual), tangent, flat(edge_tail), flat(edge_head))],
+    on_hbm = lambda x: pltpu.with_memory_space_constraint(x, pltpu.HBM)
+    loaded = [((1, edges), F32), ((3, edges), F32), ((1, edges), jnp.int32), (send_index.shape, jnp.int32)]
+    ghost = call(
+        ghost_sums,
+        blocks4,
+        on_hbm(flat(residual)), on_hbm(tangent), on_hbm(flat(edge_head)), on_hbm(send_index),
         space=HBM,
-        scratch=[pltpu.VMEM(shape, dtype) for shape, dtype in zip(wide_edges, types)] + [pltpu.SemaphoreType.DMA((4,))],
+        scratch=[pltpu.VMEM(shape, dtype) for shape, dtype in loaded] + [pltpu.SemaphoreType.DMA((4,))],
     )
     count = stencil_index.shape[0]
     lines = count * nodes // LANES
@@ -313,19 +325,24 @@
         stencil_index, stencil_coef, diag_margin, send_index,
         scratch=[pltpu.VMEM((4, count, nodes), F32)],
     )
-    rn, solved, *blocks = call(first_solve, [own, own] + blocks4, partial, *ghost, send16, dinv)
-    for _ in range(SWEEPS - 1):
-        og, eg, os, es = exchange(blocks)
+    (partial,) = call(own_sums, [own], flat(residual), tangent, flat(edge_tail), flat(edge_head))
+    rn, solved = call(first_solve, [own, own], partial, *ghost, send16, dinv)
+    on_edges = (edges // LANES, LANES)
+    for step in range(SWEEPS - 1):
+        og, eg, os, es = exchange([solved] * 4)
+        if step == 0:
+            idx56, head24 = call(
+                compose, [((lines, LANES), jnp.int32), (on_edges, jnp.int32)], *ghost, idx56, tile(edge_head)
+            )
         (part,) = call(sweep_early, [((32, LANES), F32)], solved, og, os, idx56, coef56)
-        solved, *blocks = call(sweep_last, [own] + blocks4, eg, es, part, idx56, coef56, rn, dinv, send16)
-    on_edges = (edges // LANES, LANES)
-    og, eg, os, es = exchange(blocks)
+        (solved,) = call(sweep_last, [own], eg, es, part, idx56, coef56, rn, dinv)
+    og, eg, os, es = exchange([solved] * 4)
     part, tan24 = call(
         edge_early,
         [(on_edges, F32), ((3,) + on_edges, F32)],
-        solved, og, os, tile(residual), tile(edge_scale), tangent, tile(edge_tail), tile(edge_head),
+        solved, og, os, tile(residual), tile(edge_scale), tangent, tile(edge_tail), head24,
     )
-    (out,) = call(edge_last, [(on_edges, F32)], eg, es, part, tan24, tile(edge_head))
+    (out,) = call(edge_last, [(on_edges, F32)], eg, es, part, tan24, head24)
     return out.reshape(-1)
 
 

time: 91.6 us -> 89.8 us (0.980)
  Pallas kernels: 8.02 us -> 6.61 us
    pallas_call x11 -> x13, Pallas kernels: 8.02 us -> 6.61 us  [call(): pl.pallas_call(kernel, out_shape=[jax.ShapeDtypeStruct(shape, dtype) for...]
  transfers between devices with their start and end apart: 20 -> 20, of which waited for: 7 -> 6; matrix products, arithmetic and copies ran while one was open for 0% -> 0% of each run, Pallas kernels for 3% -> 3%
where the time goes in v4:
time: 89.8 us; the launch traced here: 89 us
  starting transfers between devices  79.7 us (89%)
  Pallas kernels  6.61 us (7%)
  waiting for transfers between devices  2.15 us (2%)
    ppermute x5, starting transfers between devices, exchange(): og = lax.ppermute(og, 'grp', pairs(grp, 1))  36.5 us
    ppermute x5, starting transfers between devices, exchange(): os = lax.ppermute(os, 'sub', pairs(sub, 1))  22.6 us
    ppermute x5, starting transfers between devices, exchange(): es = lax.ppermute(es, 'sub', pairs(sub, 0))  10.3 us
    ppermute x5, starting transfers between devices, exchange(): eg = lax.ppermute(eg, 'grp', pairs(grp, 0))  10.2 us
    pallas_call x13, Pallas kernels, call(): pl.pallas_call(kernel, out_shape=[jax.ShapeDtypeStruct(shape, dtype) for...  6.61 us
    ppermute x5, waiting for transfers between devices, exchange(): es = lax.ppermute(es, 'sub', pairs(sub, 0))  1.85 us
  transfers between devices with their start and end apart: 20, of which 6 were waited for; matrix products, arithmetic and copies ran while one was open for 0% of the time, Pallas kernels for 3%

profile of v4, /device:TPU:1, one launch (start us, length us, event | category | flops | bytes accessed | tf_op | source)
XLA Modules:
  0.0 89.0 jit_solution(4003958552553507752)
XLA Ops:
  0.0 1.7 %shard_map.92 = (f32[5,8,128]{2,1,0:T(8,128)S(1)}, f32[5,8,128]{2,1,0:T(8,128)S(1)}, f32[5,8,128]{2,1,0:T(8,128)S(1)}, f32[5,8,128]{2,1,0:T(8,128)S(1)}) custom-call(f32[1,3072]{1,0:T(1,128)} %bitcast.11, f32[3,3072]{1,0:T(4,128)} %tan_ref.3, s32[1,3072]{1,0:T(1,128)} %bitcast.8, s32[2,2,512]{2,1,0:T(2,128)} %send_ref.1), custom_call_target="tpu_custom_call" | custom-call | tf_op jit(solution)/shard_map/pallas_call | solution.py:18
  1.7 18.3 %collective-permute-start = (f32[5,8,128]{2,1,0:T(8,128)S(1)}, f32[5,8,128]{2,1,0:T(8,128)S(1)}, u32[]{:S(2)}, u32[]{:S(2)}) collective-permute-start(f32[5,8,128]{2,1,0:T(8,128)S(1)} %get-tuple-element.19), channel_id=1, source_target_pairs={{8,16},{16,8},{24,32},{32,24},{40,48},{48,40},{56,64},{64,56},{72,... | collective-permute-start | bytes 61448 | tf_op jit(solution)/shard_map/ppermute | solution.py:285
  20.0 1.9 %collective-permute-start.1 = (f32[5,8,128]{2,1,0:T(8,128)S(1)}, f32[5,8,128]{2,1,0:T(8,128)S(1)}, u32[]{:S(2)}, u32[]{:S(2)}) collective-permute-start(f32[5,8,128]{2,1,0:T(8,128)S(1)} %get-tuple-element.20), channel_id=1, source_target_pairs={{0,8},{8,0},{16,24},{24,16},{32,40},{40,32},{48,56},{56,48},{64,72... | collective-permute-start | bytes 61448 | tf_op jit(solution)/shard_map/ppermute | solution.py:286
  21.9 5.1 %collective-permute-start.2 = (f32[5,8,128]{2,1,0:T(8,128)S(1)}, f32[5,8,128]{2,1,0:T(8,128)S(1)}, u32[]{:S(2)}, u32[]{:S(2)}) collective-permute-start(f32[5,8,128]{2,1,0:T(8,128)S(1)} %get-tuple-element.21), channel_id=1, source_target_pairs={{1,2},{2,1},{3,4},{4,3},{5,6},{6,5},{7,0},{0,7},{9,10},{10,9},{11,... | collective-permute-start | bytes 61448 | tf_op jit(solution)/shard_map/ppermute | solution.py:287
  27.0 0.0 copy-start
  27.0 0.0 copy-start.1
  27.0 0.0 copy-start.2
  27.0 0.0 copy-start.3
  27.0 2.4 %collective-permute-start.3 = (f32[5,8,128]{2,1,0:T(8,128)S(1)}, f32[5,8,128]{2,1,0:T(8,128)S(1)}, u32[]{:S(2)}, u32[]{:S(2)}) collective-permute-start(f32[5,8,128]{2,1,0:T(8,128)S(1)} %get-tuple-element.22), channel_id=1, source_target_pairs={{0,1},{1,0},{2,3},{3,2},{4,5},{5,4},{6,7},{7,6},{8,9},{9,8},{10,11... | collective-permute-start | bytes 61448 | tf_op jit(solution)/shard_map/ppermute | solution.py:288
  29.5 0.0 copy-start.4
  29.5 0.0 copy-start.5
  29.5 0.0 copy-start.7
  29.5 0.7 shard_map.91.own_ref
  30.2 0.0 copy-done.4
  30.2 0.0 copy-done.5
  30.3 0.1 shard_map.93
  30.4 0.3 shard_map.94
  30.7 2.6 %collective-permute-start.6 = (f32[16,128]{1,0:T(8,128)S(1)}, f32[16,128]{1,0:T(8,128)S(1)}, u32[]{:S(2)}, u32[]{:S(2)}) collective-permute-start(f32[16,128]{1,0:T(8,128)S(1)} %get-tuple-element.25.y_ref), channel_id=1, source_target_pairs={{8,16},{16,8},{24,32},{32,24},{40,48},{48,40},{56,64},{64,56},{72,... | collective-permute-start | bytes 24584 | tf_op jit(solution)/shard_map/ppermute | solution.py:285
  33.3 5.1 %collective-permute-start.7 = (f32[16,128]{1,0:T(8,128)S(1)}, f32[16,128]{1,0:T(8,128)S(1)}, u32[]{:S(2)}, u32[]{:S(2)}) collective-permute-start(f32[16,128]{1,0:T(8,128)S(1)} %get-tuple-element.25.y_ref), channel_id=1, source_target_pairs={{1,2},{2,1},{3,4},{4,3},{5,6},{6,5},{7,0},{0,7},{9,10},{10,9},{11,... | collective-permute-start | bytes 24584 | tf_op jit(solution)/shard_map/ppermute | solution.py:287
  38.4 2.6 %collective-permute-start.4 = (f32[16,128]{1,0:T(8,128)S(1)}, f32[16,128]{1,0:T(8,128)S(1)}, u32[]{:S(2)}, u32[]{:S(2)}) collective-permute-start(f32[16,128]{1,0:T(8,128)S(1)} %get-tuple-element.25.y_ref), channel_id=1, source_target_pairs={{0,8},{8,0},{16,24},{24,16},{32,40},{40,32},{48,56},{56,48},{64,72... | collective-permute-start | bytes 24584 | tf_op jit(solution)/shard_map/ppermute | solution.py:286
  40.9 1.9 %collective-permute-start.5 = (f32[16,128]{1,0:T(8,128)S(1)}, f32[16,128]{1,0:T(8,128)S(1)}, u32[]{:S(2)}, u32[]{:S(2)}) collective-permute-start(f32[16,128]{1,0:T(8,128)S(1)} %get-tuple-element.25.y_ref), channel_id=1, source_target_pairs={{0,1},{1,0},{2,3},{3,2},{4,5},{5,4},{6,7},{7,6},{8,9},{9,8},{10,11... | collective-permute-start | bytes 24584 | tf_op jit(solution)/shard_map/ppermute | solution.py:288
  42.9 0.4 shard_map.95
  43.3 0.4 shard_map.96.part_ref
  43.8 0.2 collective-permute-done.5.es_ref
  44.0 0.3 shard_map.97.y_ref
  44.3 6.1 %collective-permute-start.10 = (f32[16,128]{1,0:T(8,128)S(1)}, f32[16,128]{1,0:T(8,128)S(1)}, u32[]{:S(2)}, u32[]{:S(2)}) collective-permute-start(f32[16,128]{1,0:T(8,128)S(1)} %shard_map.97.y_ref), channel_id=1, source_target_pairs={{8,16},{16,8},{24,32},{32,24},{40,48},{48,40},{56,64},{64,56},{72,... | collective-permute-start | bytes 24584 | tf_op jit(solution)/shard_map/ppermute | solution.py:285
  50.5 4.1 %collective-permute-start.11 = (f32[16,128]{1,0:T(8,128)S(1)}, f32[16,128]{1,0:T(8,128)S(1)}, u32[]{:S(2)}, u32[]{:S(2)}) collective-permute-start(f32[16,128]{1,0:T(8,128)S(1)} %shard_map.97.y_ref), channel_id=1, source_target_pairs={{1,2},{2,1},{3,4},{4,3},{5,6},{6,5},{7,0},{0,7},{9,10},{10,9},{11,... | collective-permute-start | bytes 24584 | tf_op jit(solution)/shard_map/ppermute | solution.py:287
  54.6 1.9 %collective-permute-start.8 = (f32[16,128]{1,0:T(8,128)S(1)}, f32[16,128]{1,0:T(8,128)S(1)}, u32[]{:S(2)}, u32[]{:S(2)}) collective-permute-start(f32[16,128]{1,0:T(8,128)S(1)} %shard_map.97.y_ref), channel_id=1, source_target_pairs={{0,8},{8,0},{16,24},{24,16},{32,40},{40,32},{48,56},{56,48},{64,72... | collective-permute-start | bytes 24584 | tf_op jit(solution)/shard_map/ppermute | solution.py:286
  56.6 1.9 %collective-permute-start.9 = (f32[16,128]{1,0:T(8,128)S(1)}, f32[16,128]{1,0:T(8,128)S(1)}, u32[]{:S(2)}, u32[]{:S(2)}) collective-permute-start(f32[16,128]{1,0:T(8,128)S(1)} %shard_map.97.y_ref), channel_id=1, source_target_pairs={{0,1},{1,0},{2,3},{3,2},{4,5},{5,4},{6,7},{7,6},{8,9},{9,8},{10,11... | collective-permute-start | bytes 24584 | tf_op jit(solution)/shard_map/ppermute | solution.py:288
  58.5 0.4 shard_map.98.part_ref
  59.0 0.1 collective-permute-done.8.eg_ref
  59.0 0.6 collective-permute-done.9.es_ref
  59.6 0.3 shard_map.99.y_ref
  60.0 3.4 %collective-permute-start.14 = (f32[16,128]{1,0:T(8,128)S(1)}, f32[16,128]{1,0:T(8,128)S(1)}, u32[]{:S(2)}, u32[]{:S(2)}) collective-permute-start(f32[16,128]{1,0:T(8,128)S(1)} %shard_map.99.y_ref), channel_id=1, source_target_pairs={{8,16},{16,8},{24,32},{32,24},{40,48},{48,40},{56,64},{64,56},{72,... | collective-permute-start | bytes 24584 | tf_op jit(solution)/shard_map/ppermute | solution.py:285
  63.3 4.2 %collective-permute-start.15 = (f32[16,128]{1,0:T(8,128)S(1)}, f32[16,128]{1,0:T(8,128)S(1)}, u32[]{:S(2)}, u32[]{:S(2)}) collective-permute-start(f32[16,128]{1,0:T(8,128)S(1)} %shard_map.99.y_ref), channel_id=1, source_target_pairs={{1,2},{2,1},{3,4},{4,3},{5,6},{6,5},{7,0},{0,7},{9,10},{10,9},{11,... | collective-permute-start | bytes 24584 | tf_op jit(solution)/shard_map/ppermute | solution.py:287
  67.5 1.9 %collective-permute-start.12 = (f32[16,128]{1,0:T(8,128)S(1)}, f32[16,128]{1,0:T(8,128)S(1)}, u32[]{:S(2)}, u32[]{:S(2)}) collective-permute-start(f32[16,128]{1,0:T(8,128)S(1)} %shard_map.99.y_ref), channel_id=1, source_target_pairs={{0,8},{8,0},{16,24},{24,16},{32,40},{40,32},{48,56},{56,48},{64,72... | collective-permute-start | bytes 24584 | tf_op jit(solution)/shard_map/ppermute | solution.py:286
  69.4 2.1 %collective-permute-start.13 = (f32[16,128]{1,0:T(8,128)S(1)}, f32[16,128]{1,0:T(8,128)S(1)}, u32[]{:S(2)}, u32[]{:S(2)}) collective-permute-start(f32[16,128]{1,0:T(8,128)S(1)} %shard_map.99.y_ref), channel_id=1, source_target_pairs={{0,1},{1,0},{2,3},{3,2},{4,5},{5,4},{6,7},{7,6},{8,9},{9,8},{10,11... | collective-permute-start | bytes 24584 | tf_op jit(solution)/shard_map/ppermute | solution.py:288
  71.6 0.4 shard_map.100.part_ref
  72.1 0.4 collective-permute-done.13.es_ref
  72.5 0.3 shard_map.101.y_ref
  72.8 6.1 %collective-permute-start.18 = (f32[16,128]{1,0:T(8,128)S(1)}, f32[16,128]{1,0:T(8,128)S(1)}, u32[]{:S(2)}, u32[]{:S(2)}) collective-permute-start(f32[16,128]{1,0:T(8,128)S(1)} %shard_map.101.y_ref), channel_id=1, source_target_pairs={{8,16},{16,8},{24,32},{32,24},{40,48},{48,40},{56,64},{64,56},{72,... | collective-permute-start | bytes 24584 | tf_op jit(solution)/shard_map/ppermute | solution.py:285
  79.0 4.2 %collective-permute-start.19 = (f32[16,128]{1,0:T(8,128)S(1)}, f32[16,128]{1,0:T(8,128)S(1)}, u32[]{:S(2)}, u32[]{:S(2)}) collective-permute-start(f32[16,128]{1,0:T(8,128)S(1)} %shard_map.101.y_ref), channel_id=1, source_target_pairs={{1,2},{2,1},{3,4},{4,3},{5,6},{6,5},{7,0},{0,7},{9,10},{10,9},{11,... | collective-permute-start | bytes 24584 | tf_op jit(solution)/shard_map/ppermute | solution.py:287
  83.2 1.9 %collective-permute-start.16 = (f32[16,128]{1,0:T(8,128)S(1)}, f32[16,128]{1,0:T(8,128)S(1)}, u32[]{:S(2)}, u32[]{:S(2)}) collective-permute-start(f32[16,128]{1,0:T(8,128)S(1)} %shard_map.101.y_ref), channel_id=1, source_target_pairs={{0,8},{8,0},{16,24},{24,16},{32,40},{40,32},{48,56},{56,48},{64,72... | collective-permute-start | bytes 24584 | tf_op jit(solution)/shard_map/ppermute | solution.py:286
  85.1 1.9 %collective-permute-start.17 = (f32[16,128]{1,0:T(8,128)S(1)}, f32[16,128]{1,0:T(8,128)S(1)}, u32[]{:S(2)}, u32[]{:S(2)}) collective-permute-start(f32[16,128]{1,0:T(8,128)S(1)} %shard_map.101.y_ref), channel_id=1, source_target_pairs={{0,1},{1,0},{2,3},{3,2},{4,5},{5,4},{6,7},{7,6},{8,9},{9,8},{10,11... | collective-permute-start | bytes 24584 | tf_op jit(solution)/shard_map/ppermute | solution.py:288
  87.1 0.3 shard_map.102
  87.4 0.2 collective-permute-done.16.eg_ref
  87.6 0.6 collective-permute-done.17.es_ref
  88.2 0.8 shard_map.103
  (24 shorter events, 0.1 us)
Async XLA Ops:
  0.0 29.4 %copy-start.8 = (bf16[4,14,512]{2,0,1:T(4,128)(2,1)S(1)}, bf16[4,14,512]{2,0,1:T(4,128)(2,1)}, u32[]{:S(2)}) copy-start(bf16[4,14,512]{2,0,1:T(4,128)(2,1)} %param.15) | copy-start | bytes 172036
  1.7 28.7 %collective-permute-start = (f32[5,8,128]{2,1,0:T(8,128)S(1)}, f32[5,8,128]{2,1,0:T(8,128)S(1)}, u32[]{:S(2)}, u32[]{:S(2)}) collective-permute-start(f32[5,8,128]{2,1,0:T(8,128)S(1)} %get-tuple-element.19), channel_id=1, source_target_pairs={{8,16},{16,8},{24,32},{32,24},{40,48},{48,40},{56,64},{64,56},{72,... | collective-permute-start | bytes 61448 | tf_op jit(solution)/shard_map/ppermute | solution.py:285
  20.0 10.4 %collective-permute-start.1 = (f32[5,8,128]{2,1,0:T(8,128)S(1)}, f32[5,8,128]{2,1,0:T(8,128)S(1)}, u32[]{:S(2)}, u32[]{:S(2)}) collective-permute-start(f32[5,8,128]{2,1,0:T(8,128)S(1)} %get-tuple-element.20), channel_id=1, source_target_pairs={{0,8},{8,0},{16,24},{24,16},{32,40},{40,32},{48,56},{56,48},{64,72... | collective-permute-start | bytes 61448 | tf_op jit(solution)/shard_map/ppermute | solution.py:286
  21.9 8.5 %collective-permute-start.2 = (f32[5,8,128]{2,1,0:T(8,128)S(1)}, f32[5,8,128]{2,1,0:T(8,128)S(1)}, u32[]{:S(2)}, u32[]{:S(2)}) collective-permute-start(f32[5,8,128]{2,1,0:T(8,128)S(1)} %get-tuple-element.21), channel_id=1, source_target_pairs={{1,2},{2,1},{3,4},{4,3},{5,6},{6,5},{7,0},{0,7},{9,10},{10,9},{11,... | collective-permute-start | bytes 61448 | tf_op jit(solution)/shard_map/ppermute | solution.py:287
  27.0 2.5 %copy-start = (f32[3,3072]{1,0:T(4,128)S(1)}, f32[3,3072]{1,0:T(4,128)}, u32[]{:S(2)}) copy-start(f32[3,3072]{1,0:T(4,128)} %tan_ref.3) | copy-start | bytes 110596
  27.0 2.5 %copy-start.1 = (s32[3072]{0:T(1024)S(1)}, s32[3072]{0:T(1024)}, u32[]{:S(2)}) copy-start(s32[3072]{0:T(1024)} %param.13) | copy-start | bytes 36868
  27.0 2.4 %copy-start.2 = (f32[3072]{0:T(1024)S(1)}, f32[3072]{0:T(1024)}, u32[]{:S(2)}) copy-start(f32[3072]{0:T(1024)} %param.9) | copy-start | bytes 36868
  27.0 2.4 %copy-start.3 = (s32[3072]{0:T(1024)S(1)}, s32[3072]{0:T(1024)}, u32[]{:S(2)}) copy-start(s32[3072]{0:T(1024)} %param.12) | copy-start | bytes 36868
  27.0 3.4 %collective-permute-start.3 = (f32[5,8,128]{2,1,0:T(8,128)S(1)}, f32[5,8,128]{2,1,0:T(8,128)S(1)}, u32[]{:S(2)}, u32[]{:S(2)}) collective-permute-start(f32[5,8,128]{2,1,0:T(8,128)S(1)} %get-tuple-element.22), channel_id=1, source_target_pairs={{0,1},{1,0},{2,3},{3,2},{4,5},{5,4},{6,7},{7,6},{8,9},{9,8},{10,11... | collective-permute-start | bytes 61448 | tf_op jit(solution)/shard_map/ppermute | solution.py:288
  29.5 0.7 copy-start.4
  29.5 0.8 copy-start.5
  29.5 0.8 copy-start.7
  30.7 12.6 %collective-permute-start.6 = (f32[16,128]{1,0:T(8,128)S(1)}, f32[16,128]{1,0:T(8,128)S(1)}, u32[]{:S(2)}, u32[]{:S(2)}) collective-permute-start(f32[16,128]{1,0:T(8,128)S(1)} %get-tuple-element.25.y_ref), channel_id=1, source_target_pairs={{8,16},{16,8},{24,32},{32,24},{40,48},{48,40},{56,64},{64,56},{72,... | collective-permute-start | bytes 24584 | tf_op jit(solution)/shard_map/ppermute | solution.py:285
  33.3 10.0 %collective-permute-start.7 = (f32[16,128]{1,0:T(8,128)S(1)}, f32[16,128]{1,0:T(8,128)S(1)}, u32[]{:S(2)}, u32[]{:S(2)}) collective-permute-start(f32[16,128]{1,0:T(8,128)S(1)} %get-tuple-element.25.y_ref), channel_id=1, source_target_pairs={{1,2},{2,1},{3,4},{4,3},{5,6},{6,5},{7,0},{0,7},{9,10},{10,9},{11,... | collective-permute-start | bytes 24584 | tf_op jit(solution)/shard_map/ppermute | solution.py:287
  38.4 5.4 %collective-permute-start.4 = (f32[16,128]{1,0:T(8,128)S(1)}, f32[16,128]{1,0:T(8,128)S(1)}, u32[]{:S(2)}, u32[]{:S(2)}) collective-permute-start(f32[16,128]{1,0:T(8,128)S(1)} %get-tuple-element.25.y_ref), channel_id=1, source_target_pairs={{0,8},{8,0},{16,24},{24,16},{32,40},{40,32},{48,56},{56,48},{64,72... | collective-permute-start | bytes 24584 | tf_op jit(solution)/shard_map/ppermute | solution.py:286
  40.9 3.1 %collective-permute-start.5 = (f32[16,128]{1,0:T(8,128)S(1)}, f32[16,128]{1,0:T(8,128)S(1)}, u32[]{:S(2)}, u32[]{:S(2)}) collective-permute-start(f32[16,128]{1,0:T(8,128)S(1)} %get-tuple-element.25.y_ref), channel_id=1, source_target_pairs={{0,1},{1,0},{2,3},{3,2},{4,5},{5,4},{6,7},{7,6},{8,9},{9,8},{10,11... | collective-permute-start | bytes 24584 | tf_op jit(solution)/shard_map/ppermute | solution.py:288
  44.3 14.2 %collective-permute-start.10 = (f32[16,128]{1,0:T(8,128)S(1)}, f32[16,128]{1,0:T(8,128)S(1)}, u32[]{:S(2)}, u32[]{:S(2)}) collective-permute-start(f32[16,128]{1,0:T(8,128)S(1)} %shard_map.97.y_ref), channel_id=1, source_target_pairs={{8,16},{16,8},{24,32},{32,24},{40,48},{48,40},{56,64},{64,56},{72,... | collective-permute-start | bytes 24584 | tf_op jit(solution)/shard_map/ppermute | solution.py:285
  50.5 8.0 %collective-permute-start.11 = (f32[16,128]{1,0:T(8,128)S(1)}, f32[16,128]{1,0:T(8,128)S(1)}, u32[]{:S(2)}, u32[]{:S(2)}) collective-permute-start(f32[16,128]{1,0:T(8,128)S(1)} %shard_map.97.y_ref), channel_id=1, source_target_pairs={{1,2},{2,1},{3,4},{4,3},{5,6},{6,5},{7,0},{0,7},{9,10},{10,9},{11,... | collective-permute-start | bytes 24584 | tf_op jit(solution)/shard_map/ppermute | solution.py:287
  54.6 4.4 %collective-permute-start.8 = (f32[16,128]{1,0:T(8,128)S(1)}, f32[16,128]{1,0:T(8,128)S(1)}, u32[]{:S(2)}, u32[]{:S(2)}) collective-permute-start(f32[16,128]{1,0:T(8,128)S(1)} %shard_map.97.y_ref), channel_id=1, source_target_pairs={{0,8},{8,0},{16,24},{24,16},{32,40},{40,32},{48,56},{56,48},{64,72... | collective-permute-start | bytes 24584 | tf_op jit(solution)/shard_map/ppermute | solution.py:286
  56.6 3.1 %collective-permute-start.9 = (f32[16,128]{1,0:T(8,128)S(1)}, f32[16,128]{1,0:T(8,128)S(1)}, u32[]{:S(2)}, u32[]{:S(2)}) collective-permute-start(f32[16,128]{1,0:T(8,128)S(1)} %shard_map.97.y_ref), channel_id=1, source_target_pairs={{0,1},{1,0},{2,3},{3,2},{4,5},{5,4},{6,7},{7,6},{8,9},{9,8},{10,11... | collective-permute-start | bytes 24584 | tf_op jit(solution)/shard_map/ppermute | solution.py:288
  60.0 11.6 %collective-permute-start.14 = (f32[16,128]{1,0:T(8,128)S(1)}, f32[16,128]{1,0:T(8,128)S(1)}, u32[]{:S(2)}, u32[]{:S(2)}) collective-permute-start(f32[16,128]{1,0:T(8,128)S(1)} %shard_map.99.y_ref), channel_id=1, source_target_pairs={{8,16},{16,8},{24,32},{32,24},{40,48},{48,40},{56,64},{64,56},{72,... | collective-permute-start | bytes 24584 | tf_op jit(solution)/shard_map/ppermute | solution.py:285
  63.3 8.3 %collective-permute-start.15 = (f32[16,128]{1,0:T(8,128)S(1)}, f32[16,128]{1,0:T(8,128)S(1)}, u32[]{:S(2)}, u32[]{:S(2)}) collective-permute-start(f32[16,128]{1,0:T(8,128)S(1)} %shard_map.99.y_ref), channel_id=1, source_target_pairs={{1,2},{2,1},{3,4},{4,3},{5,6},{6,5},{7,0},{0,7},{9,10},{10,9},{11,... | collective-permute-start | bytes 24584 | tf_op jit(solution)/shard_map/ppermute | solution.py:287
  67.5 4.5 %collective-permute-start.12 = (f32[16,128]{1,0:T(8,128)S(1)}, f32[16,128]{1,0:T(8,128)S(1)}, u32[]{:S(2)}, u32[]{:S(2)}) collective-permute-start(f32[16,128]{1,0:T(8,128)S(1)} %shard_map.99.y_ref), channel_id=1, source_target_pairs={{0,8},{8,0},{16,24},{24,16},{32,40},{40,32},{48,56},{56,48},{64,72... | collective-permute-start | bytes 24584 | tf_op jit(solution)/shard_map/ppermute | solution.py:286
  69.4 3.1 %collective-permute-start.13 = (f32[16,128]{1,0:T(8,128)S(1)}, f32[16,128]{1,0:T(8,128)S(1)}, u32[]{:S(2)}, u32[]{:S(2)}) collective-permute-start(f32[16,128]{1,0:T(8,128)S(1)} %shard_map.99.y_ref), channel_id=1, source_target_pairs={{0,1},{1,0},{2,3},{3,2},{4,5},{5,4},{6,7},{7,6},{8,9},{9,8},{10,11... | collective-permute-start | bytes 24584 | tf_op jit(solution)/shard_map/ppermute | solution.py:288
  72.5 14.6 %copy-start.6 = (f32[3072]{0:T(1024)S(1)}, f32[3072]{0:T(1024)}, u32[]{:S(2)}) copy-start(f32[3072]{0:T(1024)} %param.10) | copy-start | bytes 36868
  72.8 14.2 %collective-permute-start.18 = (f32[16,128]{1,0:T(8,128)S(1)}, f32[16,128]{1,0:T(8,128)S(1)}, u32[]{:S(2)}, u32[]{:S(2)}) collective-permute-start(f32[16,128]{1,0:T(8,128)S(1)} %shard_map.101.y_ref), channel_id=1, source_target_pairs={{8,16},{16,8},{24,32},{32,24},{40,48},{48,40},{56,64},{64,56},{72,... | collective-permute-start | bytes 24584 | tf_op jit(solution)/shard_map/ppermute | solution.py:285
  79.0 8.1 %collective-permute-start.19 = (f32[16,128]{1,0:T(8,128)S(1)}, f32[16,128]{1,0:T(8,128)S(1)}, u32[]{:S(2)}, u32[]{:S(2)}) collective-permute-start(f32[16,128]{1,0:T(8,128)S(1)} %shard_map.101.y_ref), channel_id=1, source_target_pairs={{1,2},{2,1},{3,4},{4,3},{5,6},{6,5},{7,0},{0,7},{9,10},{10,9},{11,... | collective-permute-start | bytes 24584 | tf_op jit(solution)/shard_map/ppermute | solution.py:287
  83.2 4.4 %collective-permute-start.16 = (f32[16,128]{1,0:T(8,128)S(1)}, f32[16,128]{1,0:T(8,128)S(1)}, u32[]{:S(2)}, u32[]{:S(2)}) collective-permute-start(f32[16,128]{1,0:T(8,128)S(1)} %shard_map.101.y_ref), channel_id=1, source_target_pairs={{0,8},{8,0},{16,24},{24,16},{32,40},{40,32},{48,56},{56,48},{64,72... | collective-permute-start | bytes 24584 | tf_op jit(solution)/shard_map/ppermute | solution.py:286
  85.1 3.1 %collective-permute-start.17 = (f32[16,128]{1,0:T(8,128)S(1)}, f32[16,128]{1,0:T(8,128)S(1)}, u32[]{:S(2)}, u32[]{:S(2)}) collective-permute-start(f32[16,128]{1,0:T(8,128)S(1)} %shard_map.101.y_ref), channel_id=1, source_target_pairs={{0,1},{1,0},{2,3},{3,2},{4,5},{5,4},{6,7},{7,6},{8,9},{9,8},{10,11... | collective-permute-start | bytes 24584 | tf_op jit(solution)/shard_map/ppermute | solution.py:288

commit v5 on v4

--- a/solution.py
+++ b/solution.py
@@ -7,6 +7,7 @@
 
 
 SWEEPS = 4
+EARLY_ROW = 12
 LANES = 128
 F32 = jnp.float32
 BF16 = jnp.bfloat16
@@ -160,14 +161,14 @@
                 send16_ref[at : at + 1, :] = send_ref[a, b : b + 1, LANES * q : LANES * q + LANES]
 
 
-def first_solve(own_ref, og, eg, os, es, send_ref, dinv_ref, rn_ref, y_ref):
+def first_solve(own_ref, og, eg, os_early, os_late, es, send_ref, dinv_ref, rn_ref, y_ref):
     index = send_ref[...]
     row, lane = rows_of(index)
     lefts, rights = [], []
     values = []
     for c in range(4):
         before, after = sides(odd("grp"), og[c], eg[c])
-        prev, nxt = sides(odd("sub"), os[c], es[c])
+        prev, nxt = sides(odd("sub"), os_early[c] + os_late[c], es[c])
         low = before + jnp.concatenate([prev[0:4], nxt[0:4]], axis=0)
         high = after + jnp.concatenate([prev[4:8], nxt[4:8]], axis=0)
         values.append([split3(low), split3(high)])
@@ -190,11 +191,12 @@
     return odd(axis) != matching
 
 
-def compose(og_ref, eg_ref, os_ref, es_ref, idx_ref, head_ref, idx_out, head_out):
+def compose(og_ref, eg_ref, os_early_ref, os_late_ref, es_ref, idx_ref, head_ref, idx_out, head_out):
     blocks = []
-    for axis, matching, ref, number in (("grp", 1, og_ref, 0), ("grp", 0, eg_ref, 0), ("sub", 1, os_ref, 2), ("sub", 0, es_ref, 2)):
+    received = [og_ref[4], eg_ref[4], os_early_ref[4] + os_late_ref[4], es_ref[4]]
+    for values, (axis, matching, number) in zip(received, (("grp", 1, 0), ("grp", 0, 0), ("sub", 1, 2), ("sub", 0, 2))):
         number = jnp.where(from_lower(axis, matching), number, number + 1)
-        values = ref[4].astype(jnp.int32) + 4 * LANES * (number + 1)
+        values = values.astype(jnp.int32) + 4 * LANES * (number + 1)
         blocks.append((4 + 8 * number, values.astype(F32)))
     for src, dst in ((idx_ref, idx_out), (head_ref, head_out)):
         for v, index in enumerate(vectors(src)):
@@ -277,6 +279,23 @@
         part = slice(8 * v, 8 * v + 8)
         mixed = sum(tan24_ref[c, part, :] * heads[v][c + 1] for c in range(3))
         out_ref[part, :] = part_ref[part, :] + heads[v][0] + 0.5 * mixed
+
+
+def row_pairs(rows, size, offset):
+    return [(size * row + a, size * row + b) for row in rows for a, b in pairs(size, offset)]
+
+
+def first_exchange(blocks):
+    og, eg, os, es = blocks
+    grp, sub = lax.axis_size("grp"), lax.axis_size("sub")
+    early = range(0, grp, EARLY_ROW)
+    others = [row for row in range(grp) if row not in early]
+    os_early = lax.ppermute(os, ("grp", "sub"), row_pairs(early, sub, 1))
+    og = lax.ppermute(og, "grp", pairs(grp, 1))
+    os_late = lax.ppermute(os, ("grp", "sub"), row_pairs(others, sub, 1))
+    eg = lax.ppermute(eg, "grp", pairs(grp, 0))
+    es = lax.ppermute(es, "sub", pairs(sub, 0))
+    return og, eg, os_early, os_late, es
 
 
 def exchange(blocks):
@@ -318,7 +337,7 @@
     )
     count = stencil_index.shape[0]
     lines = count * nodes // LANES
-    ghost = exchange(ghost)
+    ghost = first_exchange(ghost)
     idx56, coef56, dinv, send16 = call(
         prepare,
         [((lines, LANES), jnp.int32), ((4, lines, LANES), F32), own, ((16, LANES), jnp.int32)],

time: 89.8 us -> 92 us (1.024)
  starting transfers between devices: 79.7 us -> 80.9 us
  waiting for transfers between devices: 2.15 us -> 3.16 us
    ppermute x0 -> x5, starting transfers between devices: none -> 28.6 us  [the longest x1 17.5 us: first_exchange(): og = lax.ppermute(og, 'grp', pairs(grp, 1))]
    ppermute x5 -> x4, starting transfers between devices: 36.5 us -> 18.6 us  [exchange(): og = lax.ppermute(og, 'grp', pairs(grp, 1))]
    ppermute x5 -> x4, starting transfers between devices: 22.6 us -> 15.5 us  [exchange(): os = lax.ppermute(os, 'sub', pairs(sub, 1))]
    ppermute x5 -> x4, starting transfers between devices: 10.2 us -> 8.32 us  [exchange(): eg = lax.ppermute(eg, 'grp', pairs(grp, 0))]
    ppermute x5 -> x4, waiting for transfers between devices: 0.28 us -> 2.06 us  [exchange(): eg = lax.ppermute(eg, 'grp', pairs(grp, 0))]
    ppermute x5 -> x4, waiting for transfers between devices: 1.85 us -> 1.06 us  [exchange(): es = lax.ppermute(es, 'sub', pairs(sub, 0))]
    ppermute x5 -> x4, starting transfers between devices: 10.3 us -> 9.72 us  [exchange(): es = lax.ppermute(es, 'sub', pairs(sub, 0))]
  transfers between devices with their start and end apart: 20 -> 21, of which waited for: 6 -> 4; matrix products, arithmetic and copies ran while one was open for 0% -> 0% of each run, Pallas kernels for 3% -> 3%
where the time goes in v5:
time: 92 us; the launch traced here: 91.2 us
  starting transfers between devices  80.9 us (88%)
  Pallas kernels  6.61 us (7%)
  waiting for transfers between devices  3.16 us (3%)
    ppermute x4, starting transfers between devices, exchange(): og = lax.ppermute(og, 'grp', pairs(grp, 1))  18.6 us
    ppermute x1, starting transfers between devices, first_exchange(): og = lax.ppermute(og, 'grp', pairs(grp, 1))  17.5 us
    ppermute x4, starting transfers between devices, exchange(): os = lax.ppermute(os, 'sub', pairs(sub, 1))  15.5 us
    ppermute x4, starting transfers between devices, exchange(): es = lax.ppermute(es, 'sub', pairs(sub, 0))  9.72 us
    ppermute x4, starting transfers between devices, exchange(): eg = lax.ppermute(eg, 'grp', pairs(grp, 0))  8.32 us
    pallas_call x13, Pallas kernels, call(): pl.pallas_call(kernel, out_shape=[jax.ShapeDtypeStruct(shape, dtype) for...  6.61 us
    ppermute x1, starting transfers between devices, first_exchange(): os_early = lax.ppermute(os, ('grp', 'sub'), row_pairs(early, sub, 1))  5.6 us
    ppermute x1, starting transfers between devices, first_exchange(): es = lax.ppermute(es, 'sub', pairs(sub, 0))  2.92 us
  transfers between devices with their start and end apart: 21, of which 4 were waited for; matrix products, arithmetic and copies ran while one was open for 0% of the time, Pallas kernels for 3%

profile of v5, /device:TPU:1, one launch (start us, length us, event | category | flops | bytes accessed | tf_op | source)
XLA Modules:
  0.0 91.2 jit_solution(18298803388218772904)
XLA Ops:
  0.0 1.7 %shard_map.92 = (f32[5,8,128]{2,1,0:T(8,128)S(1)}, f32[5,8,128]{2,1,0:T(8,128)S(1)}, f32[5,8,128]{2,1,0:T(8,128)S(1)}, f32[5,8,128]{2,1,0:T(8,128)S(1)}) custom-call(f32[1,3072]{1,0:T(1,128)} %bitcast.11, f32[3,3072]{1,0:T(4,128)} %tan_ref.3, s32[1,3072]{1,0:T(1,128)} %bitcast.8, s32[2,2,512]{2,1,0:T(2,128)} %send_ref.1), custom_call_target="tpu_custom_call" | custom-call | tf_op jit(solution)/shard_map/pallas_call | solution.py:19
  1.7 5.6 %collective-permute-start.2 = (f32[5,8,128]{2,1,0:T(8,128)S(1)}, f32[5,8,128]{2,1,0:T(8,128)S(1)}, u32[]{:S(2)}, u32[]{:S(2)}) collective-permute-start(f32[5,8,128]{2,1,0:T(8,128)S(1)} %get-tuple-element.21), channel_id=1, source_target_pairs={{1,2},{2,1},{3,4},{4,3},{5,6},{6,5},{7,0},{0,7},{97,98},{98,97},{9... | collective-permute-start | bytes 61448 | tf_op jit(solution)/shard_map/ppermute | solution.py:293
  7.3 0.7 collective-permute-start.3
  7.9 17.5 %collective-permute-start = (f32[5,8,128]{2,1,0:T(8,128)S(1)}, f32[5,8,128]{2,1,0:T(8,128)S(1)}, u32[]{:S(2)}, u32[]{:S(2)}) collective-permute-start(f32[5,8,128]{2,1,0:T(8,128)S(1)} %get-tuple-element.19), channel_id=1, source_target_pairs={{8,16},{16,8},{24,32},{32,24},{40,48},{48,40},{56,64},{64,56},{72,... | collective-permute-start | bytes 61448 | tf_op jit(solution)/shard_map/ppermute | solution.py:294
  25.5 1.9 %collective-permute-start.1 = (f32[5,8,128]{2,1,0:T(8,128)S(1)}, f32[5,8,128]{2,1,0:T(8,128)S(1)}, u32[]{:S(2)}, u32[]{:S(2)}) collective-permute-start(f32[5,8,128]{2,1,0:T(8,128)S(1)} %get-tuple-element.20), channel_id=1, source_target_pairs={{0,8},{8,0},{16,24},{24,16},{32,40},{40,32},{48,56},{56,48},{64,72... | collective-permute-start | bytes 61448 | tf_op jit(solution)/shard_map/ppermute | solution.py:296
  27.4 0.0 copy-start
  27.4 0.0 copy-start.1
  27.4 0.0 copy-start.2
  27.4 0.0 copy-start.3
  27.4 2.9 %collective-permute-start.4 = (f32[5,8,128]{2,1,0:T(8,128)S(1)}, f32[5,8,128]{2,1,0:T(8,128)S(1)}, u32[]{:S(2)}, u32[]{:S(2)}) collective-permute-start(f32[5,8,128]{2,1,0:T(8,128)S(1)} %get-tuple-element.22), channel_id=1, source_target_pairs={{0,1},{1,0},{2,3},{3,2},{4,5},{5,4},{6,7},{7,6},{8,9},{9,8},{10,11... | collective-permute-start | bytes 61448 | tf_op jit(solution)/shard_map/ppermute | solution.py:297
  30.4 0.0 copy-start.4
  30.5 0.0 copy-start.5
  30.5 0.0 copy-start.7
  30.5 0.7 shard_map.91.own_ref
  31.2 0.0 copy-done.4
  31.2 0.0 copy-done.5
  31.2 0.1 shard_map.93
  31.4 0.0 collective-permute-done.2.os_early.os_early_ref
  31.4 0.3 shard_map.94
  31.7 2.8 %collective-permute-start.7 = (f32[16,128]{1,0:T(8,128)S(1)}, f32[16,128]{1,0:T(8,128)S(1)}, u32[]{:S(2)}, u32[]{:S(2)}) collective-permute-start(f32[16,128]{1,0:T(8,128)S(1)} %get-tuple-element.25.y_ref), channel_id=1, source_target_pairs={{8,16},{16,8},{24,32},{32,24},{40,48},{48,40},{56,64},{64,56},{72,... | collective-permute-start | bytes 24584 | tf_op jit(solution)/shard_map/ppermute | solution.py:304
  34.5 4.0 %collective-permute-start.8 = (f32[16,128]{1,0:T(8,128)S(1)}, f32[16,128]{1,0:T(8,128)S(1)}, u32[]{:S(2)}, u32[]{:S(2)}) collective-permute-start(f32[16,128]{1,0:T(8,128)S(1)} %get-tuple-element.25.y_ref), channel_id=1, source_target_pairs={{1,2},{2,1},{3,4},{4,3},{5,6},{6,5},{7,0},{0,7},{9,10},{10,9},{11,... | collective-permute-start | bytes 24584 | tf_op jit(solution)/shard_map/ppermute | solution.py:306
  38.5 2.6 %collective-permute-start.5 = (f32[16,128]{1,0:T(8,128)S(1)}, f32[16,128]{1,0:T(8,128)S(1)}, u32[]{:S(2)}, u32[]{:S(2)}) collective-permute-start(f32[16,128]{1,0:T(8,128)S(1)} %get-tuple-element.25.y_ref), channel_id=1, source_target_pairs={{0,8},{8,0},{16,24},{24,16},{32,40},{40,32},{48,56},{56,48},{64,72... | collective-permute-start | bytes 24584 | tf_op jit(solution)/shard_map/ppermute | solution.py:305
  41.1 2.6 %collective-permute-start.6 = (f32[16,128]{1,0:T(8,128)S(1)}, f32[16,128]{1,0:T(8,128)S(1)}, u32[]{:S(2)}, u32[]{:S(2)}) collective-permute-start(f32[16,128]{1,0:T(8,128)S(1)} %get-tuple-element.25.y_ref), channel_id=1, source_target_pairs={{0,1},{1,0},{2,3},{3,2},{4,5},{5,4},{6,7},{7,6},{8,9},{9,8},{10,11... | collective-permute-start | bytes 24584 | tf_op jit(solution)/shard_map/ppermute | solution.py:307
  43.7 0.4 shard_map.95
  44.1 0.4 shard_map.96.part_ref
  44.6 0.3 shard_map.97.y_ref
  44.9 6.0 %collective-permute-start.11 = (f32[16,128]{1,0:T(8,128)S(1)}, f32[16,128]{1,0:T(8,128)S(1)}, u32[]{:S(2)}, u32[]{:S(2)}) collective-permute-start(f32[16,128]{1,0:T(8,128)S(1)} %shard_map.97.y_ref), channel_id=1, source_target_pairs={{8,16},{16,8},{24,32},{32,24},{40,48},{48,40},{56,64},{64,56},{72,... | collective-permute-start | bytes 24584 | tf_op jit(solution)/shard_map/ppermute | solution.py:304
  50.9 3.5 %collective-permute-start.12 = (f32[16,128]{1,0:T(8,128)S(1)}, f32[16,128]{1,0:T(8,128)S(1)}, u32[]{:S(2)}, u32[]{:S(2)}) collective-permute-start(f32[16,128]{1,0:T(8,128)S(1)} %shard_map.97.y_ref), channel_id=1, source_target_pairs={{1,2},{2,1},{3,4},{4,3},{5,6},{6,5},{7,0},{0,7},{9,10},{10,9},{11,... | collective-permute-start | bytes 24584 | tf_op jit(solution)/shard_map/ppermute | solution.py:306
  54.4 2.6 %collective-permute-start.10 = (f32[16,128]{1,0:T(8,128)S(1)}, f32[16,128]{1,0:T(8,128)S(1)}, u32[]{:S(2)}, u32[]{:S(2)}) collective-permute-start(f32[16,128]{1,0:T(8,128)S(1)} %shard_map.97.y_ref), channel_id=1, source_target_pairs={{0,1},{1,0},{2,3},{3,2},{4,5},{5,4},{6,7},{7,6},{8,9},{9,8},{10,11... | collective-permute-start | bytes 24584 | tf_op jit(solution)/shard_map/ppermute | solution.py:307
  57.1 1.9 %collective-permute-start.9 = (f32[16,128]{1,0:T(8,128)S(1)}, f32[16,128]{1,0:T(8,128)S(1)}, u32[]{:S(2)}, u32[]{:S(2)}) collective-permute-start(f32[16,128]{1,0:T(8,128)S(1)} %shard_map.97.y_ref), channel_id=1, source_target_pairs={{0,8},{8,0},{16,24},{24,16},{32,40},{40,32},{48,56},{56,48},{64,72... | collective-permute-start | bytes 24584 | tf_op jit(solution)/shard_map/ppermute | solution.py:305
  59.0 0.4 shard_map.98.part_ref
  59.5 2.0 %collective-permute-done.9.eg_ref = f32[16,128]{1,0:T(8,128)S(1)} collective-permute-done((f32[16,128]{1,0:T(8,128)S(1)}, f32[16,128]{1,0:T(8,128)S(1)}, u32[]{:S(2)}, u32[]{:S(2)}) %collective-permute-start.9) | collective-permute-done | bytes 8224 | tf_op jit(solution)/shard_map/ppermute | solution.py:305
  61.5 0.3 shard_map.99.y_ref
  61.8 3.9 %collective-permute-start.15 = (f32[16,128]{1,0:T(8,128)S(1)}, f32[16,128]{1,0:T(8,128)S(1)}, u32[]{:S(2)}, u32[]{:S(2)}) collective-permute-start(f32[16,128]{1,0:T(8,128)S(1)} %shard_map.99.y_ref), channel_id=1, source_target_pairs={{8,16},{16,8},{24,32},{32,24},{40,48},{48,40},{56,64},{64,56},{72,... | collective-permute-start | bytes 24584 | tf_op jit(solution)/shard_map/ppermute | solution.py:304
  65.7 5.2 %collective-permute-start.16 = (f32[16,128]{1,0:T(8,128)S(1)}, f32[16,128]{1,0:T(8,128)S(1)}, u32[]{:S(2)}, u32[]{:S(2)}) collective-permute-start(f32[16,128]{1,0:T(8,128)S(1)} %shard_map.99.y_ref), channel_id=1, source_target_pairs={{1,2},{2,1},{3,4},{4,3},{5,6},{6,5},{7,0},{0,7},{9,10},{10,9},{11,... | collective-permute-start | bytes 24584 | tf_op jit(solution)/shard_map/ppermute | solution.py:306
  70.9 1.9 %collective-permute-start.13 = (f32[16,128]{1,0:T(8,128)S(1)}, f32[16,128]{1,0:T(8,128)S(1)}, u32[]{:S(2)}, u32[]{:S(2)}) collective-permute-start(f32[16,128]{1,0:T(8,128)S(1)} %shard_map.99.y_ref), channel_id=1, source_target_pairs={{0,8},{8,0},{16,24},{24,16},{32,40},{40,32},{48,56},{56,48},{64,72... | collective-permute-start | bytes 24584 | tf_op jit(solution)/shard_map/ppermute | solution.py:305
  72.8 1.9 %collective-permute-start.14 = (f32[16,128]{1,0:T(8,128)S(1)}, f32[16,128]{1,0:T(8,128)S(1)}, u32[]{:S(2)}, u32[]{:S(2)}) collective-permute-start(f32[16,128]{1,0:T(8,128)S(1)} %shard_map.99.y_ref), channel_id=1, source_target_pairs={{0,1},{1,0},{2,3},{3,2},{4,5},{5,4},{6,7},{7,6},{8,9},{9,8},{10,11... | collective-permute-start | bytes 24584 | tf_op jit(solution)/shard_map/ppermute | solution.py:307
  74.8 0.4 shard_map.100.part_ref
  75.2 0.1 collective-permute-done.13.eg_ref
  75.3 0.6 collective-permute-done.14.es_ref
  75.9 0.3 shard_map.101.y_ref
  76.2 5.9 %collective-permute-start.19 = (f32[16,128]{1,0:T(8,128)S(1)}, f32[16,128]{1,0:T(8,128)S(1)}, u32[]{:S(2)}, u32[]{:S(2)}) collective-permute-start(f32[16,128]{1,0:T(8,128)S(1)} %shard_map.101.y_ref), channel_id=1, source_target_pairs={{8,16},{16,8},{24,32},{32,24},{40,48},{48,40},{56,64},{64,56},{72,... | collective-permute-start | bytes 24584 | tf_op jit(solution)/shard_map/ppermute | solution.py:304
  82.2 2.9 %collective-permute-start.20 = (f32[16,128]{1,0:T(8,128)S(1)}, f32[16,128]{1,0:T(8,128)S(1)}, u32[]{:S(2)}, u32[]{:S(2)}) collective-permute-start(f32[16,128]{1,0:T(8,128)S(1)} %shard_map.101.y_ref), channel_id=1, source_target_pairs={{1,2},{2,1},{3,4},{4,3},{5,6},{6,5},{7,0},{0,7},{9,10},{10,9},{11,... | collective-permute-start | bytes 24584 | tf_op jit(solution)/shard_map/ppermute | solution.py:306
  85.1 1.9 %collective-permute-start.17 = (f32[16,128]{1,0:T(8,128)S(1)}, f32[16,128]{1,0:T(8,128)S(1)}, u32[]{:S(2)}, u32[]{:S(2)}) collective-permute-start(f32[16,128]{1,0:T(8,128)S(1)} %shard_map.101.y_ref), channel_id=1, source_target_pairs={{0,8},{8,0},{16,24},{24,16},{32,40},{40,32},{48,56},{56,48},{64,72... | collective-permute-start | bytes 24584 | tf_op jit(solution)/shard_map/ppermute | solution.py:305
  87.0 2.6 %collective-permute-start.18 = (f32[16,128]{1,0:T(8,128)S(1)}, f32[16,128]{1,0:T(8,128)S(1)}, u32[]{:S(2)}, u32[]{:S(2)}) collective-permute-start(f32[16,128]{1,0:T(8,128)S(1)} %shard_map.101.y_ref), channel_id=1, source_target_pairs={{0,1},{1,0},{2,3},{3,2},{4,5},{5,4},{6,7},{7,6},{8,9},{9,8},{10,11... | collective-permute-start | bytes 24584 | tf_op jit(solution)/shard_map/ppermute | solution.py:307
  89.6 0.3 shard_map.102
  90.0 0.5 collective-permute-done.18.es_ref
  90.4 0.8 shard_map.103
  (26 shorter events, 0.1 us)
Async XLA Ops:
  0.0 30.4 %copy-start.8 = (bf16[4,14,512]{2,0,1:T(4,128)(2,1)S(1)}, bf16[4,14,512]{2,0,1:T(4,128)(2,1)}, u32[]{:S(2)}) copy-start(bf16[4,14,512]{2,0,1:T(4,128)(2,1)} %param.15) | copy-start | bytes 172036
  1.7 29.7 %collective-permute-start.2 = (f32[5,8,128]{2,1,0:T(8,128)S(1)}, f32[5,8,128]{2,1,0:T(8,128)S(1)}, u32[]{:S(2)}, u32[]{:S(2)}) collective-permute-start(f32[5,8,128]{2,1,0:T(8,128)S(1)} %get-tuple-element.21), channel_id=1, source_target_pairs={{1,2},{2,1},{3,4},{4,3},{5,6},{6,5},{7,0},{0,7},{97,98},{98,97},{9... | collective-permute-start | bytes 61448 | tf_op jit(solution)/shard_map/ppermute | solution.py:293
  7.3 24.1 %collective-permute-start.3 = (f32[5,8,128]{2,1,0:T(8,128)S(1)}, f32[5,8,128]{2,1,0:T(8,128)S(1)}, u32[]{:S(2)}, u32[]{:S(2)}) collective-permute-start(f32[5,8,128]{2,1,0:T(8,128)S(1)} %get-tuple-element.21), channel_id=1, source_target_pairs={{9,10},{10,9},{11,12},{12,11},{13,14},{14,13},{15,8},{8,15},{17,18... | collective-permute-start | bytes 61448 | tf_op jit(solution)/shard_map/ppermute | solution.py:295
  7.9 23.4 %collective-permute-start = (f32[5,8,128]{2,1,0:T(8,128)S(1)}, f32[5,8,128]{2,1,0:T(8,128)S(1)}, u32[]{:S(2)}, u32[]{:S(2)}) collective-permute-start(f32[5,8,128]{2,1,0:T(8,128)S(1)} %get-tuple-element.19), channel_id=1, source_target_pairs={{8,16},{16,8},{24,32},{32,24},{40,48},{48,40},{56,64},{64,56},{72,... | collective-permute-start | bytes 61448 | tf_op jit(solution)/shard_map/ppermute | solution.py:294
  25.5 5.9 %collective-permute-start.1 = (f32[5,8,128]{2,1,0:T(8,128)S(1)}, f32[5,8,128]{2,1,0:T(8,128)S(1)}, u32[]{:S(2)}, u32[]{:S(2)}) collective-permute-start(f32[5,8,128]{2,1,0:T(8,128)S(1)} %get-tuple-element.20), channel_id=1, source_target_pairs={{0,8},{8,0},{16,24},{24,16},{32,40},{40,32},{48,56},{56,48},{64,72... | collective-permute-start | bytes 61448 | tf_op jit(solution)/shard_map/ppermute | solution.py:296
  27.4 3.0 %copy-start = (f32[3,3072]{1,0:T(4,128)S(1)}, f32[3,3072]{1,0:T(4,128)}, u32[]{:S(2)}) copy-start(f32[3,3072]{1,0:T(4,128)} %tan_ref.3) | copy-start | bytes 110596
  27.4 3.0 %copy-start.1 = (s32[3072]{0:T(1024)S(1)}, s32[3072]{0:T(1024)}, u32[]{:S(2)}) copy-start(s32[3072]{0:T(1024)} %param.13) | copy-start | bytes 36868
  27.4 3.0 %copy-start.2 = (f32[3072]{0:T(1024)S(1)}, f32[3072]{0:T(1024)}, u32[]{:S(2)}) copy-start(f32[3072]{0:T(1024)} %param.9) | copy-start | bytes 36868
  27.4 3.0 %copy-start.3 = (s32[3072]{0:T(1024)S(1)}, s32[3072]{0:T(1024)}, u32[]{:S(2)}) copy-start(s32[3072]{0:T(1024)} %param.12) | copy-start | bytes 36868
  27.4 4.0 %collective-permute-start.4 = (f32[5,8,128]{2,1,0:T(8,128)S(1)}, f32[5,8,128]{2,1,0:T(8,128)S(1)}, u32[]{:S(2)}, u32[]{:S(2)}) collective-permute-start(f32[5,8,128]{2,1,0:T(8,128)S(1)} %get-tuple-element.22), channel_id=1, source_target_pairs={{0,1},{1,0},{2,3},{3,2},{4,5},{5,4},{6,7},{7,6},{8,9},{9,8},{10,11... | collective-permute-start | bytes 61448 | tf_op jit(solution)/shard_map/ppermute | solution.py:297
  30.4 0.7 copy-start.4
  30.5 0.8 copy-start.5
  30.5 0.8 copy-start.7
  31.7 12.4 %collective-permute-start.7 = (f32[16,128]{1,0:T(8,128)S(1)}, f32[16,128]{1,0:T(8,128)S(1)}, u32[]{:S(2)}, u32[]{:S(2)}) collective-permute-start(f32[16,128]{1,0:T(8,128)S(1)} %get-tuple-element.25.y_ref), channel_id=1, source_target_pairs={{8,16},{16,8},{24,32},{32,24},{40,48},{48,40},{56,64},{64,56},{72,... | collective-permute-start | bytes 24584 | tf_op jit(solution)/shard_map/ppermute | solution.py:304
  34.5 9.6 %collective-permute-start.8 = (f32[16,128]{1,0:T(8,128)S(1)}, f32[16,128]{1,0:T(8,128)S(1)}, u32[]{:S(2)}, u32[]{:S(2)}) collective-permute-start(f32[16,128]{1,0:T(8,128)S(1)} %get-tuple-element.25.y_ref), channel_id=1, source_target_pairs={{1,2},{2,1},{3,4},{4,3},{5,6},{6,5},{7,0},{0,7},{9,10},{10,9},{11,... | collective-permute-start | bytes 24584 | tf_op jit(solution)/shard_map/ppermute | solution.py:306
  38.5 6.1 %collective-permute-start.5 = (f32[16,128]{1,0:T(8,128)S(1)}, f32[16,128]{1,0:T(8,128)S(1)}, u32[]{:S(2)}, u32[]{:S(2)}) collective-permute-start(f32[16,128]{1,0:T(8,128)S(1)} %get-tuple-element.25.y_ref), channel_id=1, source_target_pairs={{0,8},{8,0},{16,24},{24,16},{32,40},{40,32},{48,56},{56,48},{64,72... | collective-permute-start | bytes 24584 | tf_op jit(solution)/shard_map/ppermute | solution.py:305
  41.1 3.5 %collective-permute-start.6 = (f32[16,128]{1,0:T(8,128)S(1)}, f32[16,128]{1,0:T(8,128)S(1)}, u32[]{:S(2)}, u32[]{:S(2)}) collective-permute-start(f32[16,128]{1,0:T(8,128)S(1)} %get-tuple-element.25.y_ref), channel_id=1, source_target_pairs={{0,1},{1,0},{2,3},{3,2},{4,5},{5,4},{6,7},{7,6},{8,9},{9,8},{10,11... | collective-permute-start | bytes 24584 | tf_op jit(solution)/shard_map/ppermute | solution.py:307
  44.9 14.1 %collective-permute-start.11 = (f32[16,128]{1,0:T(8,128)S(1)}, f32[16,128]{1,0:T(8,128)S(1)}, u32[]{:S(2)}, u32[]{:S(2)}) collective-permute-start(f32[16,128]{1,0:T(8,128)S(1)} %shard_map.97.y_ref), channel_id=1, source_target_pairs={{8,16},{16,8},{24,32},{32,24},{40,48},{48,40},{56,64},{64,56},{72,... | collective-permute-start | bytes 24584 | tf_op jit(solution)/shard_map/ppermute | solution.py:304
  50.9 8.1 %collective-permute-start.12 = (f32[16,128]{1,0:T(8,128)S(1)}, f32[16,128]{1,0:T(8,128)S(1)}, u32[]{:S(2)}, u32[]{:S(2)}) collective-permute-start(f32[16,128]{1,0:T(8,128)S(1)} %shard_map.97.y_ref), channel_id=1, source_target_pairs={{1,2},{2,1},{3,4},{4,3},{5,6},{6,5},{7,0},{0,7},{9,10},{10,9},{11,... | collective-permute-start | bytes 24584 | tf_op jit(solution)/shard_map/ppermute | solution.py:306
  54.4 5.0 %collective-permute-start.10 = (f32[16,128]{1,0:T(8,128)S(1)}, f32[16,128]{1,0:T(8,128)S(1)}, u32[]{:S(2)}, u32[]{:S(2)}) collective-permute-start(f32[16,128]{1,0:T(8,128)S(1)} %shard_map.97.y_ref), channel_id=1, source_target_pairs={{0,1},{1,0},{2,3},{3,2},{4,5},{5,4},{6,7},{7,6},{8,9},{9,8},{10,11... | collective-permute-start | bytes 24584 | tf_op jit(solution)/shard_map/ppermute | solution.py:307
  57.1 4.4 %collective-permute-start.9 = (f32[16,128]{1,0:T(8,128)S(1)}, f32[16,128]{1,0:T(8,128)S(1)}, u32[]{:S(2)}, u32[]{:S(2)}) collective-permute-start(f32[16,128]{1,0:T(8,128)S(1)} %shard_map.97.y_ref), channel_id=1, source_target_pairs={{0,8},{8,0},{16,24},{24,16},{32,40},{40,32},{48,56},{56,48},{64,72... | collective-permute-start | bytes 24584 | tf_op jit(solution)/shard_map/ppermute | solution.py:305
  61.8 13.0 %collective-permute-start.15 = (f32[16,128]{1,0:T(8,128)S(1)}, f32[16,128]{1,0:T(8,128)S(1)}, u32[]{:S(2)}, u32[]{:S(2)}) collective-permute-start(f32[16,128]{1,0:T(8,128)S(1)} %shard_map.99.y_ref), channel_id=1, source_target_pairs={{8,16},{16,8},{24,32},{32,24},{40,48},{48,40},{56,64},{64,56},{72,... | collective-permute-start | bytes 24584 | tf_op jit(solution)/shard_map/ppermute | solution.py:304
  65.7 9.0 %collective-permute-start.16 = (f32[16,128]{1,0:T(8,128)S(1)}, f32[16,128]{1,0:T(8,128)S(1)}, u32[]{:S(2)}, u32[]{:S(2)}) collective-permute-start(f32[16,128]{1,0:T(8,128)S(1)} %shard_map.99.y_ref), channel_id=1, source_target_pairs={{1,2},{2,1},{3,4},{4,3},{5,6},{6,5},{7,0},{0,7},{9,10},{10,9},{11,... | collective-permute-start | bytes 24584 | tf_op jit(solution)/shard_map/ppermute | solution.py:306
  70.9 4.4 %collective-permute-start.13 = (f32[16,128]{1,0:T(8,128)S(1)}, f32[16,128]{1,0:T(8,128)S(1)}, u32[]{:S(2)}, u32[]{:S(2)}) collective-permute-start(f32[16,128]{1,0:T(8,128)S(1)} %shard_map.99.y_ref), channel_id=1, source_target_pairs={{0,8},{8,0},{16,24},{24,16},{32,40},{40,32},{48,56},{56,48},{64,72... | collective-permute-start | bytes 24584 | tf_op jit(solution)/shard_map/ppermute | solution.py:305
  72.8 3.1 %collective-permute-start.14 = (f32[16,128]{1,0:T(8,128)S(1)}, f32[16,128]{1,0:T(8,128)S(1)}, u32[]{:S(2)}, u32[]{:S(2)}) collective-permute-start(f32[16,128]{1,0:T(8,128)S(1)} %shard_map.99.y_ref), channel_id=1, source_target_pairs={{0,1},{1,0},{2,3},{3,2},{4,5},{5,4},{6,7},{7,6},{8,9},{9,8},{10,11... | collective-permute-start | bytes 24584 | tf_op jit(solution)/shard_map/ppermute | solution.py:307
  75.9 13.7 %copy-start.6 = (f32[3072]{0:T(1024)S(1)}, f32[3072]{0:T(1024)}, u32[]{:S(2)}) copy-start(f32[3072]{0:T(1024)} %param.10) | copy-start | bytes 36868
  76.2 13.4 %collective-permute-start.19 = (f32[16,128]{1,0:T(8,128)S(1)}, f32[16,128]{1,0:T(8,128)S(1)}, u32[]{:S(2)}, u32[]{:S(2)}) collective-permute-start(f32[16,128]{1,0:T(8,128)S(1)} %shard_map.101.y_ref), channel_id=1, source_target_pairs={{8,16},{16,8},{24,32},{32,24},{40,48},{48,40},{56,64},{64,56},{72,... | collective-permute-start | bytes 24584 | tf_op jit(solution)/shard_map/ppermute | solution.py:304
  82.2 7.4 %collective-permute-start.20 = (f32[16,128]{1,0:T(8,128)S(1)}, f32[16,128]{1,0:T(8,128)S(1)}, u32[]{:S(2)}, u32[]{:S(2)}) collective-permute-start(f32[16,128]{1,0:T(8,128)S(1)} %shard_map.101.y_ref), channel_id=1, source_target_pairs={{1,2},{2,1},{3,4},{4,3},{5,6},{6,5},{7,0},{0,7},{9,10},{10,9},{11,... | collective-permute-start | bytes 24584 | tf_op jit(solution)/shard_map/ppermute | solution.py:306
  85.1 4.9 %collective-permute-start.17 = (f32[16,128]{1,0:T(8,128)S(1)}, f32[16,128]{1,0:T(8,128)S(1)}, u32[]{:S(2)}, u32[]{:S(2)}) collective-permute-start(f32[16,128]{1,0:T(8,128)S(1)} %shard_map.101.y_ref), channel_id=1, source_target_pairs={{0,8},{8,0},{16,24},{24,16},{32,40},{40,32},{48,56},{56,48},{64,72... | collective-permute-start | bytes 24584 | tf_op jit(solution)/shard_map/ppermute | solution.py:305
  87.0 3.4 %collective-permute-start.18 = (f32[16,128]{1,0:T(8,128)S(1)}, f32[16,128]{1,0:T(8,128)S(1)}, u32[]{:S(2)}, u32[]{:S(2)}) collective-permute-start(f32[16,128]{1,0:T(8,128)S(1)} %shard_map.101.y_ref), channel_id=1, source_target_pairs={{0,1},{1,0},{2,3},{3,2},{4,5},{5,4},{6,7},{7,6},{8,9},{9,8},{10,11... | collective-permute-start | bytes 24584 | tf_op jit(solution)/shard_map/ppermute | solution.py:307
